TPU v7x, 32 devices: a whole 2x2x4 slice. The times are simulated.
32 devices in a mesh: img: 8 (over z, y), nrn: 4 (over x, core).
Axes of the slice: x: 2, y: 2, z: 4, core: 2. Of those that a mesh axis runs over, the one named last changes fastest.
Arguments:
- images: bfloat16 [2048, 16384], P('img', 'nrn'), may hold values from 0 to 12
- weights: bfloat16 [2, 128, 512, 128], P(None, 'nrn'), may hold values from -0.375 to 0.375
- block_index: int32 [2, 128, 4], replicated, may hold values from 0 to 127, as said below
- bias: float32 [2, 16384], replicated, may hold values from -0.2 to -0.02
Outputs:
- activations: bfloat16 [2048, 16384], P('img', 'nrn')
- live_fraction: float32 [2], replicated
Inputs may be any that keep to these rules, and one draw needn't show every extreme that they name: `block_index`: the 4 entries of each row name different blocks.
All inputs are finite; a program needn't handle non-finite values.
Results may differ from a plain program's by a relative error of at most 0.005.
Values may be sent and summed in bfloat16 or wider, within the bound.
No kernel may reach another device: no remote copies, remote signals or barrier semaphores. Data moves between devices by JAX's collectives and lax.ppermute only.
A program may use at most 128 MiB of HBM per device.

v0:
```python
import functools

import jax
import jax.numpy as jnp
from jax import lax
from jax.experimental import pallas as pl
from jax.experimental.pallas import tpu as pltpu
from jax.sharding import PartitionSpec as P


live_level = 0.25


def xor_pairs(count, mask):
    return [(i, i ^ mask) for i in range(count)]


def layers_kernel(
    layout, position_ref, place_ref, shard_ref, column_ref, block_ref, bias_ref,
    own_ref, near_ref, far_ref, cross_ref, weights_ref, near_weights_ref, *refs,
):
    piece_refs, refs = refs[: len(layout)], refs[len(layout) :]
    mine_ref, theirs_ref, sums_ref, inputs, first, tiles, second_tiles, total, sems = refs
    position = position_ref[0]
    core = lax.rem(position, 2)
    half = near_ref.shape[0]
    rows, width = first.shape[0] // 4, first.shape[-1]
    deep = tiles.shape[1] // rows

    copies = []

    def fetch(source, target):
        copy = pltpu.make_async_copy(source, target, sems.at[len(copies)])
        copy.start()
        copies.append(copy)

    fetch(own_ref.at[pl.ds(pl.multiple_of(core * half, half), half), :], inputs.at[position])
    for mask, ref in ((1, near_ref), (2, far_ref), (3, cross_ref)):
        fetch(ref, inputs.at[position ^ mask])
    fetch(weights_ref.at[0], tiles.at[0])
    fetch(near_weights_ref.at[0], tiles.at[1])
    fetch(weights_ref.at[1], second_tiles.at[0])
    fetch(near_weights_ref.at[1], second_tiles.at[1])

    def each_piece(slot, act):
        for i, (ref, own_slot) in enumerate(zip(piece_refs, layout)):
            if own_slot == slot:
                place = place_ref[i]

                @pl.when(place >= 0)
                def _():
                    target = tiles.at[slot, pl.ds(pl.multiple_of(place, 16), ref.shape[0])]
                    act(pltpu.make_async_copy(ref, target, sems.at[8 + i]))

    for slot in (2, 3):
        each_piece(slot, lambda copy: copy.start())

    for copy in copies[:4]:
        copy.wait()
    total[...] = jnp.zeros_like(total)
    for mask in range(4):
        if mask < 2:
            copies[4 + mask].wait()
        else:
            each_piece(mask, lambda copy: copy.wait())
        start = (position ^ mask) * rows

        @pl.loop(0, rows, unroll=16)
        def _(r):
            row = start + r
            parts = []
            for k in range(4):
                column = pl.multiple_of(column_ref[row * 4 + k], width)
                parts.append(inputs[shard_ref[row * 4 + k], :, pl.ds(column, width)])
            tile = tiles[mask, pl.ds(pl.multiple_of(r * deep, deep), deep), :]
            result = jnp.dot(jnp.concatenate(parts, axis=1), tile, preferred_element_type=jnp.float32)
            result = jnp.maximum(result + bias_ref[pl.ds(row, 1), :], 0.0).astype(jnp.bfloat16)
            first[row] = result
            total[...] += result.astype(jnp.float32)

    ones = jnp.ones((8, width), jnp.float32)

    def collapse(value):
        return lax.dot_general(
            ones, value, (((1,), (1,)), ((), ())), precision=lax.Precision.HIGHEST, preferred_element_type=jnp.float32
        )

    sums_ref[0] = collapse(total[...])
    total[...] = jnp.zeros_like(total)
    for mask, out_ref in ((0, mine_ref), (1, theirs_ref)):
        copies[6 + mask].wait()
        start = (position ^ mask) * rows

        @pl.loop(0, rows, unroll=16)
        def _(r):
            row = start + r + 4 * rows
            parts = [first[block_ref[(start + r) * 4 + k]] for k in range(4)]
            tile = second_tiles[mask, pl.ds(pl.multiple_of(r * deep, deep), deep), :]
            result = jnp.dot(jnp.concatenate(parts, axis=1), tile, preferred_element_type=jnp.float32)
            result = jnp.maximum(result + bias_ref[pl.ds(row, 1), :], 0.0).astype(jnp.bfloat16)
            out_ref[:, pl.ds(pl.multiple_of(r * width, width), width)] = result
            total[...] += result.astype(jnp.float32)

    sums_ref[1] = collapse(total[...])


def gather_far(weights, position, group, sides, groups):
    rows, width = weights.shape[1:]
    nrn = functools.partial(lax.ppermute, axis_name="nrn")
    both = functools.partial(lax.ppermute, axis_name=("img", "nrn"))
    piece_rows = rows // groups
    piece = lax.dynamic_slice(weights, (0, group * piece_rows, 0), (1, piece_rows, width))[0]
    piece = nrn(piece, perm=xor_pairs(sides, 2))
    if groups % 2 or groups > 8:
        far = lax.all_gather(piece, "img", axis=0, tiled=True)
        return [far, nrn(far, perm=xor_pairs(sides, 1))], [2, 3], jnp.zeros((2,), jnp.int32)

    line = groups // 2
    spot, side = group // 2, group % 2
    upward = lax.rem(position, 2) == 0

    def pairs(steps, move):
        found = []
        for g in range(groups):
            for n in range(sides):
                source = g // 2 - steps if n % 2 == 0 else g // 2 + steps
                target = move(g, n)
                if 0 <= source < line and 0 <= target[0] < groups:
                    found.append((g * sides + n, target[0] * sides + target[1]))
        return found

    def onward(g, n):
        return (g + 2 if n % 2 == 0 else g - 2), n

    def beside(g, n):
        return g ^ 1, n

    arrays, slots, places = [], [], []

    def keep(array, slot, steps, crossed, passed):
        step = jnp.where(upward != passed, -steps, steps)
        source = spot + step
        row = (source * 2 + (1 - side if crossed else side)) * piece_rows
        arrays.append(array)
        slots.append(slot)
        places.append(jnp.where((source >= 0) & (source < line), row, -1))

    held = [piece, nrn(piece, perm=xor_pairs(sides, 1))]
    keep(held[0], 2, 0, False, False)
    keep(held[1], 3, 0, False, False)
    other = both(piece, perm=pairs(0, beside))
    other_near = nrn(other, perm=xor_pairs(sides, 1))
    keep(other, 2, 0, True, False)
    keep(other_near, 3, 0, True, False)
    for s in range(1, line):
        for h in range(2):
            held[h] = both(held[h], perm=pairs(s - 1, onward))
            keep(held[h], 2 + h, s, False, False)
            keep(nrn(held[h], perm=xor_pairs(sides, 1)), 3 - h, s, False, True)
            other = both(held[h], perm=pairs(s, beside))
            keep(other, 2 + h, s, True, False)
            keep(nrn(other, perm=xor_pairs(sides, 1)), 3 - h, s, True, True)
    return arrays, slots, jnp.stack(places).astype(jnp.int32)


def per_device(images, weights, block_index, bias):
    layers, rows, deep, width = weights.shape
    count, shard = images.shape
    sides = lax.axis_size("nrn")
    groups = lax.axis_size("img")
    assert layers == 2 and sides == 4 and block_index.shape[-1] == 4
    neurons = shard * sides
    position = lax.axis_index("nrn")
    group = lax.axis_index("img")
    core = lax.rem(position, 2)
    half = count // 2
    nrn = functools.partial(lax.ppermute, axis_name="nrn")

    weights = weights.reshape(layers, rows * deep, width)
    pieces, layout, places = gather_far(weights, position, group, sides, groups)

    tables = (
        position.reshape(1), places, (block_index[0] // rows).reshape(-1), (block_index[0] % rows * width).reshape(-1),
        block_index[1].reshape(-1), bias.reshape(layers * sides * rows, width),
    )
    weights, tables = lax.optimization_barrier((weights, tables))
    near_weights = nrn(weights, perm=xor_pairs(sides, 1))
    kept = lax.dynamic_slice(images, (core * half, 0), (half, shard))
    given = lax.dynamic_slice(images, ((1 - core) * half, 0), (half, shard))
    far = nrn(kept, perm=xor_pairs(sides, 2))
    cross = nrn(given, perm=xor_pairs(sides, 3))
    near = nrn(given, perm=xor_pairs(sides, 1))

    any_space = pl.BlockSpec(memory_space=pl.ANY)
    smem = pl.BlockSpec(memory_space=pltpu.SMEM)
    vmem = pl.BlockSpec(memory_space=pltpu.VMEM)
    mine, theirs, sums = pl.pallas_call(
        functools.partial(layers_kernel, layout),
        out_shape=(
            jax.ShapeDtypeStruct((half, shard), jnp.bfloat16),
            jax.ShapeDtypeStruct((half, shard), jnp.bfloat16),
            jax.ShapeDtypeStruct((layers, 8, half), jnp.float32),
        ),
        in_specs=[smem] * 5 + [vmem] + [any_space] * (6 + len(pieces)),
        out_specs=(vmem,) * 3,
        scratch_shapes=[
            pltpu.VMEM((sides, half, shard), jnp.bfloat16),
            pltpu.VMEM((sides * rows, half, width), jnp.bfloat16),
            pltpu.VMEM((sides, rows * deep, width), jnp.bfloat16),
            pltpu.VMEM((2, rows * deep, width), jnp.bfloat16),
            pltpu.VMEM((half, width), jnp.float32),
            pltpu.SemaphoreType.DMA((8 + len(pieces),)),
        ],
        compiler_params=pltpu.CompilerParams(vmem_limit_bytes=60 * 2**20),
        cost_estimate=pl.CostEstimate(flops=12 * half * rows * deep * width, bytes_accessed=2**25, transcendentals=0),
    )(
        *tables, images, near, far, cross, weights, near_weights, *pieces,
    )

    back = nrn(theirs, perm=xor_pairs(sides, 1))
    activations = jnp.where(core == 0, jnp.concatenate([mine, back]), jnp.concatenate([back, mine]))

    sums = sums[:, 0]
    second = sums[1] + nrn(sums[1], perm=xor_pairs(sides, 2))
    totals = jnp.stack([sums[0], second])
    live = jnp.sum(jnp.minimum(1.0, totals / neurons / live_level), axis=1)
    live = live + nrn(live, perm=xor_pairs(sides, 1))
    if groups & (groups - 1):
        live = lax.psum(live, "img")
    else:
        mask = 1
        while mask < groups:
            live = live + lax.ppermute(live, "img", xor_pairs(groups, mask))
            mask *= 2
    return activations, live / (count * groups)


def solution(mesh):
    in_specs = (P("img", "nrn"), P(None, "nrn", None, None), P(), P())
    out_specs = (P("img", "nrn"), P())
    return jax.shard_map(
        per_device, mesh=mesh, in_specs=in_specs, out_specs=out_specs, check_vma=False
    )
```

profile of v0, /device:TPU:0, one launch (start us, length us, event | category | flops | bytes accessed | tf_op | source)
XLA Modules:
  0.0 169.9 jit_solution(17679142474913753151)
XLA Ops:
  0.8 0.7 fusion.4
  1.6 0.7 reshape_squeeze.3.block_ref
  3.1 1.7 reshape.22.bias_ref
  4.8 0.7 stack.79.place_ref
  5.9 1.1 dynamic-slice_bitcast_fusion
  7.0 2.5 %collective-permute-start.4 = (bf16[2048,128]{1,0:T(8,128)(2,1)S(1)}, bf16[2048,128]{1,0:T(8,128)(2,1)S(1)}, u32[]{:S(2)}, u32[]{:S(2)}) collective-permute-start(bf16[2048,128]{1,0:T(8,128)(2,1)S(1)} %dynamic-slice_bitcast_fusion), channel_id=1, source_target_pairs={{0,2},{1,3},{2,0},{3,1},{4,6},{5,7},{6,4},{7,5},{8,10},{9,11},{10,... | collective-permute-start | bytes 1572872 | tf_op jit(solution)/shard_map/ppermute | solution.py:113
  9.5 12.6 %collective-permute-done.4.refs_0_ = bf16[2048,128]{1,0:T(8,128)(2,1)S(1)} collective-permute-done((bf16[2048,128]{1,0:T(8,128)(2,1)S(1)}, bf16[2048,128]{1,0:T(8,128)(2,1)S(1)}, u32[]{:S(2)}, u32[]{:S(2)}) %collective-permute-start.4) | collective-permute-done | bytes 524320 | tf_op jit(solution)/shard_map/ppermute | solution.py:113
  22.1 4.5 %collective-permute-start.8 = (bf16[2048,128]{1,0:T(8,128)(2,1)S(1)}, bf16[2048,128]{1,0:T(8,128)(2,1)}, u32[]{:S(2)}, u32[]{:S(2)}) collective-permute-start(bf16[2048,128]{1,0:T(8,128)(2,1)S(1)} %collective-permute-done.4.refs_0_), channel_id=1, source_target_pairs={{0,8},{2,10},{4,12},{6,14},{8,16},{9,1},{10,18},{11,3},{12,20},{13... | collective-permute-start | bytes 1572872 | tf_op jit(solution)/shard_map/ppermute | solution.py:157
  26.6 1.5 collective-permute-start.6
  28.2 1.7 constant_dynamic-slice_fusion
  29.8 1.6 collective-permute-start.1
  31.4 1.1 collective-permute-done.8.refs_4_
  32.5 4.7 %collective-permute-done.6.refs_2_ = bf16[2048,128]{1,0:T(8,128)(2,1)S(1)} collective-permute-done((bf16[2048,128]{1,0:T(8,128)(2,1)S(1)}, bf16[2048,128]{1,0:T(8,128)(2,1)S(1)}, u32[]{:S(2)}, u32[]{:S(2)}) %collective-permute-start.6) | collective-permute-done | bytes 524320 | tf_op jit(solution)/shard_map/ppermute | solution.py:151
  37.2 1.9 %collective-permute-done.5.refs_1_ = bf16[2048,128]{1,0:T(8,128)(2,1)S(1)} collective-permute-done((bf16[2048,128]{1,0:T(8,128)(2,1)S(1)}, bf16[2048,128]{1,0:T(8,128)(2,1)S(1)}, u32[]{:S(2)}, u32[]{:S(2)}) %collective-permute-start.5) | collective-permute-done | bytes 524320 | tf_op jit(solution)/shard_map/ppermute | solution.py:148
  39.2 0.7 collective-permute-start.16
  39.8 16.1 %collective-permute-done.1.far_ref = bf16[128,4096]{1,0:T(8,128)(2,1)S(1)} collective-permute-done((bf16[128,4096]{1,0:T(8,128)(2,1)S(1)}, bf16[128,4096]{1,0:T(8,128)(2,1)S(1)}, u32[]{:S(2)}, u32[]{:S(2)}) %collective-permute-start.1) | collective-permute-done | bytes 1048608 | tf_op jit(solution)/shard_map/ppermute | solution.py:190
  55.9 0.7 collective-permute-start.10
  56.6 16.3 %collective-permute-done.2.cross_ref = bf16[128,4096]{1,0:T(8,128)(2,1)S(1)} collective-permute-done((bf16[128,4096]{1,0:T(8,128)(2,1)S(1)}, bf16[128,4096]{1,0:T(8,128)(2,1)S(1)}, u32[]{:S(2)}, u32[]{:S(2)}) %collective-permute-start.2) | collective-permute-done | bytes 1048608 | tf_op jit(solution)/shard_map/ppermute | solution.py:191
  72.9 0.8 collective-permute-start.9
  73.8 4.3 %collective-permute-start.12 = (bf16[2048,128]{1,0:T(8,128)(2,1)S(1)}, bf16[2048,128]{1,0:T(8,128)(2,1)S(1)}, u32[]{:S(2)}, u32[]{:S(2)}) collective-permute-start(bf16[2048,128]{1,0:T(8,128)(2,1)S(1)} %collective-permute-done.5.refs_1_), channel_id=1, source_target_pairs={{0,8},{2,10},{4,12},{6,14},{8,16},{9,1},{10,18},{11,3},{12,20},{13... | collective-permute-start | bytes 1572872 | tf_op jit(solution)/shard_map/ppermute | solution.py:157
  78.2 0.7 collective-permute-start.24
  78.9 0.7 collective-permute-start.18
  79.7 5.1 %collective-permute-done.12.refs_8_ = bf16[2048,128]{1,0:T(8,128)(2,1)S(1)} collective-permute-done((bf16[2048,128]{1,0:T(8,128)(2,1)S(1)}, bf16[2048,128]{1,0:T(8,128)(2,1)S(1)}, u32[]{:S(2)}, u32[]{:S(2)}) %collective-permute-start.12) | collective-permute-done | bytes 524320 | tf_op jit(solution)/shard_map/ppermute | solution.py:157
  84.9 0.7 collective-permute-start.20
  85.6 0.7 collective-permute-start.14
  86.3 7.7 %collective-permute-start.13 = (bf16[2048,128]{1,0:T(8,128)(2,1)S(1)}, bf16[2048,128]{1,0:T(8,128)(2,1)S(1)}, u32[]{:S(2)}, u32[]{:S(2)}) collective-permute-start(bf16[2048,128]{1,0:T(8,128)(2,1)S(1)} %collective-permute-done.12.refs_8_), channel_id=1, source_target_pairs={{0,1},{1,0},{2,3},{3,2},{4,5},{5,4},{6,7},{7,6},{8,9},{9,8},{10,11... | collective-permute-start | bytes 1572872 | tf_op jit(solution)/shard_map/ppermute | solution.py:159
  94.1 0.7 collective-permute-start.26
  94.8 5.6 %collective-permute-start.25 = (bf16[2048,128]{1,0:T(8,128)(2,1)S(1)}, bf16[2048,128]{1,0:T(8,128)(2,1)S(1)}, u32[]{:S(2)}, u32[]{:S(2)}) collective-permute-start(bf16[2048,128]{1,0:T(8,128)(2,1)S(1)} %collective-permute-done.24.refs_20_), channel_id=1, source_target_pairs={{0,1},{1,0},{2,3},{3,2},{4,5},{5,4},{6,7},{7,6},{8,9},{9,8},{10,11... | collective-permute-start | bytes 1572872 | tf_op jit(solution)/shard_map/ppermute | solution.py:159
  100.4 1.3 collective-permute-start.19
  101.7 0.7 collective-permute-start.28
  102.4 0.7 collective-permute-start.22
  103.2 6.4 %collective-permute-start.21 = (bf16[2048,128]{1,0:T(8,128)(2,1)S(1)}, bf16[2048,128]{1,0:T(8,128)(2,1)S(1)}, u32[]{:S(2)}, u32[]{:S(2)}) collective-permute-start(bf16[2048,128]{1,0:T(8,128)(2,1)S(1)} %collective-permute-done.20.refs_16_), channel_id=1, source_target_pairs={{0,1},{1,0},{2,3},{3,2},{4,5},{5,4},{6,7},{7,6},{8,9},{9,8},{10,11... | collective-permute-start | bytes 1572872 | tf_op jit(solution)/shard_map/ppermute | solution.py:159
  109.7 0.7 collective-permute-start.30
  110.4 9.8 %collective-permute-start.29 = (bf16[2048,128]{1,0:T(8,128)(2,1)S(1)}, bf16[2048,128]{1,0:T(8,128)(2,1)S(1)}, u32[]{:S(2)}, u32[]{:S(2)}) collective-permute-start(bf16[2048,128]{1,0:T(8,128)(2,1)S(1)} %collective-permute-done.28.refs_24_), channel_id=1, source_target_pairs={{0,1},{1,0},{2,3},{3,2},{4,5},{5,4},{6,7},{7,6},{8,9},{9,8},{10,11... | collective-permute-start | bytes 1572872 | tf_op jit(solution)/shard_map/ppermute | solution.py:159
  120.9 7.0 %collective-permute-start.31 = (bf16[2048,128]{1,0:T(8,128)(2,1)S(1)}, bf16[2048,128]{1,0:T(8,128)(2,1)S(1)}, u32[]{:S(2)}, u32[]{:S(2)}) collective-permute-start(bf16[2048,128]{1,0:T(8,128)(2,1)S(1)} %collective-permute-done.30.refs_26_), channel_id=1, source_target_pairs={{0,1},{1,0},{2,3},{3,2},{4,5},{5,4},{6,7},{7,6},{8,9},{9,8},{10,11... | collective-permute-start | bytes 1572872 | tf_op jit(solution)/shard_map/ppermute | solution.py:162
  127.9 1.5 collective-permute-done.31.refs_27_
  129.5 0.8 copy-done.29
  130.3 17.2 %shard_map.59 = (bf16[128,4096]{1,0:T(8,128)(2,1)}, bf16[128,4096]{1,0:T(8,128)(2,1)}, f32[2,8,128]{2,1,0:T(8,128)}) custom-call(s32[1]{0:T(128)} %bitcast.1.position_ref, s32[28]{0:T(128)} %stack.79.place_ref, s32[512]{0:T(512)} %get-tuple-element.14.shard_ref, s32[512]{0:T(512)} %get-tuple-element.15.column_ref, s32[512]{0:T(512)} %reshape_squeeze.3.block_ref, ...), custom_call_target="tpu_custom_call" | custom-call | flops 3221225472 | bytes 33554432 | tf_op jit(solution)/shard_map/pallas_call | solution.py:197
  148.0 0.7 slice_bitcast_fusion.1
  148.6 1.5 collective-permute-start.33
  150.1 2.1 %collective-permute-done.33 = f32[128]{0:T(128)S(1)} collective-permute-done((f32[128]{0:T(128)S(1)}, f32[128]{0:T(128)S(1)}, u32[]{:S(2)}, u32[]{:S(2)}) %collective-permute-start.33) | collective-permute-done | bytes 544 | tf_op jit(solution)/shard_map/ppermute | solution.py:224
  152.2 0.7 add_bitcast_fusion
  153.1 1.1 collective-permute-done.34
  154.8 3.0 %collective-permute-done.35 = f32[2]{0:T(128)S(1)} collective-permute-done((f32[2]{0:T(128)S(1)}, f32[2]{0:T(128)S(1)}, u32[]{:S(2)}, u32[]{:S(2)}) %collective-permute-start.35) | collective-permute-done | bytes 40 | tf_op jit(solution)/shard_map/ppermute | solution.py:233
  157.8 3.6 %collective-permute-done.36 = f32[2]{0:T(128)S(1)} collective-permute-done((f32[2]{0:T(128)S(1)}, f32[2]{0:T(128)S(1)}, u32[]{:S(2)}, u32[]{:S(2)}) %collective-permute-start.36) | collective-permute-done | bytes 40 | tf_op jit(solution)/shard_map/ppermute | solution.py:233
  161.4 1.6 collective-permute-start.37
  163.0 2.8 %collective-permute-done.37 = f32[2]{0:T(128)S(1)} collective-permute-done((f32[2]{0:T(128)S(1)}, f32[2]{0:T(128)S(1)}, u32[]{:S(2)}, u32[]{:S(2)}) %collective-permute-start.37) | collective-permute-done | bytes 40 | tf_op jit(solution)/shard_map/ppermute | solution.py:233
  166.4 3.6 %maximum_select_fusion = bf16[256,4096]{1,0:T(8,128)(2,1)} fusion(bf16[128,4096]{1,0:T(8,128)(2,1)S(1)} %collective-permute-done.32, bf16[128,4096]{1,0:T(8,128)(2,1)} %get-tuple-element.19, pred[]{:T(512)S(6)} %eq.8), kind=kLoop, calls=%fused_computation | loop fusion | flops 9437184 | bytes 4194305 | tf_op jit(solution)/shard_map/jit(_where)/select_n | solution.py:221
  (107 shorter events, 4.3 us)
Async XLA Ops:
  5.4 124.8 %collective-permute-start.3 = (bf16[2,16384,128]{2,1,0:T(8,128)(2,1)}, bf16[2,16384,128]{2,1,0:T(8,128)(2,1)}, u32[]{:S(2)}, u32[]{:S(2)}) collective-permute-start(bf16[2,16384,128]{2,1,0:T(8,128)(2,1)} %bitcast.26), channel_id=1, source_target_pairs={{0,1},{1,0},{2,3},{3,2},{4,5},{5,4},{6,7},{7,6},{8,9},{9,8},{10,11... | collective-permute-start | bytes 25165832 | tf_op jit(solution)/shard_map/ppermute | solution.py:187
  7.0 15.1 %collective-permute-start.4 = (bf16[2048,128]{1,0:T(8,128)(2,1)S(1)}, bf16[2048,128]{1,0:T(8,128)(2,1)S(1)}, u32[]{:S(2)}, u32[]{:S(2)}) collective-permute-start(bf16[2048,128]{1,0:T(8,128)(2,1)S(1)} %dynamic-slice_bitcast_fusion), channel_id=1, source_target_pairs={{0,2},{1,3},{2,0},{3,1},{4,6},{5,7},{6,4},{7,5},{8,10},{9,11},{10,... | collective-permute-start | bytes 1572872 | tf_op jit(solution)/shard_map/ppermute | solution.py:113
  22.1 10.4 %collective-permute-start.8 = (bf16[2048,128]{1,0:T(8,128)(2,1)S(1)}, bf16[2048,128]{1,0:T(8,128)(2,1)}, u32[]{:S(2)}, u32[]{:S(2)}) collective-permute-start(bf16[2048,128]{1,0:T(8,128)(2,1)S(1)} %collective-permute-done.4.refs_0_), channel_id=1, source_target_pairs={{0,8},{2,10},{4,12},{6,14},{8,16},{9,1},{10,18},{11,3},{12,20},{13... | collective-permute-start | bytes 1572872 | tf_op jit(solution)/shard_map/ppermute | solution.py:157
  26.6 10.6 %collective-permute-start.6 = (bf16[2048,128]{1,0:T(8,128)(2,1)S(1)}, bf16[2048,128]{1,0:T(8,128)(2,1)S(1)}, u32[]{:S(2)}, u32[]{:S(2)}) collective-permute-start(bf16[2048,128]{1,0:T(8,128)(2,1)S(1)} %collective-permute-done.4.refs_0_), channel_id=1, source_target_pairs={{0,4},{1,5},{2,6},{3,7},{4,0},{5,1},{6,2},{7,3},{8,12},{9,13},{10,... | collective-permute-start | bytes 1572872 | tf_op jit(solution)/shard_map/ppermute | solution.py:151
  29.8 26.1 %collective-permute-start.1 = (bf16[128,4096]{1,0:T(8,128)(2,1)S(1)}, bf16[128,4096]{1,0:T(8,128)(2,1)S(1)}, u32[]{:S(2)}, u32[]{:S(2)}) collective-permute-start(bf16[128,4096]{1,0:T(8,128)(2,1)S(1)} %get-tuple-element.22), channel_id=1, source_target_pairs={{0,2},{1,3},{2,0},{3,1},{4,6},{5,7},{6,4},{7,5},{8,10},{9,11},{10,... | collective-permute-start | bytes 3145736 | tf_op jit(solution)/shard_map/ppermute | solution.py:190
  31.4 41.5 %collective-permute-start.2 = (bf16[128,4096]{1,0:T(8,128)(2,1)S(1)}, bf16[128,4096]{1,0:T(8,128)(2,1)S(1)}, u32[]{:S(2)}, u32[]{:S(2)}) collective-permute-start(bf16[128,4096]{1,0:T(8,128)(2,1)S(1)} %get-tuple-element.23), channel_id=1, source_target_pairs={{0,3},{1,2},{2,1},{3,0},{4,7},{5,6},{6,5},{7,4},{8,11},{9,10},{10,... | collective-permute-start | bytes 3145736 | tf_op jit(solution)/shard_map/ppermute | solution.py:191
  32.5 41.2 %collective-permute-start = (bf16[128,4096]{1,0:T(8,128)(2,1)S(1)}, bf16[128,4096]{1,0:T(8,128)(2,1)S(1)}, u32[]{:S(2)}, u32[]{:S(2)}) collective-permute-start(bf16[128,4096]{1,0:T(8,128)(2,1)S(1)} %get-tuple-element.23), channel_id=1, source_target_pairs={{0,1},{1,0},{2,3},{3,2},{4,5},{5,4},{6,7},{7,6},{8,9},{9,8},{10,11... | collective-permute-start | bytes 3145736 | tf_op jit(solution)/shard_map/ppermute | solution.py:192
  37.2 36.5 %copy-start.4 = (bf16[2048,128]{1,0:T(8,128)(2,1)}, bf16[2048,128]{1,0:T(8,128)(2,1)S(1)}, u32[]{:S(2)}) copy-start(bf16[2048,128]{1,0:T(8,128)(2,1)S(1)} %collective-permute-done.6.refs_2_) | copy-start | bytes 1572868
  37.2 1.9 %collective-permute-start.5 = (bf16[2048,128]{1,0:T(8,128)(2,1)S(1)}, bf16[2048,128]{1,0:T(8,128)(2,1)S(1)}, u32[]{:S(2)}, u32[]{:S(2)}) collective-permute-start(bf16[2048,128]{1,0:T(8,128)(2,1)S(1)} %collective-permute-done.4.refs_0_), channel_id=1, source_target_pairs={{0,1},{1,0},{2,3},{3,2},{4,5},{5,4},{6,7},{7,6},{8,9},{9,8},{10,11... | collective-permute-start | bytes 1572872 | tf_op jit(solution)/shard_map/ppermute | solution.py:148
  39.2 40.4 %copy-start.5 = (bf16[2048,128]{1,0:T(8,128)(2,1)}, bf16[2048,128]{1,0:T(8,128)(2,1)S(1)}, u32[]{:S(2)}) copy-start(bf16[2048,128]{1,0:T(8,128)(2,1)S(1)} %collective-permute-done.5.refs_1_) | copy-start | bytes 1572868
  39.2 34.7 %collective-permute-start.16 = (bf16[2048,128]{1,0:T(8,128)(2,1)}, bf16[2048,128]{1,0:T(8,128)(2,1)S(1)}, u32[]{:S(2)}, u32[]{:S(2)}) collective-permute-start(bf16[2048,128]{1,0:T(8,128)(2,1)} %collective-permute-done.8.refs_4_), channel_id=1, source_target_pairs={{8,16},{9,1},{10,18},{11,3},{12,20},{13,5},{14,22},{15,7},{16,24},... | collective-permute-start | bytes 1572872 | tf_op jit(solution)/shard_map/ppermute | solution.py:157
  55.9 74.3 %copy-start = (bf16[128,4096]{1,0:T(8,128)(2,1)}, bf16[128,4096]{1,0:T(8,128)(2,1)S(1)}, u32[]{:S(2)}) copy-start(bf16[128,4096]{1,0:T(8,128)(2,1)S(1)} %collective-permute-done.1.far_ref) | copy-start | bytes 3145732
  55.9 22.2 %collective-permute-start.10 = (bf16[2048,128]{1,0:T(8,128)(2,1)}, bf16[2048,128]{1,0:T(8,128)(2,1)S(1)}, u32[]{:S(2)}, u32[]{:S(2)}) collective-permute-start(bf16[2048,128]{1,0:T(8,128)(2,1)} %collective-permute-done.8.refs_4_), channel_id=1, source_target_pairs={{1,5},{3,7},{5,1},{7,3},{8,12},{9,13},{10,14},{11,15},{12,8},{13,9... | collective-permute-start | bytes 1572872 | tf_op jit(solution)/shard_map/ppermute | solution.py:160
  72.9 57.3 %copy-start.1 = (bf16[128,4096]{1,0:T(8,128)(2,1)}, bf16[128,4096]{1,0:T(8,128)(2,1)S(1)}, u32[]{:S(2)}) copy-start(bf16[128,4096]{1,0:T(8,128)(2,1)S(1)} %collective-permute-done.2.cross_ref) | copy-start | bytes 3145732
  72.9 5.9 %collective-permute-start.9 = (bf16[2048,128]{1,0:T(8,128)(2,1)}, bf16[2048,128]{1,0:T(8,128)(2,1)S(1)}, u32[]{:S(2)}, u32[]{:S(2)}) collective-permute-start(bf16[2048,128]{1,0:T(8,128)(2,1)} %collective-permute-done.8.refs_4_), channel_id=1, source_target_pairs={{0,1},{1,0},{2,3},{3,2},{4,5},{5,4},{6,7},{7,6},{8,9},{9,8},{10,11... | collective-permute-start | bytes 1572872 | tf_op jit(solution)/shard_map/ppermute | solution.py:159
  73.7 56.5 %copy-start.2 = (bf16[128,4096]{1,0:T(8,128)(2,1)}, bf16[128,4096]{1,0:T(8,128)(2,1)S(1)}, u32[]{:S(2)}) copy-start(bf16[128,4096]{1,0:T(8,128)(2,1)S(1)} %collective-permute-done.near_ref) | copy-start | bytes 3145732
  73.7 5.9 %collective-permute-start.7 = (bf16[2048,128]{1,0:T(8,128)(2,1)S(1)}, bf16[2048,128]{1,0:T(8,128)(2,1)S(1)}, u32[]{:S(2)}, u32[]{:S(2)}) collective-permute-start(bf16[2048,128]{1,0:T(8,128)(2,1)S(1)} %collective-permute-done.6.refs_2_), channel_id=1, source_target_pairs={{0,1},{1,0},{2,3},{3,2},{4,5},{5,4},{6,7},{7,6},{8,9},{9,8},{10,11... | collective-permute-start | bytes 1572872 | tf_op jit(solution)/shard_map/ppermute | solution.py:152
  73.8 56.4 %copy-start.6 = (bf16[2048,128]{1,0:T(8,128)(2,1)}, bf16[2048,128]{1,0:T(8,128)(2,1)S(1)}, u32[]{:S(2)}) copy-start(bf16[2048,128]{1,0:T(8,128)(2,1)S(1)} %collective-permute-done.16.refs_12_) | copy-start | bytes 1572868
  73.8 11.0 %collective-permute-start.12 = (bf16[2048,128]{1,0:T(8,128)(2,1)S(1)}, bf16[2048,128]{1,0:T(8,128)(2,1)S(1)}, u32[]{:S(2)}, u32[]{:S(2)}) collective-permute-start(bf16[2048,128]{1,0:T(8,128)(2,1)S(1)} %collective-permute-done.5.refs_1_), channel_id=1, source_target_pairs={{0,8},{2,10},{4,12},{6,14},{8,16},{9,1},{10,18},{11,3},{12,20},{13... | collective-permute-start | bytes 1572872 | tf_op jit(solution)/shard_map/ppermute | solution.py:157
  78.2 6.7 %collective-permute-start.24 = (bf16[2048,128]{1,0:T(8,128)(2,1)S(1)}, bf16[2048,128]{1,0:T(8,128)(2,1)S(1)}, u32[]{:S(2)}, u32[]{:S(2)}) collective-permute-start(bf16[2048,128]{1,0:T(8,128)(2,1)S(1)} %collective-permute-done.16.refs_12_), channel_id=1, source_target_pairs={{9,1},{11,3},{13,5},{15,7},{16,24},{18,26},{20,28},{22,30}} | collective-permute-start | bytes 1572872 | tf_op jit(solution)/shard_map/ppermute | solution.py:157
  78.9 6.7 %collective-permute-start.18 = (bf16[2048,128]{1,0:T(8,128)(2,1)S(1)}, bf16[2048,128]{1,0:T(8,128)(2,1)S(1)}, u32[]{:S(2)}, u32[]{:S(2)}) collective-permute-start(bf16[2048,128]{1,0:T(8,128)(2,1)S(1)} %collective-permute-done.16.refs_12_), channel_id=1, source_target_pairs={{1,5},{3,7},{5,1},{7,3},{9,13},{11,15},{13,9},{15,11},{16,20},{18,... | collective-permute-start | bytes 1572872 | tf_op jit(solution)/shard_map/ppermute | solution.py:160
  79.6 6.7 %collective-permute-start.17 = (bf16[2048,128]{1,0:T(8,128)(2,1)S(1)}, bf16[2048,128]{1,0:T(8,128)(2,1)S(1)}, u32[]{:S(2)}, u32[]{:S(2)}) collective-permute-start(bf16[2048,128]{1,0:T(8,128)(2,1)S(1)} %collective-permute-done.16.refs_12_), channel_id=1, source_target_pairs={{0,1},{1,0},{2,3},{3,2},{4,5},{5,4},{6,7},{7,6},{8,9},{9,8},{10,11... | collective-permute-start | bytes 1572872 | tf_op jit(solution)/shard_map/ppermute | solution.py:159
  84.8 9.3 %collective-permute-start.11 = (bf16[2048,128]{1,0:T(8,128)(2,1)S(1)}, bf16[2048,128]{1,0:T(8,128)(2,1)S(1)}, u32[]{:S(2)}, u32[]{:S(2)}) collective-permute-start(bf16[2048,128]{1,0:T(8,128)(2,1)S(1)} %collective-permute-done.10.refs_6_), channel_id=1, source_target_pairs={{0,1},{1,0},{2,3},{3,2},{4,5},{5,4},{6,7},{7,6},{8,9},{9,8},{10,11... | collective-permute-start | bytes 1572872 | tf_op jit(solution)/shard_map/ppermute | solution.py:162
  84.9 9.9 %collective-permute-start.20 = (bf16[2048,128]{1,0:T(8,128)(2,1)S(1)}, bf16[2048,128]{1,0:T(8,128)(2,1)S(1)}, u32[]{:S(2)}, u32[]{:S(2)}) collective-permute-start(bf16[2048,128]{1,0:T(8,128)(2,1)S(1)} %collective-permute-done.12.refs_8_), channel_id=1, source_target_pairs={{8,16},{9,1},{10,18},{11,3},{12,20},{13,5},{14,22},{15,7},{16,24},... | collective-permute-start | bytes 1572872 | tf_op jit(solution)/shard_map/ppermute | solution.py:157
  85.6 14.8 %collective-permute-start.14 = (bf16[2048,128]{1,0:T(8,128)(2,1)S(1)}, bf16[2048,128]{1,0:T(8,128)(2,1)S(1)}, u32[]{:S(2)}, u32[]{:S(2)}) collective-permute-start(bf16[2048,128]{1,0:T(8,128)(2,1)S(1)} %collective-permute-done.12.refs_8_), channel_id=1, source_target_pairs={{1,5},{3,7},{5,1},{7,3},{8,12},{9,13},{10,14},{11,15},{12,8},{13,9... | collective-permute-start | bytes 1572872 | tf_op jit(solution)/shard_map/ppermute | solution.py:160
  86.3 23.3 %copy-start.13 = (bf16[2048,128]{1,0:T(8,128)(2,1)}, bf16[2048,128]{1,0:T(8,128)(2,1)S(1)}, u32[]{:S(2)}) copy-start(bf16[2048,128]{1,0:T(8,128)(2,1)S(1)} %collective-permute-done.17.refs_13_) | copy-start | bytes 1572868
  86.3 15.4 %collective-permute-start.13 = (bf16[2048,128]{1,0:T(8,128)(2,1)S(1)}, bf16[2048,128]{1,0:T(8,128)(2,1)S(1)}, u32[]{:S(2)}, u32[]{:S(2)}) collective-permute-start(bf16[2048,128]{1,0:T(8,128)(2,1)S(1)} %collective-permute-done.12.refs_8_), channel_id=1, source_target_pairs={{0,1},{1,0},{2,3},{3,2},{4,5},{5,4},{6,7},{7,6},{8,9},{9,8},{10,11... | collective-permute-start | bytes 1572872 | tf_op jit(solution)/shard_map/ppermute | solution.py:159
  94.1 8.4 %collective-permute-start.26 = (bf16[2048,128]{1,0:T(8,128)(2,1)S(1)}, bf16[2048,128]{1,0:T(8,128)(2,1)S(1)}, u32[]{:S(2)}, u32[]{:S(2)}) collective-permute-start(bf16[2048,128]{1,0:T(8,128)(2,1)S(1)} %collective-permute-done.24.refs_20_), channel_id=1, source_target_pairs={{1,5},{3,7},{5,1},{7,3},{24,28},{26,30},{28,24},{30,26}} | collective-permute-start | bytes 1572872 | tf_op jit(solution)/shard_map/ppermute | solution.py:160
  94.8 8.3 %collective-permute-start.25 = (bf16[2048,128]{1,0:T(8,128)(2,1)S(1)}, bf16[2048,128]{1,0:T(8,128)(2,1)S(1)}, u32[]{:S(2)}, u32[]{:S(2)}) collective-permute-start(bf16[2048,128]{1,0:T(8,128)(2,1)S(1)} %collective-permute-done.24.refs_20_), channel_id=1, source_target_pairs={{0,1},{1,0},{2,3},{3,2},{4,5},{5,4},{6,7},{7,6},{8,9},{9,8},{10,11... | collective-permute-start | bytes 1572872 | tf_op jit(solution)/shard_map/ppermute | solution.py:159
  100.4 19.8 %copy-start.16 = (bf16[2048,128]{1,0:T(8,128)(2,1)}, bf16[2048,128]{1,0:T(8,128)(2,1)S(1)}, u32[]{:S(2)}) copy-start(bf16[2048,128]{1,0:T(8,128)(2,1)S(1)} %collective-permute-done.14.refs_10_) | copy-start | bytes 1572868
  100.4 9.2 %collective-permute-start.19 = (bf16[2048,128]{1,0:T(8,128)(2,1)S(1)}, bf16[2048,128]{1,0:T(8,128)(2,1)S(1)}, u32[]{:S(2)}, u32[]{:S(2)}) collective-permute-start(bf16[2048,128]{1,0:T(8,128)(2,1)S(1)} %collective-permute-done.18.refs_14_), channel_id=1, source_target_pairs={{0,1},{1,0},{2,3},{3,2},{4,5},{5,4},{6,7},{7,6},{8,9},{9,8},{10,11... | collective-permute-start | bytes 1572872 | tf_op jit(solution)/shard_map/ppermute | solution.py:162
  101.7 8.0 %collective-permute-start.28 = (bf16[2048,128]{1,0:T(8,128)(2,1)S(1)}, bf16[2048,128]{1,0:T(8,128)(2,1)S(1)}, u32[]{:S(2)}, u32[]{:S(2)}) collective-permute-start(bf16[2048,128]{1,0:T(8,128)(2,1)S(1)} %collective-permute-done.20.refs_16_), channel_id=1, source_target_pairs={{9,1},{11,3},{13,5},{15,7},{16,24},{18,26},{20,28},{22,30}} | collective-permute-start | bytes 1572872 | tf_op jit(solution)/shard_map/ppermute | solution.py:157
  102.4 8.0 %collective-permute-start.22 = (bf16[2048,128]{1,0:T(8,128)(2,1)S(1)}, bf16[2048,128]{1,0:T(8,128)(2,1)S(1)}, u32[]{:S(2)}, u32[]{:S(2)}) collective-permute-start(bf16[2048,128]{1,0:T(8,128)(2,1)S(1)} %collective-permute-done.20.refs_16_), channel_id=1, source_target_pairs={{1,5},{3,7},{5,1},{7,3},{9,13},{11,15},{13,9},{15,11},{16,20},{18,... | collective-permute-start | bytes 1572872 | tf_op jit(solution)/shard_map/ppermute | solution.py:160
  103.2 24.7 %copy-start.19 = (bf16[2048,128]{1,0:T(8,128)(2,1)}, bf16[2048,128]{1,0:T(8,128)(2,1)S(1)}, u32[]{:S(2)}) copy-start(bf16[2048,128]{1,0:T(8,128)(2,1)S(1)} %collective-permute-done.25.refs_21_) | copy-start | bytes 1572868
  103.2 17.0 %collective-permute-start.21 = (bf16[2048,128]{1,0:T(8,128)(2,1)S(1)}, bf16[2048,128]{1,0:T(8,128)(2,1)S(1)}, u32[]{:S(2)}, u32[]{:S(2)}) collective-permute-start(bf16[2048,128]{1,0:T(8,128)(2,1)S(1)} %collective-permute-done.20.refs_16_), channel_id=1, source_target_pairs={{0,1},{1,0},{2,3},{3,2},{4,5},{5,4},{6,7},{7,6},{8,9},{9,8},{10,11... | collective-permute-start | bytes 1572872 | tf_op jit(solution)/shard_map/ppermute | solution.py:159
  109.6 10.7 %collective-permute-start.15 = (bf16[2048,128]{1,0:T(8,128)(2,1)S(1)}, bf16[2048,128]{1,0:T(8,128)(2,1)S(1)}, u32[]{:S(2)}, u32[]{:S(2)}) collective-permute-start(bf16[2048,128]{1,0:T(8,128)(2,1)S(1)} %collective-permute-done.14.refs_10_), channel_id=1, source_target_pairs={{0,1},{1,0},{2,3},{3,2},{4,5},{5,4},{6,7},{7,6},{8,9},{9,8},{10,11... | collective-permute-start | bytes 1572872 | tf_op jit(solution)/shard_map/ppermute | solution.py:162
  109.7 11.1 %collective-permute-start.30 = (bf16[2048,128]{1,0:T(8,128)(2,1)S(1)}, bf16[2048,128]{1,0:T(8,128)(2,1)S(1)}, u32[]{:S(2)}, u32[]{:S(2)}) collective-permute-start(bf16[2048,128]{1,0:T(8,128)(2,1)S(1)} %collective-permute-done.28.refs_24_), channel_id=1, source_target_pairs={{1,5},{3,7},{5,1},{7,3},{24,28},{26,30},{28,24},{30,26}} | collective-permute-start | bytes 1572872 | tf_op jit(solution)/shard_map/ppermute | solution.py:160
  110.4 19.0 %copy-start.22 = (bf16[2048,128]{1,0:T(8,128)(2,1)}, bf16[2048,128]{1,0:T(8,128)(2,1)S(1)}, u32[]{:S(2)}) copy-start(bf16[2048,128]{1,0:T(8,128)(2,1)S(1)} %collective-permute-done.22.refs_18_) | copy-start | bytes 1572868
  110.4 17.4 %collective-permute-start.29 = (bf16[2048,128]{1,0:T(8,128)(2,1)S(1)}, bf16[2048,128]{1,0:T(8,128)(2,1)S(1)}, u32[]{:S(2)}, u32[]{:S(2)}) collective-permute-start(bf16[2048,128]{1,0:T(8,128)(2,1)S(1)} %collective-permute-done.28.refs_24_), channel_id=1, source_target_pairs={{0,1},{1,0},{2,3},{3,2},{4,5},{5,4},{6,7},{7,6},{8,9},{9,8},{10,11... | collective-permute-start | bytes 1572872 | tf_op jit(solution)/shard_map/ppermute | solution.py:159
  120.2 7.7 %collective-permute-start.27 = (bf16[2048,128]{1,0:T(8,128)(2,1)S(1)}, bf16[2048,128]{1,0:T(8,128)(2,1)S(1)}, u32[]{:S(2)}, u32[]{:S(2)}) collective-permute-start(bf16[2048,128]{1,0:T(8,128)(2,1)S(1)} %collective-permute-done.26.refs_22_), channel_id=1, source_target_pairs={{0,1},{1,0},{2,3},{3,2},{4,5},{5,4},{6,7},{7,6},{8,9},{9,8},{10,11... | collective-permute-start | bytes 1572872 | tf_op jit(solution)/shard_map/ppermute | solution.py:162
  120.3 7.6 %collective-permute-start.23 = (bf16[2048,128]{1,0:T(8,128)(2,1)S(1)}, bf16[2048,128]{1,0:T(8,128)(2,1)S(1)}, u32[]{:S(2)}, u32[]{:S(2)}) collective-permute-start(bf16[2048,128]{1,0:T(8,128)(2,1)S(1)} %collective-permute-done.22.refs_18_), channel_id=1, source_target_pairs={{0,1},{1,0},{2,3},{3,2},{4,5},{5,4},{6,7},{7,6},{8,9},{9,8},{10,11... | collective-permute-start | bytes 1572872 | tf_op jit(solution)/shard_map/ppermute | solution.py:162
  120.9 8.6 %collective-permute-start.31 = (bf16[2048,128]{1,0:T(8,128)(2,1)S(1)}, bf16[2048,128]{1,0:T(8,128)(2,1)S(1)}, u32[]{:S(2)}, u32[]{:S(2)}) collective-permute-start(bf16[2048,128]{1,0:T(8,128)(2,1)S(1)} %collective-permute-done.30.refs_26_), channel_id=1, source_target_pairs={{0,1},{1,0},{2,3},{3,2},{4,5},{5,4},{6,7},{7,6},{8,9},{9,8},{10,11... | collective-permute-start | bytes 1572872 | tf_op jit(solution)/shard_map/ppermute | solution.py:162
  147.4 18.9 %collective-permute-start.32 = (bf16[128,4096]{1,0:T(8,128)(2,1)}, bf16[128,4096]{1,0:T(8,128)(2,1)S(1)}, u32[]{:S(2)}, u32[]{:S(2)}) collective-permute-start(bf16[128,4096]{1,0:T(8,128)(2,1)} %get-tuple-element.20), channel_id=1, source_target_pairs={{0,1},{1,0},{2,3},{3,2},{4,5},{5,4},{6,7},{7,6},{8,9},{9,8},{10,11... | collective-permute-start | bytes 3145736 | tf_op jit(solution)/shard_map/ppermute | solution.py:220
  148.6 3.6 %collective-permute-start.33 = (f32[128]{0:T(128)S(1)}, f32[128]{0:T(128)S(1)}, u32[]{:S(2)}, u32[]{:S(2)}) collective-permute-start(f32[128]{0:T(128)S(1)} %get-tuple-element.25), channel_id=1, source_target_pairs={{0,2},{1,3},{2,0},{3,1},{4,6},{5,7},{6,4},{7,5},{8,10},{9,11},{10,... | collective-permute-start | bytes 1544 | tf_op jit(solution)/shard_map/ppermute | solution.py:224
  153.0 1.2 collective-permute-start.34
  154.2 3.6 %collective-permute-start.35 = (f32[2]{0:T(128)S(1)}, f32[2]{0:T(128)S(1)}, u32[]{:S(2)}, u32[]{:S(2)}) collective-permute-start(f32[2]{0:T(128)S(1)} %add.160), channel_id=1, source_target_pairs={{0,4},{4,0},{8,12},{12,8},{16,20},{20,16},{24,28},{28,24},{1,5},{5... | collective-permute-start | bytes 32 | tf_op jit(solution)/shard_map/ppermute | solution.py:233
  157.8 3.6 %collective-permute-start.36 = (f32[2]{0:T(128)S(1)}, f32[2]{0:T(128)S(1)}, u32[]{:S(2)}, u32[]{:S(2)}) collective-permute-start(f32[2]{0:T(128)S(1)} %add.161), channel_id=1, source_target_pairs={{0,8},{4,12},{8,0},{12,4},{16,24},{20,28},{24,16},{28,20},{1,9},{5... | collective-permute-start | bytes 32 | tf_op jit(solution)/shard_map/ppermute | solution.py:233
  161.4 4.5 %collective-permute-start.37 = (f32[2]{0:T(128)S(1)}, f32[2]{0:T(128)S(1)}, u32[]{:S(2)}, u32[]{:S(2)}) collective-permute-start(f32[2]{0:T(128)S(1)} %add.162), channel_id=1, source_target_pairs={{0,16},{4,20},{8,24},{12,28},{16,0},{20,4},{24,8},{28,12},{1,17},{... | collective-permute-start | bytes 32 | tf_op jit(solution)/shard_map/ppermute | solution.py:233
  (20 other events, 234.4 us)
where the time goes:
time: 171 us; the launch traced here: 170 us
  waiting for transfers between devices  72 us (42%)
  starting transfers between devices  65.7 us (38%)
  Pallas kernels  17.2 us (10%)
  local copies, waits for them, and re-layouts  8.34 us (5%)
  other arithmetic  5.52 us (3%)
    ppermute x6, starting transfers between devices, gather_far(): keep(nrn(held[h], perm=xor_pairs(sides, 1)), 3 - h, s, False, True)  30.4 us
    pallas_call x1, Pallas kernels, per_device(): pl.pallas_call(functools.partial(layers_kernel, layout), out_shape=(jax.S...  17.2 us
    ppermute x1, waiting for transfers between devices, per_device(): cross = nrn(given, perm=xor_pairs(sides, 3))  16.3 us
    ppermute x1, waiting for transfers between devices, per_device(): far = nrn(kept, perm=xor_pairs(sides, 2))  16.1 us
    ppermute x1, waiting for transfers between devices, gather_far(): piece = nrn(piece, perm=xor_pairs(sides, 2))  12.6 us
    ppermute x6, starting transfers between devices, gather_far(): held[h] = both(held[h], perm=pairs(s - 1, onward))  11.6 us
    ppermute x3, waiting for transfers between devices, per_device(): live = live + lax.ppermute(live, 'img', xor_pairs(groups, mask))  9.45 us
    ppermute x6, starting transfers between devices, gather_far(): keep(nrn(other, perm=xor_pairs(sides, 1)), 3 - h, s, True, True)  9.13 us
  transfers between devices with their start and end apart: 38, of which 13 were waited for; matrix products, arithmetic and copies ran while one was open for 3% of the time, Pallas kernels for 0%

commit v1 on v0

v1 whole, which is shorter than its diff:
```python
import functools

import jax
import jax.numpy as jnp
from jax import lax
from jax.experimental import pallas as pl
from jax.experimental.pallas import tpu as pltpu
from jax.sharding import PartitionSpec as P


live_level = 0.25


def xor_pairs(count, mask):
    return [(i, i ^ mask) for i in range(count)]


def layers_kernel(
    slots, position_ref, place_ref, block_ref, bias_ref,
    own_ref, near_ref, far_ref, cross_ref, weights_ref, near_weights_ref, *refs,
):
    piece_refs, refs = refs[: len(slots)], refs[len(slots) :]
    activations_ref, theirs_ref, sums_ref, second_sums_ref, inputs, first, tiles, second_tiles, outputs, sems = refs
    position = position_ref[0]
    core = lax.rem(position, 2)
    own_rows = pl.ds(pl.multiple_of(core * near_ref.shape[0], near_ref.shape[0]), near_ref.shape[0])
    sides = tiles.shape[0]
    blocks, half, width = first.shape
    rows = blocks // sides
    deep = tiles.shape[1] // rows

    sources = ((0, own_ref.at[own_rows]), (1, near_ref), (2, far_ref), (3, cross_ref))
    for mask, ref in sources:
        for r in range(rows):
            block = (position ^ mask) * rows + r
            pltpu.make_async_copy(ref.at[:, pl.ds(r * width, width)], inputs.at[block], sems.at[0]).start()
    loads = [
        pltpu.make_async_copy(ref.at[layer], target.at[mask], sems.at[1 + 2 * layer + mask])
        for layer, target in ((0, tiles), (1, second_tiles)) for mask, ref in ((0, weights_ref), (1, near_weights_ref))
    ]

    def each_piece(slot, act):
        for i, (ref, own_slot) in enumerate(zip(piece_refs, slots)):
            if own_slot == slot:
                place = place_ref[i]

                @pl.when(place >= 0)
                def _():
                    target = tiles.at[slot, pl.ds(pl.multiple_of(place, 16), ref.shape[0])]
                    act(pltpu.make_async_copy(ref, target, sems.at[7 + i]))

    for load in loads[:2]:
        load.start()
    for slot in (2, 3):
        each_piece(slot, lambda copy: copy.start())
    for load in loads[2:]:
        load.start()
    pltpu.make_async_copy(inputs, inputs, sems.at[0]).wait()

    def outcome(parts, tile, row):
        result = jnp.dot(jnp.concatenate(parts, axis=1), tile, preferred_element_type=jnp.float32)
        return jnp.maximum(result + bias_ref[pl.ds(row, 1), :], 0.0).astype(jnp.bfloat16)

    def first_layer(mask, total):
        for slot in range(sides):
            @pl.when(mask == slot)
            def _():
                if slot < 2:
                    loads[slot].wait()
                else:
                    each_piece(slot, lambda copy: copy.wait())

        for r in range(rows):
            row = (position ^ mask) * rows + r
            parts = [inputs[block_ref[row * 4 + k]] for k in range(4)]
            first[row] = result = outcome(parts, tiles[mask, r * deep : (r + 1) * deep, :], row)
            total = total + result.astype(jnp.float32)
        return total

    def second_layer(step, total):
        mask = 1 - step
        for slot in range(2):
            @pl.when(mask == slot)
            def _():
                loads[2 + slot].wait()

        for r in range(rows):
            row = (position ^ mask) * rows + r + blocks
            parts = [first[block_ref[row * 4 + k]] for k in range(4)]
            result = outcome(parts, second_tiles[mask, r * deep : (r + 1) * deep, :], row)
            outputs[mask, :, r * width : (r + 1) * width] = result
            total = total + result.astype(jnp.float32)

        @pl.when(mask == 1)
        def _():
            pltpu.make_async_copy(outputs.at[1], theirs_ref, sems.at[5]).start()

        return total

    ones = jnp.ones((8, width), jnp.float32)

    def collapse(value):
        return lax.dot_general(
            ones, value, (((1,), (1,)), ((), ())), precision=lax.Precision.HIGHEST, preferred_element_type=jnp.float32
        )

    zero = jnp.zeros((half, width), jnp.float32)
    sums_ref[...] = collapse(lax.fori_loop(0, sides, first_layer, zero))
    second_total = lax.fori_loop(0, 2, second_layer, zero)
    mine = pltpu.make_async_copy(outputs.at[0], activations_ref.at[own_rows], sems.at[6])
    mine.start()
    second_sums_ref[...] = collapse(second_total)
    pltpu.make_async_copy(outputs.at[1], theirs_ref, sems.at[5]).wait()
    mine.wait()


def gather_far(weights, position, group, sides, groups):
    rows, width = weights.shape[1:]
    nrn = functools.partial(lax.ppermute, axis_name="nrn")
    both = functools.partial(lax.ppermute, axis_name=("img", "nrn"))
    piece_rows = rows // groups
    splits = 2 if piece_rows % 32 == 0 else 1
    part_rows = piece_rows // splits
    parts = []
    for h in range(splits):
        part = lax.dynamic_slice(weights, (0, group * piece_rows + h * part_rows, 0), (1, part_rows, width))[0]
        parts.append(nrn(part, perm=xor_pairs(sides, 2)))
    if groups % 2 or groups > 8:
        piece = jnp.concatenate(parts)
        far = lax.all_gather(piece, "img", axis=0, tiled=True)
        return [far, nrn(far, perm=xor_pairs(sides, 1))], [2, 3], jnp.zeros((2,), jnp.int32)

    line = groups // 2
    spot, side = group // 2, group % 2
    upward = lax.rem(position, 2) == 0

    def pairs(steps, move):
        found = []
        for g in range(groups):
            for n in range(sides):
                source = g // 2 - steps if n % 2 == 0 else g // 2 + steps
                target = move(g, n)
                if 0 <= source < line and 0 <= target[0] < groups:
                    found.append((g * sides + n, target[0] * sides + target[1]))
        return found

    def onward(g, n):
        return (g + 2 if n % 2 == 0 else g - 2), n

    def beside(g, n):
        return g ^ 1, n

    arrays, slots, places = [], [], []

    def keep(array, slot, steps, crossed, passed, offset=0):
        step = jnp.where(upward != passed, -steps, steps)
        source = spot + step
        row = (source * 2 + (1 - side if crossed else side)) * piece_rows + offset
        arrays.append(array)
        slots.append(slot)
        places.append(jnp.where((source >= 0) & (source < line), row, -1))

    for h, part in enumerate(parts):
        other = both(part, perm=pairs(0, beside))
        keep(other, 2, 0, True, False, h * part_rows)
        keep(nrn(other, perm=xor_pairs(sides, 1)), 3, 0, True, False, h * part_rows)
    piece = jnp.concatenate(parts)
    held = [piece, nrn(piece, perm=xor_pairs(sides, 1))]
    keep(held[0], 2, 0, False, False)
    keep(held[1], 3, 0, False, False)
    for s in range(1, line):
        for h in range(2):
            held[h] = both(held[h], perm=pairs(s - 1, onward))
            keep(held[h], 2 + h, s, False, False)
            keep(nrn(held[h], perm=xor_pairs(sides, 1)), 3 - h, s, False, True)
            other = both(held[h], perm=pairs(s, beside))
            keep(other, 2 + h, s, True, False)
            keep(nrn(other, perm=xor_pairs(sides, 1)), 3 - h, s, True, True)
    return arrays, slots, jnp.stack(places).astype(jnp.int32)


def per_device(images, weights, block_index, bias):
    layers, rows, deep, width = weights.shape
    count, shard = images.shape
    sides = lax.axis_size("nrn")
    groups = lax.axis_size("img")
    assert layers == 2 and sides == 4 and block_index.shape[-1] == 4
    neurons = shard * sides
    position = lax.axis_index("nrn")
    group = lax.axis_index("img")
    core = lax.rem(position, 2)
    half = count // 2
    nrn = functools.partial(lax.ppermute, axis_name="nrn")

    weights = weights.reshape(layers, rows * deep, width)
    pieces, slots, places = gather_far(weights, position, group, sides, groups)

    kept = lax.dynamic_slice(images, (core * half, 0), (half, shard))
    given = lax.dynamic_slice(images, ((1 - core) * half, 0), (half, shard))
    far = nrn(kept, perm=xor_pairs(sides, 2))
    cross = nrn(given, perm=xor_pairs(sides, 3))
    tables = position.reshape(1), places, block_index.reshape(-1), bias.reshape(layers * sides * rows, width)
    given, tables = lax.optimization_barrier((given, tables))
    near = nrn(given, perm=xor_pairs(sides, 1))
    near_weights = nrn(weights, perm=xor_pairs(sides, 1))

    any_space = pl.BlockSpec(memory_space=pl.ANY)
    smem = pl.BlockSpec(memory_space=pltpu.SMEM)
    vmem = pl.BlockSpec(memory_space=pltpu.VMEM)
    activations, theirs, first_sums, second_sums = pl.pallas_call(
        functools.partial(layers_kernel, slots),
        out_shape=(
            jax.ShapeDtypeStruct((count, shard), jnp.bfloat16),
            jax.ShapeDtypeStruct((half, shard), jnp.bfloat16),
            jax.ShapeDtypeStruct((8, half), jnp.float32),
            jax.ShapeDtypeStruct((8, half), jnp.float32),
        ),
        in_specs=[smem] * 3 + [vmem] + [any_space] * (6 + len(pieces)),
        out_specs=(any_space, any_space, vmem, vmem),
        scratch_shapes=[
            pltpu.VMEM((sides * rows, half, width), jnp.bfloat16),
            pltpu.VMEM((sides * rows, half, width), jnp.bfloat16),
            pltpu.VMEM((sides, rows * deep, width), jnp.bfloat16),
            pltpu.VMEM((2, rows * deep, width), jnp.bfloat16),
            pltpu.VMEM((2, half, shard), jnp.bfloat16),
            pltpu.SemaphoreType.DMA((7 + len(pieces),)),
        ],
        compiler_params=pltpu.CompilerParams(vmem_limit_bytes=36 * 2**20),
        cost_estimate=pl.CostEstimate(flops=12 * half * rows * deep * width, bytes_accessed=2**25, transcendentals=0),
    )(*tables, images, near, far, cross, weights, near_weights, *pieces)

    back = nrn(theirs, perm=xor_pairs(sides, 1))
    activations = lax.dynamic_update_slice(activations, back, ((1 - core) * half, 0))

    second_sums = second_sums + nrn(second_sums, perm=xor_pairs(sides, 2))
    totals = jnp.stack([first_sums[0], second_sums[0]])
    live = jnp.sum(jnp.minimum(1.0, totals / neurons / live_level), axis=1)
    if groups & (groups - 1):
        live = live + nrn(live, perm=xor_pairs(sides, 1))
        live = lax.psum(live, "img")
    else:
        live = live + nrn(live, perm=xor_pairs(sides, 1))
        mask = 1
        while mask < groups:
            live = live + lax.ppermute(live, "img", xor_pairs(groups, mask))
            mask *= 2
    return activations, live / (count * groups)


def solution(mesh):
    in_specs = (P("img", "nrn"), P(None, "nrn", None, None), P(), P())
    out_specs = (P("img", "nrn"), P())
    return jax.shard_map(
        per_device, mesh=mesh, in_specs=in_specs, out_specs=out_specs, check_vma=False
    )
```

time: 171 us -> 160 us (0.936)
  other arithmetic: 5.52 us -> 0.65 us
  local copies, waits for them, and re-layouts: 8.34 us -> 4.35 us
  Pallas kernels: 17.2 us -> 13.5 us
    ppermute x4 -> x7, waiting for transfers between devices: 19.4 us -> 14.3 us  [the longest x2 10.4 us: gather_far(): parts.append(nrn(part, perm=xor_pairs(sides, 2)))]
    ppermute x1, waiting for transfers between devices: 16.3 us -> 21.1 us  [per_device(): cross = nrn(given, perm=xor_pairs(sides, 3))]
    pallas_call x1, Pallas kernels: 17.2 us -> 13.5 us  [per_device(): pl.pallas_call(functools.partial(layers_kernel, slots), out_shape=(jax.Sh...]
    select_n x1 -> x0, other arithmetic: 3.58 us -> none  [per_device(): jnp.where(core == 0, jnp.concatenate([mine, back]), jnp.concatenate([back...]
    ppermute x4 -> x7, starting transfers between devices: 5.66 us -> 8.04 us  [the longest x2 3.82 us: gather_far(): other = both(part, perm=pairs(0, beside))]
    ppermute x6, starting transfers between devices: 11.6 us -> 9.73 us  [gather_far(): held[h] = both(held[h], perm=pairs(s - 1, onward))]
  transfers between devices with their start and end apart: 38 -> 41, of which waited for: 13 -> 15; matrix products, arithmetic and copies ran while one was open for 3% -> 2% of each run, Pallas kernels for 0% -> 0%
where the time goes in v1:
time: 160 us
  waiting for transfers between devices  73.1 us (46%)
  starting transfers between devices  67 us (42%)
  Pallas kernels  13.5 us (8%)
  local copies, waits for them, and re-layouts  4.35 us (3%)
    ppermute x6, starting transfers between devices, gather_far(): keep(nrn(held[h], perm=xor_pairs(sides, 1)), 3 - h, s, False, True)  30.1 us
    ppermute x1, waiting for transfers between devices, per_device(): cross = nrn(given, perm=xor_pairs(sides, 3))  21.1 us
    ppermute x1, waiting for transfers between devices, per_device(): far = nrn(kept, perm=xor_pairs(sides, 2))  16.2 us
    pallas_call x1, Pallas kernels, per_device(): pl.pallas_call(functools.partial(layers_kernel, slots), out_shape=(jax.Sh...  13.5 us
    ppermute x2, waiting for transfers between devices, gather_far(): parts.append(nrn(part, perm=xor_pairs(sides, 2)))  10.4 us
    ppermute x3, waiting for transfers between devices, per_device(): live = live + lax.ppermute(live, 'img', xor_pairs(groups, mask))  10.1 us
    ppermute x6, starting transfers between devices, gather_far(): held[h] = both(held[h], perm=pairs(s - 1, onward))  9.73 us
    ppermute x6, starting transfers between devices, gather_far(): keep(nrn(other, perm=xor_pairs(sides, 1)), 3 - h, s, True, True)  9.4 us
  transfers between devices with their start and end apart: 41, of which 15 were waited for; matrix products, arithmetic and copies ran while one was open for 2% of the time, Pallas kernels for 0%

profile of v1, /device:TPU:0, one launch (start us, length us, event | category | flops | bytes accessed | tf_op | source)
XLA Modules:
  0.0 159.7 jit_solution(2822731778884974874)
XLA Ops:
  0.6 0.6 collective-permute-start.3
  1.2 1.1 dynamic-slice_bitcast_fusion
  2.3 2.6 %collective-permute-start.7 = (bf16[1024,128]{1,0:T(8,128)(2,1)S(1)}, bf16[1024,128]{1,0:T(8,128)(2,1)S(1)}, u32[]{:S(2)}, u32[]{:S(2)}) collective-permute-start(bf16[1024,128]{1,0:T(8,128)(2,1)S(1)} %get-tuple-element.20), channel_id=1, source_target_pairs={{0,2},{1,3},{2,0},{3,1},{4,6},{5,7},{6,4},{7,5},{8,10},{9,11},{10,... | collective-permute-start | bytes 786440 | tf_op jit(solution)/shard_map/ppermute | solution.py:127
  4.9 7.1 %collective-permute-done.7 = bf16[1024,128]{1,0:T(8,128)(2,1)S(1)} collective-permute-done((bf16[1024,128]{1,0:T(8,128)(2,1)S(1)}, bf16[1024,128]{1,0:T(8,128)(2,1)S(1)}, u32[]{:S(2)}, u32[]{:S(2)}) %collective-permute-start.7) | collective-permute-done | bytes 262176 | tf_op jit(solution)/shard_map/ppermute | solution.py:127
  12.0 2.0 %collective-permute-start.8 = (bf16[1024,128]{1,0:T(8,128)(2,1)S(1)}, bf16[1024,128]{1,0:T(8,128)(2,1)S(1)}, u32[]{:S(2)}, u32[]{:S(2)}) collective-permute-start(bf16[1024,128]{1,0:T(8,128)(2,1)S(1)} %collective-permute-done.7), channel_id=1, source_target_pairs={{0,4},{1,5},{2,6},{3,7},{4,0},{5,1},{6,2},{7,3},{8,12},{9,13},{10,... | collective-permute-start | bytes 786440 | tf_op jit(solution)/shard_map/ppermute | solution.py:164
  14.0 3.4 %collective-permute-done.4 = bf16[1024,128]{1,0:T(8,128)(2,1)S(1)} collective-permute-done((bf16[1024,128]{1,0:T(8,128)(2,1)S(1)}, bf16[1024,128]{1,0:T(8,128)(2,1)S(1)}, u32[]{:S(2)}, u32[]{:S(2)}) %collective-permute-start.4) | collective-permute-done | bytes 262176 | tf_op jit(solution)/shard_map/ppermute | solution.py:127
  17.4 1.8 %collective-permute-start.5 = (bf16[1024,128]{1,0:T(8,128)(2,1)S(1)}, bf16[1024,128]{1,0:T(8,128)(2,1)S(1)}, u32[]{:S(2)}, u32[]{:S(2)}) collective-permute-start(bf16[1024,128]{1,0:T(8,128)(2,1)S(1)} %collective-permute-done.4), channel_id=1, source_target_pairs={{0,4},{1,5},{2,6},{3,7},{4,0},{5,1},{6,2},{7,3},{8,12},{9,13},{10,... | collective-permute-start | bytes 786440 | tf_op jit(solution)/shard_map/ppermute | solution.py:164
  19.2 1.7 %constant_dynamic-slice_fusion = (bf16[128,4096]{1,0:T(8,128)(2,1)S(1)}, bf16[128,4096]{1,0:T(8,128)(2,1)S(1)}) fusion(bf16[256,4096]{1,0:T(8,128)(2,1)} %own_ref.1, s32[]{:T(128)S(6)} %select_n.152, s32[]{:T(128)S(6)} %select_n.128), kind=kLoop, calls=%fused_computation.5 | loop fusion | bytes 4194312 | tf_op jit(solution)/shard_map/dynamic_slice | solution.py:198
  21.7 3.5 %collective-permute-start.11 = (bf16[2048,128]{1,0:T(8,128)(2,1)S(1)}, bf16[2048,128]{1,0:T(8,128)(2,1)S(1)}, u32[]{:S(2)}, u32[]{:S(2)}) collective-permute-start(bf16[2048,128]{1,0:T(8,128)(2,1)S(1)} %constant_dynamic-update-slice_fusion.refs_4_), channel_id=1, source_target_pairs={{0,8},{2,10},{4,12},{6,14},{8,16},{9,1},{10,18},{11,3},{12,20},{13... | collective-permute-start | bytes 1572872 | tf_op jit(solution)/shard_map/ppermute | solution.py:173
  25.5 1.5 collective-permute-start.1
  27.0 1.5 collective-permute-done.6.refs_1_
  28.5 1.0 collective-permute-start.2
  29.5 2.3 %collective-permute-done.11.refs_6_ = bf16[2048,128]{1,0:T(8,128)(2,1)S(1)} collective-permute-done((bf16[2048,128]{1,0:T(8,128)(2,1)S(1)}, bf16[2048,128]{1,0:T(8,128)(2,1)S(1)}, u32[]{:S(2)}, u32[]{:S(2)}) %collective-permute-start.11) | collective-permute-done | bytes 524320 | tf_op jit(solution)/shard_map/ppermute | solution.py:173
  31.8 0.5 collective-permute-start.10
  32.4 1.5 collective-permute-done.10.refs_5_
  33.9 0.7 collective-permute-start.19
  34.6 0.7 collective-permute-start.13
  35.3 16.2 %collective-permute-done.1.far_ref = bf16[128,4096]{1,0:T(8,128)(2,1)S(1)} collective-permute-done((bf16[128,4096]{1,0:T(8,128)(2,1)S(1)}, bf16[128,4096]{1,0:T(8,128)(2,1)S(1)}, u32[]{:S(2)}, u32[]{:S(2)}) %collective-permute-start.1) | collective-permute-done | bytes 1048608 | tf_op jit(solution)/shard_map/ppermute | solution.py:200
  51.5 21.1 %collective-permute-done.2.cross_ref = bf16[128,4096]{1,0:T(8,128)(2,1)S(1)} collective-permute-done((bf16[128,4096]{1,0:T(8,128)(2,1)S(1)}, bf16[128,4096]{1,0:T(8,128)(2,1)S(1)}, u32[]{:S(2)}, u32[]{:S(2)}) %collective-permute-start.2) | collective-permute-done | bytes 1048608 | tf_op jit(solution)/shard_map/ppermute | solution.py:201
  72.6 3.5 %collective-permute-start.15 = (bf16[2048,128]{1,0:T(8,128)(2,1)S(1)}, bf16[2048,128]{1,0:T(8,128)(2,1)S(1)}, u32[]{:S(2)}, u32[]{:S(2)}) collective-permute-start(bf16[2048,128]{1,0:T(8,128)(2,1)S(1)} %collective-permute-done.10.refs_5_), channel_id=1, source_target_pairs={{0,8},{2,10},{4,12},{6,14},{8,16},{9,1},{10,18},{11,3},{12,20},{13... | collective-permute-start | bytes 1572872 | tf_op jit(solution)/shard_map/ppermute | solution.py:173
  76.1 0.7 collective-permute-start.27
  76.8 0.7 collective-permute-start.21
  77.5 0.4 collective-permute-start.20
  78.0 4.8 %collective-permute-done.15.refs_10_ = bf16[2048,128]{1,0:T(8,128)(2,1)S(1)} collective-permute-done((bf16[2048,128]{1,0:T(8,128)(2,1)S(1)}, bf16[2048,128]{1,0:T(8,128)(2,1)S(1)}, u32[]{:S(2)}, u32[]{:S(2)}) %collective-permute-start.15) | collective-permute-done | bytes 524320 | tf_op jit(solution)/shard_map/ppermute | solution.py:173
  83.0 0.7 collective-permute-start.23
  83.7 0.7 collective-permute-start.17
  84.5 7.7 %collective-permute-start.16 = (bf16[2048,128]{1,0:T(8,128)(2,1)S(1)}, bf16[2048,128]{1,0:T(8,128)(2,1)S(1)}, u32[]{:S(2)}, u32[]{:S(2)}) collective-permute-start(bf16[2048,128]{1,0:T(8,128)(2,1)S(1)} %collective-permute-done.15.refs_10_), channel_id=1, source_target_pairs={{0,1},{1,0},{2,3},{3,2},{4,5},{5,4},{6,7},{7,6},{8,9},{9,8},{10,11... | collective-permute-start | bytes 1572872 | tf_op jit(solution)/shard_map/ppermute | solution.py:175
  92.2 0.7 collective-permute-start.29
  92.9 5.7 %collective-permute-start.28 = (bf16[2048,128]{1,0:T(8,128)(2,1)S(1)}, bf16[2048,128]{1,0:T(8,128)(2,1)S(1)}, u32[]{:S(2)}, u32[]{:S(2)}) collective-permute-start(bf16[2048,128]{1,0:T(8,128)(2,1)S(1)} %collective-permute-done.27.refs_22_), channel_id=1, source_target_pairs={{0,1},{1,0},{2,3},{3,2},{4,5},{5,4},{6,7},{7,6},{8,9},{9,8},{10,11... | collective-permute-start | bytes 1572872 | tf_op jit(solution)/shard_map/ppermute | solution.py:175
  98.6 1.3 collective-permute-start.22
  99.9 0.7 collective-permute-start.31
  100.6 0.7 collective-permute-start.25
  101.3 6.4 %collective-permute-start.24 = (bf16[2048,128]{1,0:T(8,128)(2,1)S(1)}, bf16[2048,128]{1,0:T(8,128)(2,1)S(1)}, u32[]{:S(2)}, u32[]{:S(2)}) collective-permute-start(bf16[2048,128]{1,0:T(8,128)(2,1)S(1)} %collective-permute-done.23.refs_18_), channel_id=1, source_target_pairs={{0,1},{1,0},{2,3},{3,2},{4,5},{5,4},{6,7},{7,6},{8,9},{9,8},{10,11... | collective-permute-start | bytes 1572872 | tf_op jit(solution)/shard_map/ppermute | solution.py:175
  107.8 0.7 collective-permute-start.33
  108.5 9.8 %collective-permute-start.32 = (bf16[2048,128]{1,0:T(8,128)(2,1)S(1)}, bf16[2048,128]{1,0:T(8,128)(2,1)S(1)}, u32[]{:S(2)}, u32[]{:S(2)}) collective-permute-start(bf16[2048,128]{1,0:T(8,128)(2,1)S(1)} %collective-permute-done.31.refs_26_), channel_id=1, source_target_pairs={{0,1},{1,0},{2,3},{3,2},{4,5},{5,4},{6,7},{7,6},{8,9},{9,8},{10,11... | collective-permute-start | bytes 1572872 | tf_op jit(solution)/shard_map/ppermute | solution.py:175
  118.8 7.2 %collective-permute-start.34 = (bf16[2048,128]{1,0:T(8,128)(2,1)S(1)}, bf16[2048,128]{1,0:T(8,128)(2,1)S(1)}, u32[]{:S(2)}, u32[]{:S(2)}) collective-permute-start(bf16[2048,128]{1,0:T(8,128)(2,1)S(1)} %collective-permute-done.33.refs_28_), channel_id=1, source_target_pairs={{0,1},{1,0},{2,3},{3,2},{4,5},{5,4},{6,7},{7,6},{8,9},{9,8},{10,11... | collective-permute-start | bytes 1572872 | tf_op jit(solution)/shard_map/ppermute | solution.py:178
  126.0 1.5 collective-permute-done.34.refs_29_
  127.6 13.5 %shard_map.59 = (bf16[256,4096]{1,0:T(8,128)(2,1)}, bf16[128,4096]{1,0:T(8,128)(2,1)S(1)}, f32[8,128]{1,0:T(8,128)S(1)}, f32[8,128]{1,0:T(8,128)S(1)}) custom-call(s32[1]{0:T(128)} %bitcast.position_ref, s32[30]{0:T(128)S(1)} %stack.81.place_ref, s32[1024]{0:T(1024)S(1)} %reshape.17.block_ref, f32[256,128]{1,0:T(8,128)S(1)} %reshape.18.bias_ref, ...), custom_call_target="tpu_custom_call" | custom-call | flops 3221225472 | bytes 33554432 | tf_op jit(solution)/shard_map/pallas_call | solution.py:210
  141.5 1.5 collective-permute-start.36
  143.0 2.1 %collective-permute-done.36 = f32[8,128]{1,0:T(8,128)S(1)} collective-permute-done((f32[8,128]{1,0:T(8,128)S(1)}, f32[8,128]{1,0:T(8,128)S(1)}, u32[]{:S(2)}, u32[]{:S(2)}) %collective-permute-start.36) | collective-permute-done | bytes 4128 | tf_op jit(solution)/shard_map/ppermute | solution.py:235
  145.3 1.1 collective-permute-done.37
  146.5 0.5 collective-permute-start.38
  147.0 3.1 %collective-permute-done.38 = f32[2]{0:T(128)S(1)} collective-permute-done((f32[2]{0:T(128)S(1)}, f32[2]{0:T(128)S(1)}, u32[]{:S(2)}, u32[]{:S(2)}) %collective-permute-start.38) | collective-permute-done | bytes 40 | tf_op jit(solution)/shard_map/ppermute | solution.py:245
  150.1 3.6 %collective-permute-done.39 = f32[2]{0:T(128)S(1)} collective-permute-done((f32[2]{0:T(128)S(1)}, f32[2]{0:T(128)S(1)}, u32[]{:S(2)}, u32[]{:S(2)}) %collective-permute-start.39) | collective-permute-done | bytes 40 | tf_op jit(solution)/shard_map/ppermute | solution.py:245
  153.6 1.0 collective-permute-start.40
  154.6 3.5 %collective-permute-done.40 = f32[2]{0:T(128)S(1)} collective-permute-done((f32[2]{0:T(128)S(1)}, f32[2]{0:T(128)S(1)}, u32[]{:S(2)}, u32[]{:S(2)}) %collective-permute-start.40) | collective-permute-done | bytes 40 | tf_op jit(solution)/shard_map/ppermute | solution.py:245
  158.1 0.5 add_multiply_fusion
  158.6 1.1 constant_dynamic-update-slice_fusion.2
  (58 shorter events, 2.6 us)
Async XLA Ops:
  0.6 126.9 %collective-permute-start.3 = (bf16[2,16384,128]{2,1,0:T(8,128)(2,1)}, bf16[2,16384,128]{2,1,0:T(8,128)(2,1)}, u32[]{:S(2)}, u32[]{:S(2)}) collective-permute-start(bf16[2,16384,128]{2,1,0:T(8,128)(2,1)} %bitcast.21), channel_id=1, source_target_pairs={{0,1},{1,0},{2,3},{3,2},{4,5},{5,4},{6,7},{7,6},{8,9},{9,8},{10,11... | collective-permute-start | bytes 25165832 | tf_op jit(solution)/shard_map/ppermute | solution.py:205
  2.3 9.7 %collective-permute-start.7 = (bf16[1024,128]{1,0:T(8,128)(2,1)S(1)}, bf16[1024,128]{1,0:T(8,128)(2,1)S(1)}, u32[]{:S(2)}, u32[]{:S(2)}) collective-permute-start(bf16[1024,128]{1,0:T(8,128)(2,1)S(1)} %get-tuple-element.20), channel_id=1, source_target_pairs={{0,2},{1,3},{2,0},{3,1},{4,6},{5,7},{6,4},{7,5},{8,10},{9,11},{10,... | collective-permute-start | bytes 786440 | tf_op jit(solution)/shard_map/ppermute | solution.py:127
  4.8 12.6 %collective-permute-start.4 = (bf16[1024,128]{1,0:T(8,128)(2,1)S(1)}, bf16[1024,128]{1,0:T(8,128)(2,1)S(1)}, u32[]{:S(2)}, u32[]{:S(2)}) collective-permute-start(bf16[1024,128]{1,0:T(8,128)(2,1)S(1)} %get-tuple-element.21), channel_id=1, source_target_pairs={{0,2},{1,3},{2,0},{3,1},{4,6},{5,7},{6,4},{7,5},{8,10},{9,11},{10,... | collective-permute-start | bytes 786440 | tf_op jit(solution)/shard_map/ppermute | solution.py:127
  4.9 16.1 %copy-start.2 = (s32[2,128,4]{1,2,0:T(4,128)S(1)}, s32[2,128,4]{1,2,0:T(4,128)}, u32[]{:S(2)}) copy-start(s32[2,128,4]{1,2,0:T(4,128)} %param.6) | copy-start | bytes 12292
  4.9 16.4 %copy-start.1 = (f32[2,16384]{1,0:T(2,128)S(1)}, f32[2,16384]{1,0:T(2,128)}, u32[]{:S(2)}) copy-start(f32[2,16384]{1,0:T(2,128)} %param.7) | copy-start | bytes 393220
  12.0 9.6 %collective-permute-start.8 = (bf16[1024,128]{1,0:T(8,128)(2,1)S(1)}, bf16[1024,128]{1,0:T(8,128)(2,1)S(1)}, u32[]{:S(2)}, u32[]{:S(2)}) collective-permute-start(bf16[1024,128]{1,0:T(8,128)(2,1)S(1)} %collective-permute-done.7), channel_id=1, source_target_pairs={{0,4},{1,5},{2,6},{3,7},{4,0},{5,1},{6,2},{7,3},{8,12},{9,13},{10,... | collective-permute-start | bytes 786440 | tf_op jit(solution)/shard_map/ppermute | solution.py:164
  17.4 8.1 %collective-permute-start.5 = (bf16[1024,128]{1,0:T(8,128)(2,1)S(1)}, bf16[1024,128]{1,0:T(8,128)(2,1)S(1)}, u32[]{:S(2)}, u32[]{:S(2)}) collective-permute-start(bf16[1024,128]{1,0:T(8,128)(2,1)S(1)} %collective-permute-done.4), channel_id=1, source_target_pairs={{0,4},{1,5},{2,6},{3,7},{4,0},{5,1},{6,2},{7,3},{8,12},{9,13},{10,... | collective-permute-start | bytes 786440 | tf_op jit(solution)/shard_map/ppermute | solution.py:164
  21.5 5.4 %collective-permute-start.9 = (bf16[1024,128]{1,0:T(8,128)(2,1)S(1)}, bf16[1024,128]{1,0:T(8,128)(2,1)S(1)}, u32[]{:S(2)}, u32[]{:S(2)}) collective-permute-start(bf16[1024,128]{1,0:T(8,128)(2,1)S(1)} %collective-permute-done.8.refs_2_), channel_id=1, source_target_pairs={{0,1},{1,0},{2,3},{3,2},{4,5},{5,4},{6,7},{7,6},{8,9},{9,8},{10,11... | collective-permute-start | bytes 786440 | tf_op jit(solution)/shard_map/ppermute | solution.py:166
  21.7 10.2 %collective-permute-start.11 = (bf16[2048,128]{1,0:T(8,128)(2,1)S(1)}, bf16[2048,128]{1,0:T(8,128)(2,1)S(1)}, u32[]{:S(2)}, u32[]{:S(2)}) collective-permute-start(bf16[2048,128]{1,0:T(8,128)(2,1)S(1)} %constant_dynamic-update-slice_fusion.refs_4_), channel_id=1, source_target_pairs={{0,8},{2,10},{4,12},{6,14},{8,16},{9,1},{10,18},{11,3},{12,20},{13... | collective-permute-start | bytes 1572872 | tf_op jit(solution)/shard_map/ppermute | solution.py:173
  25.2 9.4 %collective-permute-start = (bf16[128,4096]{1,0:T(8,128)(2,1)S(1)}, bf16[128,4096]{1,0:T(8,128)(2,1)S(1)}, u32[]{:S(2)}, u32[]{:S(2)}) collective-permute-start(bf16[128,4096]{1,0:T(8,128)(2,1)S(1)} %get-tuple-element.15), channel_id=1, source_target_pairs={{0,1},{1,0},{2,3},{3,2},{4,5},{5,4},{6,7},{7,6},{8,9},{9,8},{10,11... | collective-permute-start | bytes 3145736 | tf_op jit(solution)/shard_map/ppermute | solution.py:204
  25.5 26.0 %collective-permute-start.1 = (bf16[128,4096]{1,0:T(8,128)(2,1)S(1)}, bf16[128,4096]{1,0:T(8,128)(2,1)S(1)}, u32[]{:S(2)}, u32[]{:S(2)}) collective-permute-start(bf16[128,4096]{1,0:T(8,128)(2,1)S(1)} %get-tuple-element.22), channel_id=1, source_target_pairs={{0,2},{1,3},{2,0},{3,1},{4,6},{5,7},{6,4},{7,5},{8,10},{9,11},{10,... | collective-permute-start | bytes 3145736 | tf_op jit(solution)/shard_map/ppermute | solution.py:200
  27.0 1.5 collective-permute-start.6
  28.5 44.1 %collective-permute-start.2 = (bf16[128,4096]{1,0:T(8,128)(2,1)S(1)}, bf16[128,4096]{1,0:T(8,128)(2,1)S(1)}, u32[]{:S(2)}, u32[]{:S(2)}) collective-permute-start(bf16[128,4096]{1,0:T(8,128)(2,1)S(1)} %get-tuple-element.15), channel_id=1, source_target_pairs={{0,3},{1,2},{2,1},{3,0},{4,7},{5,6},{6,5},{7,4},{8,11},{9,10},{10,... | collective-permute-start | bytes 3145736 | tf_op jit(solution)/shard_map/ppermute | solution.py:201
  31.8 2.1 %collective-permute-start.10 = (bf16[2048,128]{1,0:T(8,128)(2,1)S(1)}, bf16[2048,128]{1,0:T(8,128)(2,1)S(1)}, u32[]{:S(2)}, u32[]{:S(2)}) collective-permute-start(bf16[2048,128]{1,0:T(8,128)(2,1)S(1)} %constant_dynamic-update-slice_fusion.refs_4_), channel_id=1, source_target_pairs={{0,1},{1,0},{2,3},{3,2},{4,5},{5,4},{6,7},{7,6},{8,9},{9,8},{10,11... | collective-permute-start | bytes 1572872 | tf_op jit(solution)/shard_map/ppermute | solution.py:168
  33.9 42.2 %collective-permute-start.19 = (bf16[2048,128]{1,0:T(8,128)(2,1)S(1)}, bf16[2048,128]{1,0:T(8,128)(2,1)S(1)}, u32[]{:S(2)}, u32[]{:S(2)}) collective-permute-start(bf16[2048,128]{1,0:T(8,128)(2,1)S(1)} %collective-permute-done.11.refs_6_), channel_id=1, source_target_pairs={{8,16},{9,1},{10,18},{11,3},{12,20},{13,5},{14,22},{15,7},{16,24},... | collective-permute-start | bytes 1572872 | tf_op jit(solution)/shard_map/ppermute | solution.py:173
  34.6 42.2 %collective-permute-start.13 = (bf16[2048,128]{1,0:T(8,128)(2,1)S(1)}, bf16[2048,128]{1,0:T(8,128)(2,1)S(1)}, u32[]{:S(2)}, u32[]{:S(2)}) collective-permute-start(bf16[2048,128]{1,0:T(8,128)(2,1)S(1)} %collective-permute-done.11.refs_6_), channel_id=1, source_target_pairs={{1,5},{3,7},{5,1},{7,3},{8,12},{9,13},{10,14},{11,15},{12,8},{13,9... | collective-permute-start | bytes 1572872 | tf_op jit(solution)/shard_map/ppermute | solution.py:176
  51.5 26.0 %collective-permute-start.12 = (bf16[2048,128]{1,0:T(8,128)(2,1)S(1)}, bf16[2048,128]{1,0:T(8,128)(2,1)S(1)}, u32[]{:S(2)}, u32[]{:S(2)}) collective-permute-start(bf16[2048,128]{1,0:T(8,128)(2,1)S(1)} %collective-permute-done.11.refs_6_), channel_id=1, source_target_pairs={{0,1},{1,0},{2,3},{3,2},{4,5},{5,4},{6,7},{7,6},{8,9},{9,8},{10,11... | collective-permute-start | bytes 1572872 | tf_op jit(solution)/shard_map/ppermute | solution.py:175
  72.6 55.0 %copy-start = (bf16[128,4096]{1,0:T(8,128)(2,1)}, bf16[128,4096]{1,0:T(8,128)(2,1)S(1)}, u32[]{:S(2)}) copy-start(bf16[128,4096]{1,0:T(8,128)(2,1)S(1)} %collective-permute-done.2.cross_ref) | copy-start | bytes 3145732
  72.6 10.1 %collective-permute-start.15 = (bf16[2048,128]{1,0:T(8,128)(2,1)S(1)}, bf16[2048,128]{1,0:T(8,128)(2,1)S(1)}, u32[]{:S(2)}, u32[]{:S(2)}) collective-permute-start(bf16[2048,128]{1,0:T(8,128)(2,1)S(1)} %collective-permute-done.10.refs_5_), channel_id=1, source_target_pairs={{0,8},{2,10},{4,12},{6,14},{8,16},{9,1},{10,18},{11,3},{12,20},{13... | collective-permute-start | bytes 1572872 | tf_op jit(solution)/shard_map/ppermute | solution.py:173
  76.1 7.0 %collective-permute-start.27 = (bf16[2048,128]{1,0:T(8,128)(2,1)S(1)}, bf16[2048,128]{1,0:T(8,128)(2,1)S(1)}, u32[]{:S(2)}, u32[]{:S(2)}) collective-permute-start(bf16[2048,128]{1,0:T(8,128)(2,1)S(1)} %collective-permute-done.19.refs_14_), channel_id=1, source_target_pairs={{9,1},{11,3},{13,5},{15,7},{16,24},{18,26},{20,28},{22,30}} | collective-permute-start | bytes 1572872 | tf_op jit(solution)/shard_map/ppermute | solution.py:173
  76.8 6.9 %collective-permute-start.21 = (bf16[2048,128]{1,0:T(8,128)(2,1)S(1)}, bf16[2048,128]{1,0:T(8,128)(2,1)S(1)}, u32[]{:S(2)}, u32[]{:S(2)}) collective-permute-start(bf16[2048,128]{1,0:T(8,128)(2,1)S(1)} %collective-permute-done.19.refs_14_), channel_id=1, source_target_pairs={{1,5},{3,7},{5,1},{7,3},{9,13},{11,15},{13,9},{15,11},{16,20},{18,... | collective-permute-start | bytes 1572872 | tf_op jit(solution)/shard_map/ppermute | solution.py:176
  77.5 6.9 %collective-permute-start.20 = (bf16[2048,128]{1,0:T(8,128)(2,1)S(1)}, bf16[2048,128]{1,0:T(8,128)(2,1)S(1)}, u32[]{:S(2)}, u32[]{:S(2)}) collective-permute-start(bf16[2048,128]{1,0:T(8,128)(2,1)S(1)} %collective-permute-done.19.refs_14_), channel_id=1, source_target_pairs={{0,1},{1,0},{2,3},{3,2},{4,5},{5,4},{6,7},{7,6},{8,9},{9,8},{10,11... | collective-permute-start | bytes 1572872 | tf_op jit(solution)/shard_map/ppermute | solution.py:175
  82.7 9.4 %collective-permute-start.14 = (bf16[2048,128]{1,0:T(8,128)(2,1)S(1)}, bf16[2048,128]{1,0:T(8,128)(2,1)S(1)}, u32[]{:S(2)}, u32[]{:S(2)}) collective-permute-start(bf16[2048,128]{1,0:T(8,128)(2,1)S(1)} %collective-permute-done.13.refs_8_), channel_id=1, source_target_pairs={{0,1},{1,0},{2,3},{3,2},{4,5},{5,4},{6,7},{7,6},{8,9},{9,8},{10,11... | collective-permute-start | bytes 1572872 | tf_op jit(solution)/shard_map/ppermute | solution.py:178
  83.0 9.8 %collective-permute-start.23 = (bf16[2048,128]{1,0:T(8,128)(2,1)S(1)}, bf16[2048,128]{1,0:T(8,128)(2,1)S(1)}, u32[]{:S(2)}, u32[]{:S(2)}) collective-permute-start(bf16[2048,128]{1,0:T(8,128)(2,1)S(1)} %collective-permute-done.15.refs_10_), channel_id=1, source_target_pairs={{8,16},{9,1},{10,18},{11,3},{12,20},{13,5},{14,22},{15,7},{16,24},... | collective-permute-start | bytes 1572872 | tf_op jit(solution)/shard_map/ppermute | solution.py:173
  83.7 14.8 %collective-permute-start.17 = (bf16[2048,128]{1,0:T(8,128)(2,1)S(1)}, bf16[2048,128]{1,0:T(8,128)(2,1)S(1)}, u32[]{:S(2)}, u32[]{:S(2)}) collective-permute-start(bf16[2048,128]{1,0:T(8,128)(2,1)S(1)} %collective-permute-done.15.refs_10_), channel_id=1, source_target_pairs={{1,5},{3,7},{5,1},{7,3},{8,12},{9,13},{10,14},{11,15},{12,8},{13,9... | collective-permute-start | bytes 1572872 | tf_op jit(solution)/shard_map/ppermute | solution.py:176
  84.5 15.4 %collective-permute-start.16 = (bf16[2048,128]{1,0:T(8,128)(2,1)S(1)}, bf16[2048,128]{1,0:T(8,128)(2,1)S(1)}, u32[]{:S(2)}, u32[]{:S(2)}) collective-permute-start(bf16[2048,128]{1,0:T(8,128)(2,1)S(1)} %collective-permute-done.15.refs_10_), channel_id=1, source_target_pairs={{0,1},{1,0},{2,3},{3,2},{4,5},{5,4},{6,7},{7,6},{8,9},{9,8},{10,11... | collective-permute-start | bytes 1572872 | tf_op jit(solution)/shard_map/ppermute | solution.py:175
  92.2 8.4 %collective-permute-start.29 = (bf16[2048,128]{1,0:T(8,128)(2,1)S(1)}, bf16[2048,128]{1,0:T(8,128)(2,1)S(1)}, u32[]{:S(2)}, u32[]{:S(2)}) collective-permute-start(bf16[2048,128]{1,0:T(8,128)(2,1)S(1)} %collective-permute-done.27.refs_22_), channel_id=1, source_target_pairs={{1,5},{3,7},{5,1},{7,3},{24,28},{26,30},{28,24},{30,26}} | collective-permute-start | bytes 1572872 | tf_op jit(solution)/shard_map/ppermute | solution.py:176
  92.9 8.4 %collective-permute-start.28 = (bf16[2048,128]{1,0:T(8,128)(2,1)S(1)}, bf16[2048,128]{1,0:T(8,128)(2,1)S(1)}, u32[]{:S(2)}, u32[]{:S(2)}) collective-permute-start(bf16[2048,128]{1,0:T(8,128)(2,1)S(1)} %collective-permute-done.27.refs_22_), channel_id=1, source_target_pairs={{0,1},{1,0},{2,3},{3,2},{4,5},{5,4},{6,7},{7,6},{8,9},{9,8},{10,11... | collective-permute-start | bytes 1572872 | tf_op jit(solution)/shard_map/ppermute | solution.py:175
  98.6 9.1 %collective-permute-start.22 = (bf16[2048,128]{1,0:T(8,128)(2,1)S(1)}, bf16[2048,128]{1,0:T(8,128)(2,1)S(1)}, u32[]{:S(2)}, u32[]{:S(2)}) collective-permute-start(bf16[2048,128]{1,0:T(8,128)(2,1)S(1)} %collective-permute-done.21.refs_16_), channel_id=1, source_target_pairs={{0,1},{1,0},{2,3},{3,2},{4,5},{5,4},{6,7},{7,6},{8,9},{9,8},{10,11... | collective-permute-start | bytes 1572872 | tf_op jit(solution)/shard_map/ppermute | solution.py:178
  99.9 7.9 %collective-permute-start.31 = (bf16[2048,128]{1,0:T(8,128)(2,1)S(1)}, bf16[2048,128]{1,0:T(8,128)(2,1)S(1)}, u32[]{:S(2)}, u32[]{:S(2)}) collective-permute-start(bf16[2048,128]{1,0:T(8,128)(2,1)S(1)} %collective-permute-done.23.refs_18_), channel_id=1, source_target_pairs={{9,1},{11,3},{13,5},{15,7},{16,24},{18,26},{20,28},{22,30}} | collective-permute-start | bytes 1572872 | tf_op jit(solution)/shard_map/ppermute | solution.py:173
  100.6 7.9 %collective-permute-start.25 = (bf16[2048,128]{1,0:T(8,128)(2,1)S(1)}, bf16[2048,128]{1,0:T(8,128)(2,1)S(1)}, u32[]{:S(2)}, u32[]{:S(2)}) collective-permute-start(bf16[2048,128]{1,0:T(8,128)(2,1)S(1)} %collective-permute-done.23.refs_18_), channel_id=1, source_target_pairs={{1,5},{3,7},{5,1},{7,3},{9,13},{11,15},{13,9},{15,11},{16,20},{18,... | collective-permute-start | bytes 1572872 | tf_op jit(solution)/shard_map/ppermute | solution.py:176
  101.3 17.0 %collective-permute-start.24 = (bf16[2048,128]{1,0:T(8,128)(2,1)S(1)}, bf16[2048,128]{1,0:T(8,128)(2,1)S(1)}, u32[]{:S(2)}, u32[]{:S(2)}) collective-permute-start(bf16[2048,128]{1,0:T(8,128)(2,1)S(1)} %collective-permute-done.23.refs_18_), channel_id=1, source_target_pairs={{0,1},{1,0},{2,3},{3,2},{4,5},{5,4},{6,7},{7,6},{8,9},{9,8},{10,11... | collective-permute-start | bytes 1572872 | tf_op jit(solution)/shard_map/ppermute | solution.py:175
  107.7 10.7 %collective-permute-start.18 = (bf16[2048,128]{1,0:T(8,128)(2,1)S(1)}, bf16[2048,128]{1,0:T(8,128)(2,1)S(1)}, u32[]{:S(2)}, u32[]{:S(2)}) collective-permute-start(bf16[2048,128]{1,0:T(8,128)(2,1)S(1)} %collective-permute-done.17.refs_12_), channel_id=1, source_target_pairs={{0,1},{1,0},{2,3},{3,2},{4,5},{5,4},{6,7},{7,6},{8,9},{9,8},{10,11... | collective-permute-start | bytes 1572872 | tf_op jit(solution)/shard_map/ppermute | solution.py:178
  107.8 11.0 %collective-permute-start.33 = (bf16[2048,128]{1,0:T(8,128)(2,1)S(1)}, bf16[2048,128]{1,0:T(8,128)(2,1)S(1)}, u32[]{:S(2)}, u32[]{:S(2)}) collective-permute-start(bf16[2048,128]{1,0:T(8,128)(2,1)S(1)} %collective-permute-done.31.refs_26_), channel_id=1, source_target_pairs={{1,5},{3,7},{5,1},{7,3},{24,28},{26,30},{28,24},{30,26}} | collective-permute-start | bytes 1572872 | tf_op jit(solution)/shard_map/ppermute | solution.py:176
  108.5 17.5 %collective-permute-start.32 = (bf16[2048,128]{1,0:T(8,128)(2,1)S(1)}, bf16[2048,128]{1,0:T(8,128)(2,1)S(1)}, u32[]{:S(2)}, u32[]{:S(2)}) collective-permute-start(bf16[2048,128]{1,0:T(8,128)(2,1)S(1)} %collective-permute-done.31.refs_26_), channel_id=1, source_target_pairs={{0,1},{1,0},{2,3},{3,2},{4,5},{5,4},{6,7},{7,6},{8,9},{9,8},{10,11... | collective-permute-start | bytes 1572872 | tf_op jit(solution)/shard_map/ppermute | solution.py:175
  118.3 7.7 %collective-permute-start.30 = (bf16[2048,128]{1,0:T(8,128)(2,1)S(1)}, bf16[2048,128]{1,0:T(8,128)(2,1)S(1)}, u32[]{:S(2)}, u32[]{:S(2)}) collective-permute-start(bf16[2048,128]{1,0:T(8,128)(2,1)S(1)} %collective-permute-done.29.refs_24_), channel_id=1, source_target_pairs={{0,1},{1,0},{2,3},{3,2},{4,5},{5,4},{6,7},{7,6},{8,9},{9,8},{10,11... | collective-permute-start | bytes 1572872 | tf_op jit(solution)/shard_map/ppermute | solution.py:178
  118.4 7.6 %collective-permute-start.26 = (bf16[2048,128]{1,0:T(8,128)(2,1)S(1)}, bf16[2048,128]{1,0:T(8,128)(2,1)S(1)}, u32[]{:S(2)}, u32[]{:S(2)}) collective-permute-start(bf16[2048,128]{1,0:T(8,128)(2,1)S(1)} %collective-permute-done.25.refs_20_), channel_id=1, source_target_pairs={{0,1},{1,0},{2,3},{3,2},{4,5},{5,4},{6,7},{7,6},{8,9},{9,8},{10,11... | collective-permute-start | bytes 1572872 | tf_op jit(solution)/shard_map/ppermute | solution.py:178
  118.8 8.7 %collective-permute-start.34 = (bf16[2048,128]{1,0:T(8,128)(2,1)S(1)}, bf16[2048,128]{1,0:T(8,128)(2,1)S(1)}, u32[]{:S(2)}, u32[]{:S(2)}) collective-permute-start(bf16[2048,128]{1,0:T(8,128)(2,1)S(1)} %collective-permute-done.33.refs_28_), channel_id=1, source_target_pairs={{0,1},{1,0},{2,3},{3,2},{4,5},{5,4},{6,7},{7,6},{8,9},{9,8},{10,11... | collective-permute-start | bytes 1572872 | tf_op jit(solution)/shard_map/ppermute | solution.py:178
  141.1 17.5 %collective-permute-start.35 = (bf16[128,4096]{1,0:T(8,128)(2,1)S(1)}, bf16[128,4096]{1,0:T(8,128)(2,1)S(1)}, u32[]{:S(2)}, u32[]{:S(2)}) collective-permute-start(bf16[128,4096]{1,0:T(8,128)(2,1)S(1)} %get-tuple-element.17), channel_id=1, source_target_pairs={{0,1},{1,0},{2,3},{3,2},{4,5},{5,4},{6,7},{7,6},{8,9},{9,8},{10,11... | collective-permute-start | bytes 3145736 | tf_op jit(solution)/shard_map/ppermute | solution.py:232
  141.5 3.6 %collective-permute-start.36 = (f32[8,128]{1,0:T(8,128)S(1)}, f32[8,128]{1,0:T(8,128)S(1)}, u32[]{:S(2)}, u32[]{:S(2)}) collective-permute-start(f32[8,128]{1,0:T(8,128)S(1)} %get-tuple-element.19), channel_id=1, source_target_pairs={{0,2},{1,3},{2,0},{3,1},{4,6},{5,7},{6,4},{7,5},{8,10},{9,11},{10,... | collective-permute-start | bytes 12296 | tf_op jit(solution)/shard_map/ppermute | solution.py:235
  145.3 1.2 collective-permute-start.37
  146.5 3.6 %collective-permute-start.38 = (f32[2]{0:T(128)S(1)}, f32[2]{0:T(128)S(1)}, u32[]{:S(2)}, u32[]{:S(2)}) collective-permute-start(f32[2]{0:T(128)S(1)} %add.170), channel_id=1, source_target_pairs={{0,4},{4,0},{8,12},{12,8},{16,20},{20,16},{24,28},{28,24},{1,5},{5... | collective-permute-start | bytes 32 | tf_op jit(solution)/shard_map/ppermute | solution.py:245
  150.1 3.6 %collective-permute-start.39 = (f32[2]{0:T(128)S(1)}, f32[2]{0:T(128)S(1)}, u32[]{:S(2)}, u32[]{:S(2)}) collective-permute-start(f32[2]{0:T(128)S(1)} %add.171), channel_id=1, source_target_pairs={{0,8},{4,12},{8,0},{12,4},{16,24},{20,28},{24,16},{28,20},{1,9},{5... | collective-permute-start | bytes 32 | tf_op jit(solution)/shard_map/ppermute | solution.py:245
  153.6 4.5 %collective-permute-start.40 = (f32[2]{0:T(128)S(1)}, f32[2]{0:T(128)S(1)}, u32[]{:S(2)}, u32[]{:S(2)}) collective-permute-start(f32[2]{0:T(128)S(1)} %add.172), channel_id=1, source_target_pairs={{0,16},{4,20},{8,24},{12,28},{16,0},{20,4},{24,8},{28,12},{1,17},{... | collective-permute-start | bytes 32 | tf_op jit(solution)/shard_map/ppermute | solution.py:245

commit v2 on v1

--- a/solution.py
+++ b/solution.py
@@ -9,35 +9,74 @@
 
 
 live_level = 0.25
+near_limit = 36 * 2**20
+far_limit = 32 * 2**20
 
 
 def xor_pairs(count, mask):
     return [(i, i ^ mask) for i in range(count)]
 
 
-def layers_kernel(
-    slots, position_ref, place_ref, block_ref, bias_ref,
-    own_ref, near_ref, far_ref, cross_ref, weights_ref, near_weights_ref, *refs,
+def outcome(parts, tile, bias):
+    result = jnp.dot(jnp.concatenate(parts, axis=1), tile, preferred_element_type=jnp.float32)
+    return jnp.maximum(result + bias, 0.0).astype(jnp.bfloat16)
+
+
+def collapse(value):
+    ones = jnp.ones((8, value.shape[1]), jnp.float32)
+    return lax.dot_general(
+        ones, value, (((1,), (1,)), ((), ())), precision=lax.Precision.HIGHEST, preferred_element_type=jnp.float32
+    )
+
+
+def near_kernel(
+    position_ref, block_ref, bias_ref, own_ref, near_ref, far_ref, cross_ref, weights_ref, near_weights_ref,
+    inputs, first, total_ref, tiles, sems,
 ):
-    piece_refs, refs = refs[: len(slots)], refs[len(slots) :]
-    activations_ref, theirs_ref, sums_ref, second_sums_ref, inputs, first, tiles, second_tiles, outputs, sems = refs
     position = position_ref[0]
     core = lax.rem(position, 2)
-    own_rows = pl.ds(pl.multiple_of(core * near_ref.shape[0], near_ref.shape[0]), near_ref.shape[0])
-    sides = tiles.shape[0]
-    blocks, half, width = first.shape
-    rows = blocks // sides
+    half = near_ref.shape[0]
+    slots, rows, _, width = first.shape
     deep = tiles.shape[1] // rows
-
-    sources = ((0, own_ref.at[own_rows]), (1, near_ref), (2, far_ref), (3, cross_ref))
-    for mask, ref in sources:
+    own_rows = pl.ds(pl.multiple_of(core * half, half), half)
+    for mask, ref in ((0, own_ref.at[own_rows]), (1, near_ref), (2, far_ref), (3, cross_ref)):
         for r in range(rows):
             block = (position ^ mask) * rows + r
             pltpu.make_async_copy(ref.at[:, pl.ds(r * width, width)], inputs.at[block], sems.at[0]).start()
     loads = [
-        pltpu.make_async_copy(ref.at[layer], target.at[mask], sems.at[1 + 2 * layer + mask])
-        for layer, target in ((0, tiles), (1, second_tiles)) for mask, ref in ((0, weights_ref), (1, near_weights_ref))
+        pltpu.make_async_copy(ref.at[0], tiles.at[mask], sems.at[1 + mask])
+        for mask, ref in enumerate((weights_ref, near_weights_ref))
     ]
+    for load in loads:
+        load.start()
+    pltpu.make_async_copy(inputs, inputs, sems.at[0]).wait()
+
+    def layer(mask, total):
+        for slot in range(slots):
+            @pl.when(mask == slot)
+            def _():
+                loads[slot].wait()
+
+        for r in range(rows):
+            row = (position ^ mask) * rows + r
+            parts = [inputs[block_ref[row * 4 + k]] for k in range(4)]
+            first[mask, r] = result = outcome(parts, tiles[mask, r * deep : (r + 1) * deep, :], bias_ref[pl.ds(row, 1), :])
+            total = total + result.astype(jnp.float32)
+        return total
+
+    total_ref[...] = lax.fori_loop(0, slots, layer, jnp.zeros((half, width), jnp.float32))
+
+
+def far_kernel(
+    slots, position_ref, place_ref, block_ref, bias_ref, inputs, near_first, total_ref, weights_ref, near_weights_ref, *refs,
+):
+    piece_refs, refs = refs[: len(slots)], refs[len(slots) :]
+    activations_ref, theirs_ref, sums_ref, second_sums_ref, first, tiles, second_tiles, outputs, sems = refs
+    position = position_ref[0]
+    core = lax.rem(position, 2)
+    blocks, half, width = first.shape
+    rows = near_first.shape[1]
+    deep = tiles.shape[1] // rows
 
     def each_piece(slot, act):
         for i, (ref, own_slot) in enumerate(zip(piece_refs, slots)):
@@ -46,71 +85,67 @@
 
                 @pl.when(place >= 0)
                 def _():
-                    target = tiles.at[slot, pl.ds(pl.multiple_of(place, 16), ref.shape[0])]
-                    act(pltpu.make_async_copy(ref, target, sems.at[7 + i]))
-
-    for load in loads[:2]:
-        load.start()
+                    target = tiles.at[slot - 2, pl.ds(pl.multiple_of(place, 16), ref.shape[0])]
+                    act(pltpu.make_async_copy(ref, target, sems.at[6 + i]))
+
+    loads = [
+        pltpu.make_async_copy(ref.at[1], second_tiles.at[mask], sems.at[mask])
+        for mask, ref in enumerate((weights_ref, near_weights_ref))
+    ]
+    moves = [
+        pltpu.make_async_copy(
+            near_first.at[mask], first.at[pl.ds(pl.multiple_of((position ^ mask) * rows, rows), rows)], sems.at[2 + mask]
+        )
+        for mask in range(2)
+    ]
     for slot in (2, 3):
         each_piece(slot, lambda copy: copy.start())
-    for load in loads[2:]:
-        load.start()
-    pltpu.make_async_copy(inputs, inputs, sems.at[0]).wait()
-
-    def outcome(parts, tile, row):
-        result = jnp.dot(jnp.concatenate(parts, axis=1), tile, preferred_element_type=jnp.float32)
-        return jnp.maximum(result + bias_ref[pl.ds(row, 1), :], 0.0).astype(jnp.bfloat16)
-
-    def first_layer(mask, total):
-        for slot in range(sides):
-            @pl.when(mask == slot)
+    for copy in loads + moves:
+        copy.start()
+
+    def first_layer(step, total):
+        for slot in (2, 3):
+            @pl.when(step == slot - 2)
             def _():
-                if slot < 2:
-                    loads[slot].wait()
-                else:
-                    each_piece(slot, lambda copy: copy.wait())
+                each_piece(slot, lambda copy: copy.wait())
 
         for r in range(rows):
-            row = (position ^ mask) * rows + r
+            row = (position ^ (step + 2)) * rows + r
             parts = [inputs[block_ref[row * 4 + k]] for k in range(4)]
-            first[row] = result = outcome(parts, tiles[mask, r * deep : (r + 1) * deep, :], row)
+            first[row] = result = outcome(parts, tiles[step, r * deep : (r + 1) * deep, :], bias_ref[pl.ds(row, 1), :])
             total = total + result.astype(jnp.float32)
         return total
+
+    sums_ref[...] = collapse(lax.fori_loop(0, 2, first_layer, total_ref[...]))
+    for move in moves:
+        move.wait()
 
     def second_layer(step, total):
         mask = 1 - step
         for slot in range(2):
             @pl.when(mask == slot)
             def _():
-                loads[2 + slot].wait()
+                loads[slot].wait()
 
         for r in range(rows):
             row = (position ^ mask) * rows + r + blocks
             parts = [first[block_ref[row * 4 + k]] for k in range(4)]
-            result = outcome(parts, second_tiles[mask, r * deep : (r + 1) * deep, :], row)
+            result = outcome(parts, second_tiles[mask, r * deep : (r + 1) * deep, :], bias_ref[pl.ds(row, 1), :])
             outputs[mask, :, r * width : (r + 1) * width] = result
             total = total + result.astype(jnp.float32)
 
         @pl.when(mask == 1)
         def _():
-            pltpu.make_async_copy(outputs.at[1], theirs_ref, sems.at[5]).start()
+            pltpu.make_async_copy(outputs.at[1], theirs_ref, sems.at[4]).start()
 
         return total
 
-    ones = jnp.ones((8, width), jnp.float32)
-
-    def collapse(value):
-        return lax.dot_general(
-            ones, value, (((1,), (1,)), ((), ())), precision=lax.Precision.HIGHEST, preferred_element_type=jnp.float32
-        )
-
-    zero = jnp.zeros((half, width), jnp.float32)
-    sums_ref[...] = collapse(lax.fori_loop(0, sides, first_layer, zero))
-    second_total = lax.fori_loop(0, 2, second_layer, zero)
-    mine = pltpu.make_async_copy(outputs.at[0], activations_ref.at[own_rows], sems.at[6])
+    second_total = lax.fori_loop(0, 2, second_layer, jnp.zeros((half, width), jnp.float32))
+    own_rows = pl.ds(pl.multiple_of(core * half, half), half)
+    mine = pltpu.make_async_copy(outputs.at[0], activations_ref.at[own_rows], sems.at[5])
     mine.start()
     second_sums_ref[...] = collapse(second_total)
-    pltpu.make_async_copy(outputs.at[1], theirs_ref, sems.at[5]).wait()
+    pltpu.make_async_copy(outputs.at[1], theirs_ref, sems.at[4]).wait()
     mine.wait()
 
 
@@ -200,34 +235,47 @@
     far = nrn(kept, perm=xor_pairs(sides, 2))
     cross = nrn(given, perm=xor_pairs(sides, 3))
     tables = position.reshape(1), places, block_index.reshape(-1), bias.reshape(layers * sides * rows, width)
-    given, tables = lax.optimization_barrier((given, tables))
+    given, (place, places, blocks, biases) = lax.optimization_barrier((given, tables))
     near = nrn(given, perm=xor_pairs(sides, 1))
     near_weights = nrn(weights, perm=xor_pairs(sides, 1))
 
     any_space = pl.BlockSpec(memory_space=pl.ANY)
     smem = pl.BlockSpec(memory_space=pltpu.SMEM)
     vmem = pl.BlockSpec(memory_space=pltpu.VMEM)
+    flops = 2 * half * rows * deep * width
+    inputs, near_first, total = pl.pallas_call(
+        near_kernel,
+        out_shape=(
+            jax.ShapeDtypeStruct((sides * rows, half, width), jnp.bfloat16),
+            jax.ShapeDtypeStruct((2, rows, half, width), jnp.bfloat16),
+            jax.ShapeDtypeStruct((half, width), jnp.float32),
+        ),
+        in_specs=[smem] * 2 + [vmem] + [any_space] * 6,
+        out_specs=(vmem,) * 3,
+        scratch_shapes=[pltpu.VMEM((2, rows * deep, width), jnp.bfloat16), pltpu.SemaphoreType.DMA((3,))],
+        compiler_params=pltpu.CompilerParams(vmem_limit_bytes=near_limit),
+        cost_estimate=pl.CostEstimate(flops=2 * flops, bytes_accessed=2**24, transcendentals=0),
+    )(place, blocks, biases, images, near, far, cross, weights, near_weights)
     activations, theirs, first_sums, second_sums = pl.pallas_call(
-        functools.partial(layers_kernel, slots),
+        functools.partial(far_kernel, slots),
         out_shape=(
             jax.ShapeDtypeStruct((count, shard), jnp.bfloat16),
             jax.ShapeDtypeStruct((half, shard), jnp.bfloat16),
             jax.ShapeDtypeStruct((8, half), jnp.float32),
             jax.ShapeDtypeStruct((8, half), jnp.float32),
         ),
-        in_specs=[smem] * 3 + [vmem] + [any_space] * (6 + len(pieces)),
+        in_specs=[smem] * 3 + [vmem] * 4 + [any_space] * (2 + len(pieces)),
         out_specs=(any_space, any_space, vmem, vmem),
         scratch_shapes=[
             pltpu.VMEM((sides * rows, half, width), jnp.bfloat16),
-            pltpu.VMEM((sides * rows, half, width), jnp.bfloat16),
-            pltpu.VMEM((sides, rows * deep, width), jnp.bfloat16),
+            pltpu.VMEM((2, rows * deep, width), jnp.bfloat16),
             pltpu.VMEM((2, rows * deep, width), jnp.bfloat16),
             pltpu.VMEM((2, half, shard), jnp.bfloat16),
-            pltpu.SemaphoreType.DMA((7 + len(pieces),)),
+            pltpu.SemaphoreType.DMA((6 + len(pieces),)),
         ],
-        compiler_params=pltpu.CompilerParams(vmem_limit_bytes=36 * 2**20),
-        cost_estimate=pl.CostEstimate(flops=12 * half * rows * deep * width, bytes_accessed=2**25, transcendentals=0),
-    )(*tables, images, near, far, cross, weights, near_weights, *pieces)
+        compiler_params=pltpu.CompilerParams(vmem_limit_bytes=far_limit),
+        cost_estimate=pl.CostEstimate(flops=4 * flops, bytes_accessed=2**24, transcendentals=0),
+    )(place, places, blocks, biases, inputs, near_first, total, weights, near_weights, *pieces)
 
     back = nrn(theirs, perm=xor_pairs(sides, 1))
     activations = lax.dynamic_update_slice(activations, back, ((1 - core) * half, 0))

time: 160 us -> 159 us (level)
  waiting for transfers between devices: 73.1 us -> 66.3 us
  starting transfers between devices: 67 us -> 68.9 us
  local copies, waits for them, and re-layouts: 4.35 us -> 6.16 us
  Pallas kernels: 13.5 us -> 15.3 us
    ppermute x6, starting transfers between devices: 30.1 us -> 21.8 us  [gather_far(): keep(nrn(held[h], perm=xor_pairs(sides, 1)), 3 - h, s, False, True)]
    ppermute x6, starting transfers between devices: 9.4 us -> 16.2 us  [gather_far(): keep(nrn(other, perm=xor_pairs(sides, 1)), 3 - h, s, True, True)]
    ppermute x2, waiting for transfers between devices: 10.4 us -> 6.43 us  [gather_far(): parts.append(nrn(part, perm=xor_pairs(sides, 2)))]
    ppermute x3, starting transfers between devices: 1.47 us -> 5.09 us  [per_device(): live = live + lax.ppermute(live, 'img', xor_pairs(groups, mask))]
    ppermute x1, waiting for transfers between devices: 16.2 us -> 19.2 us  [per_device(): far = nrn(kept, perm=xor_pairs(sides, 2))]
    ppermute x3, waiting for transfers between devices: 10.1 us -> 7.22 us  [per_device(): live = live + lax.ppermute(live, 'img', xor_pairs(groups, mask))]
    ppermute x6, waiting for transfers between devices: 7.1 us -> 4.85 us  [gather_far(): held[h] = both(held[h], perm=pairs(s - 1, onward))]
    ppermute x2, waiting for transfers between devices: 0.24 us -> 2.18 us  [gather_far(): other = both(part, perm=pairs(0, beside))]
  transfers between devices with their start and end apart: 41 -> 41, of which waited for: 15 -> 14; matrix products, arithmetic and copies ran while one was open for 2% -> 4% of each run, Pallas kernels for 0% -> 4%
where the time goes in v2:
time: 159 us; the launch traced here: 158 us
  starting transfers between devices  68.9 us (43%)
  waiting for transfers between devices  66.3 us (42%)
  Pallas kernels  15.3 us (10%)
  local copies, waits for them, and re-layouts  6.16 us (4%)
    ppermute x6, starting transfers between devices, gather_far(): keep(nrn(held[h], perm=xor_pairs(sides, 1)), 3 - h, s, False, True)  21.8 us
    ppermute x1, waiting for transfers between devices, per_device(): cross = nrn(given, perm=xor_pairs(sides, 3))  20.9 us
    ppermute x1, waiting for transfers between devices, per_device(): far = nrn(kept, perm=xor_pairs(sides, 2))  19.2 us
    ppermute x6, starting transfers between devices, gather_far(): keep(nrn(other, perm=xor_pairs(sides, 1)), 3 - h, s, True, True)  16.2 us
    ppermute x6, starting transfers between devices, gather_far(): held[h] = both(held[h], perm=pairs(s - 1, onward))  9.72 us
    pallas_call x1, Pallas kernels, per_device(): pl.pallas_call(functools.partial(far_kernel, slots), out_shape=(jax.Shape...  8.83 us
    ppermute x3, waiting for transfers between devices, per_device(): live = live + lax.ppermute(live, 'img', xor_pairs(groups, mask))  7.22 us
    pallas_call x1, Pallas kernels, per_device(): pl.pallas_call(near_kernel, out_shape=(jax.ShapeDtypeStruct((sides * rows...  6.5 us
  transfers between devices with their start and end apart: 41, of which 14 were waited for; matrix products, arithmetic and copies ran while one was open for 4% of the time, Pallas kernels for 4%

profile of v2, /device:TPU:0, one launch (start us, length us, event | category | flops | bytes accessed | tf_op | source)
XLA Modules:
  0.0 158.4 jit_solution(18132080431261841977)
XLA Ops:
  1.2 1.1 dynamic-slice_bitcast_fusion
  2.3 2.6 %collective-permute-start.7 = (bf16[1024,128]{1,0:T(8,128)(2,1)S(1)}, bf16[1024,128]{1,0:T(8,128)(2,1)S(1)}, u32[]{:S(2)}, u32[]{:S(2)}) collective-permute-start(bf16[1024,128]{1,0:T(8,128)(2,1)S(1)} %get-tuple-element.26), channel_id=1, source_target_pairs={{0,2},{1,3},{2,0},{3,1},{4,6},{5,7},{6,4},{7,5},{8,10},{9,11},{10,... | collective-permute-start | bytes 786440 | tf_op jit(solution)/shard_map/ppermute | solution.py:162
  4.9 0.8 copy.6
  5.8 1.0 reshape.18.bias_ref
  7.0 1.9 %constant_dynamic-slice_fusion = (bf16[128,4096]{1,0:T(8,128)(2,1)S(1)}, bf16[128,4096]{1,0:T(8,128)(2,1)S(1)}) fusion(bf16[256,4096]{1,0:T(8,128)(2,1)} %own_ref.1, s32[]{:T(128)S(6)} %select_n.152, s32[]{:T(128)S(6)} %select_n.128), kind=kLoop, calls=%fused_computation.5 | loop fusion | bytes 4194312 | tf_op jit(solution)/shard_map/dynamic_slice | solution.py:233
  8.9 3.1 %collective-permute-done.7 = bf16[1024,128]{1,0:T(8,128)(2,1)S(1)} collective-permute-done((bf16[1024,128]{1,0:T(8,128)(2,1)S(1)}, bf16[1024,128]{1,0:T(8,128)(2,1)S(1)}, u32[]{:S(2)}, u32[]{:S(2)}) %collective-permute-start.7) | collective-permute-done | bytes 262176 | tf_op jit(solution)/shard_map/ppermute | solution.py:162
  12.0 2.0 %collective-permute-start.8 = (bf16[1024,128]{1,0:T(8,128)(2,1)S(1)}, bf16[1024,128]{1,0:T(8,128)(2,1)S(1)}, u32[]{:S(2)}, u32[]{:S(2)}) collective-permute-start(bf16[1024,128]{1,0:T(8,128)(2,1)S(1)} %collective-permute-done.7), channel_id=1, source_target_pairs={{0,4},{1,5},{2,6},{3,7},{4,0},{5,1},{6,2},{7,3},{8,12},{9,13},{10,... | collective-permute-start | bytes 786440 | tf_op jit(solution)/shard_map/ppermute | solution.py:199
  14.0 3.4 %collective-permute-done.4 = bf16[1024,128]{1,0:T(8,128)(2,1)S(1)} collective-permute-done((bf16[1024,128]{1,0:T(8,128)(2,1)S(1)}, bf16[1024,128]{1,0:T(8,128)(2,1)S(1)}, u32[]{:S(2)}, u32[]{:S(2)}) %collective-permute-start.4) | collective-permute-done | bytes 262176 | tf_op jit(solution)/shard_map/ppermute | solution.py:162
  17.4 1.8 %collective-permute-start.5 = (bf16[1024,128]{1,0:T(8,128)(2,1)S(1)}, bf16[1024,128]{1,0:T(8,128)(2,1)S(1)}, u32[]{:S(2)}, u32[]{:S(2)}) collective-permute-start(bf16[1024,128]{1,0:T(8,128)(2,1)S(1)} %collective-permute-done.4), channel_id=1, source_target_pairs={{0,4},{1,5},{2,6},{3,7},{4,0},{5,1},{6,2},{7,3},{8,12},{9,13},{10,... | collective-permute-start | bytes 786440 | tf_op jit(solution)/shard_map/ppermute | solution.py:199
  19.2 3.5 %collective-permute-start.11 = (bf16[2048,128]{1,0:T(8,128)(2,1)S(1)}, bf16[2048,128]{1,0:T(8,128)(2,1)S(1)}, u32[]{:S(2)}, u32[]{:S(2)}) collective-permute-start(bf16[2048,128]{1,0:T(8,128)(2,1)S(1)} %constant_dynamic-update-slice_fusion.refs_4_), channel_id=1, source_target_pairs={{0,8},{2,10},{4,12},{6,14},{8,16},{9,1},{10,18},{11,3},{12,20},{13... | collective-permute-start | bytes 1572872 | tf_op jit(solution)/shard_map/ppermute | solution.py:208
  23.3 2.2 %collective-permute-done.5.refs_0_ = bf16[1024,128]{1,0:T(8,128)(2,1)S(1)} collective-permute-done((bf16[1024,128]{1,0:T(8,128)(2,1)S(1)}, bf16[1024,128]{1,0:T(8,128)(2,1)S(1)}, u32[]{:S(2)}, u32[]{:S(2)}) %collective-permute-start.5) | collective-permute-done | bytes 262176 | tf_op jit(solution)/shard_map/ppermute | solution.py:199
  25.8 1.5 collective-permute-start.1
  27.3 0.9 collective-permute-start.2
  28.2 1.2 collective-permute-done.11.refs_6_
  29.4 1.9 %collective-permute-done.10.refs_5_ = bf16[2048,128]{1,0:T(8,128)(2,1)S(1)} collective-permute-done((bf16[2048,128]{1,0:T(8,128)(2,1)S(1)}, bf16[2048,128]{1,0:T(8,128)(2,1)S(1)}, u32[]{:S(2)}, u32[]{:S(2)}) %collective-permute-start.10) | collective-permute-done | bytes 524320 | tf_op jit(solution)/shard_map/ppermute | solution.py:203
  31.3 0.7 collective-permute-start.19
  32.0 0.7 collective-permute-start.13
  32.7 19.2 %collective-permute-done.1.far_ref = bf16[128,4096]{1,0:T(8,128)(2,1)S(1)} collective-permute-done((bf16[128,4096]{1,0:T(8,128)(2,1)S(1)}, bf16[128,4096]{1,0:T(8,128)(2,1)S(1)}, u32[]{:S(2)}, u32[]{:S(2)}) %collective-permute-start.1) | collective-permute-done | bytes 1048608 | tf_op jit(solution)/shard_map/ppermute | solution.py:235
  51.9 20.9 %collective-permute-done.2.cross_ref = bf16[128,4096]{1,0:T(8,128)(2,1)S(1)} collective-permute-done((bf16[128,4096]{1,0:T(8,128)(2,1)S(1)}, bf16[128,4096]{1,0:T(8,128)(2,1)S(1)}, u32[]{:S(2)}, u32[]{:S(2)}) %collective-permute-start.2) | collective-permute-done | bytes 1048608 | tf_op jit(solution)/shard_map/ppermute | solution.py:236
  72.8 3.5 %collective-permute-start.15 = (bf16[2048,128]{1,0:T(8,128)(2,1)S(1)}, bf16[2048,128]{1,0:T(8,128)(2,1)S(1)}, u32[]{:S(2)}, u32[]{:S(2)}) collective-permute-start(bf16[2048,128]{1,0:T(8,128)(2,1)S(1)} %collective-permute-done.10.refs_5_), channel_id=1, source_target_pairs={{0,8},{2,10},{4,12},{6,14},{8,16},{9,1},{10,18},{11,3},{12,20},{13... | collective-permute-start | bytes 1572872 | tf_op jit(solution)/shard_map/ppermute | solution.py:208
  76.2 0.7 collective-permute-start.27
  77.0 0.7 collective-permute-start.21
  77.7 1.5 collective-permute-start.20
  79.2 3.7 %collective-permute-done.15.refs_10_ = bf16[2048,128]{1,0:T(8,128)(2,1)S(1)} collective-permute-done((bf16[2048,128]{1,0:T(8,128)(2,1)S(1)}, bf16[2048,128]{1,0:T(8,128)(2,1)S(1)}, u32[]{:S(2)}, u32[]{:S(2)}) %collective-permute-start.15) | collective-permute-done | bytes 524320 | tf_op jit(solution)/shard_map/ppermute | solution.py:208
  83.3 0.7 collective-permute-start.23
  84.0 0.7 collective-permute-start.17
  84.7 8.7 %collective-permute-start.16 = (bf16[2048,128]{1,0:T(8,128)(2,1)S(1)}, bf16[2048,128]{1,0:T(8,128)(2,1)S(1)}, u32[]{:S(2)}, u32[]{:S(2)}) collective-permute-start(bf16[2048,128]{1,0:T(8,128)(2,1)S(1)} %collective-permute-done.15.refs_10_), channel_id=1, source_target_pairs={{0,1},{1,0},{2,3},{3,2},{4,5},{5,4},{6,7},{7,6},{8,9},{9,8},{10,11... | collective-permute-start | bytes 1572872 | tf_op jit(solution)/shard_map/ppermute | solution.py:210
  93.4 0.7 collective-permute-start.29
  94.1 4.7 %collective-permute-start.28 = (bf16[2048,128]{1,0:T(8,128)(2,1)S(1)}, bf16[2048,128]{1,0:T(8,128)(2,1)S(1)}, u32[]{:S(2)}, u32[]{:S(2)}) collective-permute-start(bf16[2048,128]{1,0:T(8,128)(2,1)S(1)} %collective-permute-done.27.refs_22_), channel_id=1, source_target_pairs={{0,1},{1,0},{2,3},{3,2},{4,5},{5,4},{6,7},{7,6},{8,9},{9,8},{10,11... | collective-permute-start | bytes 1572872 | tf_op jit(solution)/shard_map/ppermute | solution.py:210
  98.8 0.7 collective-permute-start.31
  99.5 2.0 %collective-permute-start.22 = (bf16[2048,128]{1,0:T(8,128)(2,1)S(1)}, bf16[2048,128]{1,0:T(8,128)(2,1)S(1)}, u32[]{:S(2)}, u32[]{:S(2)}) collective-permute-start(bf16[2048,128]{1,0:T(8,128)(2,1)S(1)} %collective-permute-done.21.refs_16_), channel_id=1, source_target_pairs={{0,1},{1,0},{2,3},{3,2},{4,5},{5,4},{6,7},{7,6},{8,9},{9,8},{10,11... | collective-permute-start | bytes 1572872 | tf_op jit(solution)/shard_map/ppermute | solution.py:213
  101.5 0.7 collective-permute-start.25
  102.2 6.7 %collective-permute-start.24 = (bf16[2048,128]{1,0:T(8,128)(2,1)S(1)}, bf16[2048,128]{1,0:T(8,128)(2,1)S(1)}, u32[]{:S(2)}, u32[]{:S(2)}) collective-permute-start(bf16[2048,128]{1,0:T(8,128)(2,1)S(1)} %collective-permute-done.23.refs_18_), channel_id=1, source_target_pairs={{0,1},{1,0},{2,3},{3,2},{4,5},{5,4},{6,7},{7,6},{8,9},{9,8},{10,11... | collective-permute-start | bytes 1572872 | tf_op jit(solution)/shard_map/ppermute | solution.py:210
  108.9 0.7 collective-permute-start.33
  109.6 7.1 %collective-permute-start.18 = (bf16[2048,128]{1,0:T(8,128)(2,1)S(1)}, bf16[2048,128]{1,0:T(8,128)(2,1)S(1)}, u32[]{:S(2)}, u32[]{:S(2)}) collective-permute-start(bf16[2048,128]{1,0:T(8,128)(2,1)S(1)} %collective-permute-done.17.refs_12_), channel_id=1, source_target_pairs={{0,1},{1,0},{2,3},{3,2},{4,5},{5,4},{6,7},{7,6},{8,9},{9,8},{10,11... | collective-permute-start | bytes 1572872 | tf_op jit(solution)/shard_map/ppermute | solution.py:213
  117.3 6.2 %collective-permute-start.26 = (bf16[2048,128]{1,0:T(8,128)(2,1)S(1)}, bf16[2048,128]{1,0:T(8,128)(2,1)S(1)}, u32[]{:S(2)}, u32[]{:S(2)}) collective-permute-start(bf16[2048,128]{1,0:T(8,128)(2,1)S(1)} %collective-permute-done.25.refs_20_), channel_id=1, source_target_pairs={{0,1},{1,0},{2,3},{3,2},{4,5},{5,4},{6,7},{7,6},{8,9},{9,8},{10,11... | collective-permute-start | bytes 1572872 | tf_op jit(solution)/shard_map/ppermute | solution.py:213
  123.6 6.5 %shard_map.59 = (bf16[128,128,128]{2,1,0:T(8,128)(2,1)S(1)}, bf16[2,32,128,128]{3,2,1,0:T(8,128)(2,1)S(1)}, f32[128,128]{1,0:T(8,128)S(1)}) custom-call(s32[1]{0:T(128)} %bitcast.position_ref, s32[1024]{0:T(1024)S(1)} %reshape.17.block_ref, f32[256,128]{1,0:T(8,128)S(1)} %reshape.18.bias_ref, bf16[256,4096]{1,0:T(8,128)(2,1)S(1)} %copy-done, ...), custom_call_target="tpu_custom_call" | custom-call | flops 1073741824 | bytes 16777216 | tf_op jit(solution)/shard_map/pallas_call | solution.py:246
  130.1 8.8 %shard_map.60 = (bf16[256,4096]{1,0:T(8,128)(2,1)}, bf16[128,4096]{1,0:T(8,128)(2,1)S(1)}, f32[8,128]{1,0:T(8,128)S(1)}, f32[8,128]{1,0:T(8,128)S(1)}) custom-call(s32[1]{0:T(128)} %bitcast.position_ref, s32[30]{0:T(128)S(1)} %stack.81.place_ref, s32[1024]{0:T(1024)S(1)} %reshape.17.block_ref, f32[256,128]{1,0:T(8,128)S(1)} %reshape.18.bias_ref, ...), custom_call_target="tpu_custom_call" | custom-call | flops 2147483648 | bytes 16777216 | tf_op jit(solution)/shard_map/pallas_call | solution.py:259
  138.9 0.6 collective-permute-start.35
  139.5 1.4 collective-permute-start.36
  141.0 2.2 %collective-permute-done.36 = f32[8,128]{1,0:T(8,128)S(1)} collective-permute-done((f32[8,128]{1,0:T(8,128)S(1)}, f32[8,128]{1,0:T(8,128)S(1)}, u32[]{:S(2)}, u32[]{:S(2)}) %collective-permute-start.36) | collective-permute-done | bytes 4128 | tf_op jit(solution)/shard_map/ppermute | solution.py:283
  143.3 1.1 collective-permute-done.37
  144.5 1.5 collective-permute-start.38
  145.9 2.1 %collective-permute-done.38 = f32[2]{0:T(128)S(1)} collective-permute-done((f32[2]{0:T(128)S(1)}, f32[2]{0:T(128)S(1)}, u32[]{:S(2)}, u32[]{:S(2)}) %collective-permute-start.38) | collective-permute-done | bytes 40 | tf_op jit(solution)/shard_map/ppermute | solution.py:293
  148.1 3.6 %collective-permute-done.39 = f32[2]{0:T(128)S(1)} collective-permute-done((f32[2]{0:T(128)S(1)}, f32[2]{0:T(128)S(1)}, u32[]{:S(2)}, u32[]{:S(2)}) %collective-permute-start.39) | collective-permute-done | bytes 40 | tf_op jit(solution)/shard_map/ppermute | solution.py:293
  151.6 3.6 %collective-permute-start.40 = (f32[2]{0:T(128)S(1)}, f32[2]{0:T(128)S(1)}, u32[]{:S(2)}, u32[]{:S(2)}) collective-permute-start(f32[2]{0:T(128)S(1)} %add.172), channel_id=1, source_target_pairs={{0,16},{4,20},{8,24},{12,28},{16,0},{20,4},{24,8},{28,12},{1,17},{... | collective-permute-start | bytes 32 | tf_op jit(solution)/shard_map/ppermute | solution.py:293
  155.3 1.5 collective-permute-done.40
  157.3 1.1 constant_dynamic-update-slice_fusion.2
  (55 shorter events, 3.6 us)
Async XLA Ops:
  0.6 122.9 %collective-permute-start.3 = (bf16[2,16384,128]{2,1,0:T(8,128)(2,1)}, bf16[2,16384,128]{2,1,0:T(8,128)(2,1)}, u32[]{:S(2)}, u32[]{:S(2)}) collective-permute-start(bf16[2,16384,128]{2,1,0:T(8,128)(2,1)} %bitcast.21), channel_id=1, source_target_pairs={{0,1},{1,0},{2,3},{3,2},{4,5},{5,4},{6,7},{7,6},{8,9},{9,8},{10,11... | collective-permute-start | bytes 25165832 | tf_op jit(solution)/shard_map/ppermute | solution.py:240
  2.3 9.7 %collective-permute-start.7 = (bf16[1024,128]{1,0:T(8,128)(2,1)S(1)}, bf16[1024,128]{1,0:T(8,128)(2,1)S(1)}, u32[]{:S(2)}, u32[]{:S(2)}) collective-permute-start(bf16[1024,128]{1,0:T(8,128)(2,1)S(1)} %get-tuple-element.26), channel_id=1, source_target_pairs={{0,2},{1,3},{2,0},{3,1},{4,6},{5,7},{6,4},{7,5},{8,10},{9,11},{10,... | collective-permute-start | bytes 786440 | tf_op jit(solution)/shard_map/ppermute | solution.py:162
  4.8 12.6 %collective-permute-start.4 = (bf16[1024,128]{1,0:T(8,128)(2,1)S(1)}, bf16[1024,128]{1,0:T(8,128)(2,1)S(1)}, u32[]{:S(2)}, u32[]{:S(2)}) collective-permute-start(bf16[1024,128]{1,0:T(8,128)(2,1)S(1)} %get-tuple-element.27), channel_id=1, source_target_pairs={{0,2},{1,3},{2,0},{3,1},{4,6},{5,7},{6,4},{7,5},{8,10},{9,11},{10,... | collective-permute-start | bytes 786440 | tf_op jit(solution)/shard_map/ppermute | solution.py:162
  7.0 116.6 %copy-start = (bf16[256,4096]{1,0:T(8,128)(2,1)S(1)}, bf16[256,4096]{1,0:T(8,128)(2,1)}, u32[]{:S(2)}) copy-start(bf16[256,4096]{1,0:T(8,128)(2,1)} %own_ref.1) | copy-start | bytes 6291460
  12.0 10.8 %collective-permute-start.8 = (bf16[1024,128]{1,0:T(8,128)(2,1)S(1)}, bf16[1024,128]{1,0:T(8,128)(2,1)S(1)}, u32[]{:S(2)}, u32[]{:S(2)}) collective-permute-start(bf16[1024,128]{1,0:T(8,128)(2,1)S(1)} %collective-permute-done.7), channel_id=1, source_target_pairs={{0,4},{1,5},{2,6},{3,7},{4,0},{5,1},{6,2},{7,3},{8,12},{9,13},{10,... | collective-permute-start | bytes 786440 | tf_op jit(solution)/shard_map/ppermute | solution.py:199
  17.4 8.1 %collective-permute-start.5 = (bf16[1024,128]{1,0:T(8,128)(2,1)S(1)}, bf16[1024,128]{1,0:T(8,128)(2,1)S(1)}, u32[]{:S(2)}, u32[]{:S(2)}) collective-permute-start(bf16[1024,128]{1,0:T(8,128)(2,1)S(1)} %collective-permute-done.4), channel_id=1, source_target_pairs={{0,4},{1,5},{2,6},{3,7},{4,0},{5,1},{6,2},{7,3},{8,12},{9,13},{10,... | collective-permute-start | bytes 786440 | tf_op jit(solution)/shard_map/ppermute | solution.py:199
  19.2 10.2 %collective-permute-start.11 = (bf16[2048,128]{1,0:T(8,128)(2,1)S(1)}, bf16[2048,128]{1,0:T(8,128)(2,1)S(1)}, u32[]{:S(2)}, u32[]{:S(2)}) collective-permute-start(bf16[2048,128]{1,0:T(8,128)(2,1)S(1)} %constant_dynamic-update-slice_fusion.refs_4_), channel_id=1, source_target_pairs={{0,8},{2,10},{4,12},{6,14},{8,16},{9,1},{10,18},{11,3},{12,20},{13... | collective-permute-start | bytes 1572872 | tf_op jit(solution)/shard_map/ppermute | solution.py:208
  22.7 9.3 %collective-permute-start = (bf16[128,4096]{1,0:T(8,128)(2,1)S(1)}, bf16[128,4096]{1,0:T(8,128)(2,1)S(1)}, u32[]{:S(2)}, u32[]{:S(2)}) collective-permute-start(bf16[128,4096]{1,0:T(8,128)(2,1)S(1)} %get-tuple-element.18), channel_id=1, source_target_pairs={{0,1},{1,0},{2,3},{3,2},{4,5},{5,4},{6,7},{7,6},{8,9},{9,8},{10,11... | collective-permute-start | bytes 3145736 | tf_op jit(solution)/shard_map/ppermute | solution.py:239
  22.8 3.0 %collective-permute-start.9 = (bf16[1024,128]{1,0:T(8,128)(2,1)S(1)}, bf16[1024,128]{1,0:T(8,128)(2,1)S(1)}, u32[]{:S(2)}, u32[]{:S(2)}) collective-permute-start(bf16[1024,128]{1,0:T(8,128)(2,1)S(1)} %collective-permute-done.8.refs_2_), channel_id=1, source_target_pairs={{0,1},{1,0},{2,3},{3,2},{4,5},{5,4},{6,7},{7,6},{8,9},{9,8},{10,11... | collective-permute-start | bytes 786440 | tf_op jit(solution)/shard_map/ppermute | solution.py:201
  25.5 1.8 %collective-permute-start.6 = (bf16[1024,128]{1,0:T(8,128)(2,1)S(1)}, bf16[1024,128]{1,0:T(8,128)(2,1)S(1)}, u32[]{:S(2)}, u32[]{:S(2)}) collective-permute-start(bf16[1024,128]{1,0:T(8,128)(2,1)S(1)} %collective-permute-done.5.refs_0_), channel_id=1, source_target_pairs={{0,1},{1,0},{2,3},{3,2},{4,5},{5,4},{6,7},{7,6},{8,9},{9,8},{10,11... | collective-permute-start | bytes 786440 | tf_op jit(solution)/shard_map/ppermute | solution.py:201
  25.8 26.0 %collective-permute-start.1 = (bf16[128,4096]{1,0:T(8,128)(2,1)S(1)}, bf16[128,4096]{1,0:T(8,128)(2,1)S(1)}, u32[]{:S(2)}, u32[]{:S(2)}) collective-permute-start(bf16[128,4096]{1,0:T(8,128)(2,1)S(1)} %get-tuple-element.28), channel_id=1, source_target_pairs={{0,2},{1,3},{2,0},{3,1},{4,6},{5,7},{6,4},{7,5},{8,10},{9,11},{10,... | collective-permute-start | bytes 3145736 | tf_op jit(solution)/shard_map/ppermute | solution.py:235
  27.3 45.4 %collective-permute-start.2 = (bf16[128,4096]{1,0:T(8,128)(2,1)S(1)}, bf16[128,4096]{1,0:T(8,128)(2,1)S(1)}, u32[]{:S(2)}, u32[]{:S(2)}) collective-permute-start(bf16[128,4096]{1,0:T(8,128)(2,1)S(1)} %get-tuple-element.18), channel_id=1, source_target_pairs={{0,3},{1,2},{2,1},{3,0},{4,7},{5,6},{6,5},{7,4},{8,11},{9,10},{10,... | collective-permute-start | bytes 3145736 | tf_op jit(solution)/shard_map/ppermute | solution.py:236
  29.4 1.9 %collective-permute-start.10 = (bf16[2048,128]{1,0:T(8,128)(2,1)S(1)}, bf16[2048,128]{1,0:T(8,128)(2,1)S(1)}, u32[]{:S(2)}, u32[]{:S(2)}) collective-permute-start(bf16[2048,128]{1,0:T(8,128)(2,1)S(1)} %constant_dynamic-update-slice_fusion.refs_4_), channel_id=1, source_target_pairs={{0,1},{1,0},{2,3},{3,2},{4,5},{5,4},{6,7},{7,6},{8,9},{9,8},{10,11... | collective-permute-start | bytes 1572872 | tf_op jit(solution)/shard_map/ppermute | solution.py:203
  31.3 44.9 %collective-permute-start.19 = (bf16[2048,128]{1,0:T(8,128)(2,1)S(1)}, bf16[2048,128]{1,0:T(8,128)(2,1)S(1)}, u32[]{:S(2)}, u32[]{:S(2)}) collective-permute-start(bf16[2048,128]{1,0:T(8,128)(2,1)S(1)} %collective-permute-done.11.refs_6_), channel_id=1, source_target_pairs={{8,16},{9,1},{10,18},{11,3},{12,20},{13,5},{14,22},{15,7},{16,24},... | collective-permute-start | bytes 1572872 | tf_op jit(solution)/shard_map/ppermute | solution.py:208
  32.0 44.9 %collective-permute-start.13 = (bf16[2048,128]{1,0:T(8,128)(2,1)S(1)}, bf16[2048,128]{1,0:T(8,128)(2,1)S(1)}, u32[]{:S(2)}, u32[]{:S(2)}) collective-permute-start(bf16[2048,128]{1,0:T(8,128)(2,1)S(1)} %collective-permute-done.11.refs_6_), channel_id=1, source_target_pairs={{1,5},{3,7},{5,1},{7,3},{8,12},{9,13},{10,14},{11,15},{12,8},{13,9... | collective-permute-start | bytes 1572872 | tf_op jit(solution)/shard_map/ppermute | solution.py:211
  51.9 25.8 %collective-permute-start.12 = (bf16[2048,128]{1,0:T(8,128)(2,1)S(1)}, bf16[2048,128]{1,0:T(8,128)(2,1)S(1)}, u32[]{:S(2)}, u32[]{:S(2)}) collective-permute-start(bf16[2048,128]{1,0:T(8,128)(2,1)S(1)} %collective-permute-done.11.refs_6_), channel_id=1, source_target_pairs={{0,1},{1,0},{2,3},{3,2},{4,5},{5,4},{6,7},{7,6},{8,9},{9,8},{10,11... | collective-permute-start | bytes 1572872 | tf_op jit(solution)/shard_map/ppermute | solution.py:210
  72.8 10.1 %collective-permute-start.15 = (bf16[2048,128]{1,0:T(8,128)(2,1)S(1)}, bf16[2048,128]{1,0:T(8,128)(2,1)S(1)}, u32[]{:S(2)}, u32[]{:S(2)}) collective-permute-start(bf16[2048,128]{1,0:T(8,128)(2,1)S(1)} %collective-permute-done.10.refs_5_), channel_id=1, source_target_pairs={{0,8},{2,10},{4,12},{6,14},{8,16},{9,1},{10,18},{11,3},{12,20},{13... | collective-permute-start | bytes 1572872 | tf_op jit(solution)/shard_map/ppermute | solution.py:208
  76.2 7.1 %collective-permute-start.27 = (bf16[2048,128]{1,0:T(8,128)(2,1)S(1)}, bf16[2048,128]{1,0:T(8,128)(2,1)S(1)}, u32[]{:S(2)}, u32[]{:S(2)}) collective-permute-start(bf16[2048,128]{1,0:T(8,128)(2,1)S(1)} %collective-permute-done.19.refs_14_), channel_id=1, source_target_pairs={{9,1},{11,3},{13,5},{15,7},{16,24},{18,26},{20,28},{22,30}} | collective-permute-start | bytes 1572872 | tf_op jit(solution)/shard_map/ppermute | solution.py:208
  77.0 7.0 %collective-permute-start.21 = (bf16[2048,128]{1,0:T(8,128)(2,1)S(1)}, bf16[2048,128]{1,0:T(8,128)(2,1)S(1)}, u32[]{:S(2)}, u32[]{:S(2)}) collective-permute-start(bf16[2048,128]{1,0:T(8,128)(2,1)S(1)} %collective-permute-done.19.refs_14_), channel_id=1, source_target_pairs={{1,5},{3,7},{5,1},{7,3},{9,13},{11,15},{13,9},{15,11},{16,20},{18,... | collective-permute-start | bytes 1572872 | tf_op jit(solution)/shard_map/ppermute | solution.py:211
  77.7 7.0 %collective-permute-start.20 = (bf16[2048,128]{1,0:T(8,128)(2,1)S(1)}, bf16[2048,128]{1,0:T(8,128)(2,1)S(1)}, u32[]{:S(2)}, u32[]{:S(2)}) collective-permute-start(bf16[2048,128]{1,0:T(8,128)(2,1)S(1)} %collective-permute-done.19.refs_14_), channel_id=1, source_target_pairs={{0,1},{1,0},{2,3},{3,2},{4,5},{5,4},{6,7},{7,6},{8,9},{9,8},{10,11... | collective-permute-start | bytes 1572872 | tf_op jit(solution)/shard_map/ppermute | solution.py:210
  82.9 10.5 %collective-permute-start.14 = (bf16[2048,128]{1,0:T(8,128)(2,1)S(1)}, bf16[2048,128]{1,0:T(8,128)(2,1)S(1)}, u32[]{:S(2)}, u32[]{:S(2)}) collective-permute-start(bf16[2048,128]{1,0:T(8,128)(2,1)S(1)} %collective-permute-done.13.refs_8_), channel_id=1, source_target_pairs={{0,1},{1,0},{2,3},{3,2},{4,5},{5,4},{6,7},{7,6},{8,9},{9,8},{10,11... | collective-permute-start | bytes 1572872 | tf_op jit(solution)/shard_map/ppermute | solution.py:213
  83.3 10.8 %collective-permute-start.23 = (bf16[2048,128]{1,0:T(8,128)(2,1)S(1)}, bf16[2048,128]{1,0:T(8,128)(2,1)S(1)}, u32[]{:S(2)}, u32[]{:S(2)}) collective-permute-start(bf16[2048,128]{1,0:T(8,128)(2,1)S(1)} %collective-permute-done.15.refs_10_), channel_id=1, source_target_pairs={{8,16},{9,1},{10,18},{11,3},{12,20},{13,5},{14,22},{15,7},{16,24},... | collective-permute-start | bytes 1572872 | tf_op jit(solution)/shard_map/ppermute | solution.py:208
  84.0 14.8 %collective-permute-start.17 = (bf16[2048,128]{1,0:T(8,128)(2,1)S(1)}, bf16[2048,128]{1,0:T(8,128)(2,1)S(1)}, u32[]{:S(2)}, u32[]{:S(2)}) collective-permute-start(bf16[2048,128]{1,0:T(8,128)(2,1)S(1)} %collective-permute-done.15.refs_10_), channel_id=1, source_target_pairs={{1,5},{3,7},{5,1},{7,3},{8,12},{9,13},{10,14},{11,15},{12,8},{13,9... | collective-permute-start | bytes 1572872 | tf_op jit(solution)/shard_map/ppermute | solution.py:211
  84.7 14.8 %collective-permute-start.16 = (bf16[2048,128]{1,0:T(8,128)(2,1)S(1)}, bf16[2048,128]{1,0:T(8,128)(2,1)S(1)}, u32[]{:S(2)}, u32[]{:S(2)}) collective-permute-start(bf16[2048,128]{1,0:T(8,128)(2,1)S(1)} %collective-permute-done.15.refs_10_), channel_id=1, source_target_pairs={{0,1},{1,0},{2,3},{3,2},{4,5},{5,4},{6,7},{7,6},{8,9},{9,8},{10,11... | collective-permute-start | bytes 1572872 | tf_op jit(solution)/shard_map/ppermute | solution.py:210
  93.4 8.1 %collective-permute-start.29 = (bf16[2048,128]{1,0:T(8,128)(2,1)S(1)}, bf16[2048,128]{1,0:T(8,128)(2,1)S(1)}, u32[]{:S(2)}, u32[]{:S(2)}) collective-permute-start(bf16[2048,128]{1,0:T(8,128)(2,1)S(1)} %collective-permute-done.27.refs_22_), channel_id=1, source_target_pairs={{1,5},{3,7},{5,1},{7,3},{24,28},{26,30},{28,24},{30,26}} | collective-permute-start | bytes 1572872 | tf_op jit(solution)/shard_map/ppermute | solution.py:211
  94.1 8.1 %collective-permute-start.28 = (bf16[2048,128]{1,0:T(8,128)(2,1)S(1)}, bf16[2048,128]{1,0:T(8,128)(2,1)S(1)}, u32[]{:S(2)}, u32[]{:S(2)}) collective-permute-start(bf16[2048,128]{1,0:T(8,128)(2,1)S(1)} %collective-permute-done.27.refs_22_), channel_id=1, source_target_pairs={{0,1},{1,0},{2,3},{3,2},{4,5},{5,4},{6,7},{7,6},{8,9},{9,8},{10,11... | collective-permute-start | bytes 1572872 | tf_op jit(solution)/shard_map/ppermute | solution.py:210
  98.8 10.1 %collective-permute-start.31 = (bf16[2048,128]{1,0:T(8,128)(2,1)S(1)}, bf16[2048,128]{1,0:T(8,128)(2,1)S(1)}, u32[]{:S(2)}, u32[]{:S(2)}) collective-permute-start(bf16[2048,128]{1,0:T(8,128)(2,1)S(1)} %collective-permute-done.23.refs_18_), channel_id=1, source_target_pairs={{9,1},{11,3},{13,5},{15,7},{16,24},{18,26},{20,28},{22,30}} | collective-permute-start | bytes 1572872 | tf_op jit(solution)/shard_map/ppermute | solution.py:208
  99.5 10.1 %collective-permute-start.22 = (bf16[2048,128]{1,0:T(8,128)(2,1)S(1)}, bf16[2048,128]{1,0:T(8,128)(2,1)S(1)}, u32[]{:S(2)}, u32[]{:S(2)}) collective-permute-start(bf16[2048,128]{1,0:T(8,128)(2,1)S(1)} %collective-permute-done.21.refs_16_), channel_id=1, source_target_pairs={{0,1},{1,0},{2,3},{3,2},{4,5},{5,4},{6,7},{7,6},{8,9},{9,8},{10,11... | collective-permute-start | bytes 1572872 | tf_op jit(solution)/shard_map/ppermute | solution.py:213
  101.5 15.3 %collective-permute-start.25 = (bf16[2048,128]{1,0:T(8,128)(2,1)S(1)}, bf16[2048,128]{1,0:T(8,128)(2,1)S(1)}, u32[]{:S(2)}, u32[]{:S(2)}) collective-permute-start(bf16[2048,128]{1,0:T(8,128)(2,1)S(1)} %collective-permute-done.23.refs_18_), channel_id=1, source_target_pairs={{1,5},{3,7},{5,1},{7,3},{9,13},{11,15},{13,9},{15,11},{16,20},{18,... | collective-permute-start | bytes 1572872 | tf_op jit(solution)/shard_map/ppermute | solution.py:211
  102.2 14.7 %collective-permute-start.24 = (bf16[2048,128]{1,0:T(8,128)(2,1)S(1)}, bf16[2048,128]{1,0:T(8,128)(2,1)S(1)}, u32[]{:S(2)}, u32[]{:S(2)}) collective-permute-start(bf16[2048,128]{1,0:T(8,128)(2,1)S(1)} %collective-permute-done.23.refs_18_), channel_id=1, source_target_pairs={{0,1},{1,0},{2,3},{3,2},{4,5},{5,4},{6,7},{7,6},{8,9},{9,8},{10,11... | collective-permute-start | bytes 1572872 | tf_op jit(solution)/shard_map/ppermute | solution.py:210
  108.9 8.4 %collective-permute-start.33 = (bf16[2048,128]{1,0:T(8,128)(2,1)S(1)}, bf16[2048,128]{1,0:T(8,128)(2,1)S(1)}, u32[]{:S(2)}, u32[]{:S(2)}) collective-permute-start(bf16[2048,128]{1,0:T(8,128)(2,1)S(1)} %collective-permute-done.31.refs_26_), channel_id=1, source_target_pairs={{1,5},{3,7},{5,1},{7,3},{24,28},{26,30},{28,24},{30,26}} | collective-permute-start | bytes 1572872 | tf_op jit(solution)/shard_map/ppermute | solution.py:211
  109.6 20.4 %collective-permute-start.18 = (bf16[2048,128]{1,0:T(8,128)(2,1)S(1)}, bf16[2048,128]{1,0:T(8,128)(2,1)S(1)}, u32[]{:S(2)}, u32[]{:S(2)}) collective-permute-start(bf16[2048,128]{1,0:T(8,128)(2,1)S(1)} %collective-permute-done.17.refs_12_), channel_id=1, source_target_pairs={{0,1},{1,0},{2,3},{3,2},{4,5},{5,4},{6,7},{7,6},{8,9},{9,8},{10,11... | collective-permute-start | bytes 1572872 | tf_op jit(solution)/shard_map/ppermute | solution.py:213
  116.8 13.3 %collective-permute-start.32 = (bf16[2048,128]{1,0:T(8,128)(2,1)S(1)}, bf16[2048,128]{1,0:T(8,128)(2,1)S(1)}, u32[]{:S(2)}, u32[]{:S(2)}) collective-permute-start(bf16[2048,128]{1,0:T(8,128)(2,1)S(1)} %collective-permute-done.31.refs_26_), channel_id=1, source_target_pairs={{0,1},{1,0},{2,3},{3,2},{4,5},{5,4},{6,7},{7,6},{8,9},{9,8},{10,11... | collective-permute-start | bytes 1572872 | tf_op jit(solution)/shard_map/ppermute | solution.py:210
  116.9 13.2 %collective-permute-start.30 = (bf16[2048,128]{1,0:T(8,128)(2,1)S(1)}, bf16[2048,128]{1,0:T(8,128)(2,1)S(1)}, u32[]{:S(2)}, u32[]{:S(2)}) collective-permute-start(bf16[2048,128]{1,0:T(8,128)(2,1)S(1)} %collective-permute-done.29.refs_24_), channel_id=1, source_target_pairs={{0,1},{1,0},{2,3},{3,2},{4,5},{5,4},{6,7},{7,6},{8,9},{9,8},{10,11... | collective-permute-start | bytes 1572872 | tf_op jit(solution)/shard_map/ppermute | solution.py:213
  117.3 12.8 %collective-permute-start.26 = (bf16[2048,128]{1,0:T(8,128)(2,1)S(1)}, bf16[2048,128]{1,0:T(8,128)(2,1)S(1)}, u32[]{:S(2)}, u32[]{:S(2)}) collective-permute-start(bf16[2048,128]{1,0:T(8,128)(2,1)S(1)} %collective-permute-done.25.refs_20_), channel_id=1, source_target_pairs={{0,1},{1,0},{2,3},{3,2},{4,5},{5,4},{6,7},{7,6},{8,9},{9,8},{10,11... | collective-permute-start | bytes 1572872 | tf_op jit(solution)/shard_map/ppermute | solution.py:213
  123.5 6.6 %collective-permute-start.34 = (bf16[2048,128]{1,0:T(8,128)(2,1)S(1)}, bf16[2048,128]{1,0:T(8,128)(2,1)S(1)}, u32[]{:S(2)}, u32[]{:S(2)}) collective-permute-start(bf16[2048,128]{1,0:T(8,128)(2,1)S(1)} %collective-permute-done.33.refs_28_), channel_id=1, source_target_pairs={{0,1},{1,0},{2,3},{3,2},{4,5},{5,4},{6,7},{7,6},{8,9},{9,8},{10,11... | collective-permute-start | bytes 1572872 | tf_op jit(solution)/shard_map/ppermute | solution.py:213
  138.9 18.4 %collective-permute-start.35 = (bf16[128,4096]{1,0:T(8,128)(2,1)S(1)}, bf16[128,4096]{1,0:T(8,128)(2,1)S(1)}, u32[]{:S(2)}, u32[]{:S(2)}) collective-permute-start(bf16[128,4096]{1,0:T(8,128)(2,1)S(1)} %get-tuple-element.23), channel_id=1, source_target_pairs={{0,1},{1,0},{2,3},{3,2},{4,5},{5,4},{6,7},{7,6},{8,9},{9,8},{10,11... | collective-permute-start | bytes 3145736 | tf_op jit(solution)/shard_map/ppermute | solution.py:280
  139.5 3.6 %collective-permute-start.36 = (f32[8,128]{1,0:T(8,128)S(1)}, f32[8,128]{1,0:T(8,128)S(1)}, u32[]{:S(2)}, u32[]{:S(2)}) collective-permute-start(f32[8,128]{1,0:T(8,128)S(1)} %get-tuple-element.25), channel_id=1, source_target_pairs={{0,2},{1,3},{2,0},{3,1},{4,6},{5,7},{6,4},{7,5},{8,10},{9,11},{10,... | collective-permute-start | bytes 12296 | tf_op jit(solution)/shard_map/ppermute | solution.py:283
  143.3 1.2 collective-permute-start.37
  144.5 3.6 %collective-permute-start.38 = (f32[2]{0:T(128)S(1)}, f32[2]{0:T(128)S(1)}, u32[]{:S(2)}, u32[]{:S(2)}) collective-permute-start(f32[2]{0:T(128)S(1)} %add.170), channel_id=1, source_target_pairs={{0,4},{4,0},{8,12},{12,8},{16,20},{20,16},{24,28},{28,24},{1,5},{5... | collective-permute-start | bytes 32 | tf_op jit(solution)/shard_map/ppermute | solution.py:293
  148.1 3.6 %collective-permute-start.39 = (f32[2]{0:T(128)S(1)}, f32[2]{0:T(128)S(1)}, u32[]{:S(2)}, u32[]{:S(2)}) collective-permute-start(f32[2]{0:T(128)S(1)} %add.171), channel_id=1, source_target_pairs={{0,8},{4,12},{8,0},{12,4},{16,24},{20,28},{24,16},{28,20},{1,9},{5... | collective-permute-start | bytes 32 | tf_op jit(solution)/shard_map/ppermute | solution.py:293
  151.6 5.2 %collective-permute-start.40 = (f32[2]{0:T(128)S(1)}, f32[2]{0:T(128)S(1)}, u32[]{:S(2)}, u32[]{:S(2)}) collective-permute-start(f32[2]{0:T(128)S(1)} %add.172), channel_id=1, source_target_pairs={{0,16},{4,20},{8,24},{12,28},{16,0},{20,4},{24,8},{28,12},{1,17},{... | collective-permute-start | bytes 32 | tf_op jit(solution)/shard_map/ppermute | solution.py:293

commit v3 on v2

--- a/solution.py
+++ b/solution.py
@@ -71,7 +71,7 @@
     slots, position_ref, place_ref, block_ref, bias_ref, inputs, near_first, total_ref, weights_ref, near_weights_ref, *refs,
 ):
     piece_refs, refs = refs[: len(slots)], refs[len(slots) :]
-    activations_ref, theirs_ref, sums_ref, second_sums_ref, first, tiles, second_tiles, outputs, sems = refs
+    activations_ref, theirs_ref, sums_ref, first, tiles, second_tiles, outputs, sems = refs
     position = position_ref[0]
     core = lax.rem(position, 2)
     blocks, half, width = first.shape
@@ -116,7 +116,7 @@
             total = total + result.astype(jnp.float32)
         return total
 
-    sums_ref[...] = collapse(lax.fori_loop(0, 2, first_layer, total_ref[...]))
+    sums_ref[0] = collapse(lax.fori_loop(0, 2, first_layer, total_ref[...]))
     for move in moves:
         move.wait()
 
@@ -144,7 +144,7 @@
     own_rows = pl.ds(pl.multiple_of(core * half, half), half)
     mine = pltpu.make_async_copy(outputs.at[0], activations_ref.at[own_rows], sems.at[5])
     mine.start()
-    second_sums_ref[...] = collapse(second_total)
+    sums_ref[1] = collapse(second_total)
     pltpu.make_async_copy(outputs.at[1], theirs_ref, sems.at[4]).wait()
     mine.wait()
 
@@ -163,19 +163,22 @@
     if groups % 2 or groups > 8:
         piece = jnp.concatenate(parts)
         far = lax.all_gather(piece, "img", axis=0, tiled=True)
-        return [far, nrn(far, perm=xor_pairs(sides, 1))], [2, 3], jnp.zeros((2,), jnp.int32)
+        return [far, nrn(far, perm=xor_pairs(sides, 1))], [2, 3], jnp.zeros((2,), jnp.int32), piece
 
     line = groups // 2
     spot, side = group // 2, group % 2
     upward = lax.rem(position, 2) == 0
 
-    def pairs(steps, move):
+    def far_end(z):
+        return line - 1 if 2 * z < line else 0
+
+    def pairs(steps, move, direct=False):
         found = []
         for g in range(groups):
             for n in range(sides):
                 source = g // 2 - steps if n % 2 == 0 else g // 2 + steps
                 target = move(g, n)
-                if 0 <= source < line and 0 <= target[0] < groups:
+                if 0 <= source < line and 0 <= target[0] < groups and not (direct and source == far_end(g // 2)):
                     found.append((g * sides + n, target[0] * sides + target[1]))
         return found
 
@@ -187,13 +190,29 @@
 
     arrays, slots, places = [], [], []
 
-    def keep(array, slot, steps, crossed, passed, offset=0):
+    last = jnp.where(2 * spot < line, line - 1, 0)
+
+    def keep(array, slot, steps, crossed, passed, offset=0, direct=False):
         step = jnp.where(upward != passed, -steps, steps)
         source = spot + step
         row = (source * 2 + (1 - side if crossed else side)) * piece_rows + offset
+        came = (source >= 0) & (source < line)
+        if direct:
+            came = came & (source != last)
         arrays.append(array)
         slots.append(slot)
-        places.append(jnp.where((source >= 0) & (source < line), row, -1))
+        places.append(jnp.where(came, row, -1))
+
+    last_row = (last * 2 + 1 - side) * piece_rows
+    extra = lax.dynamic_slice(weights, (0, last_row, 0), (1, piece_rows, width))[0]
+    extra = both(extra, perm=[
+        (g * sides + n, g * sides + (n ^ 2)) for g in range(groups) for n in range(sides) if (n % 2 == 0) == (g < line)
+    ])
+    extra_near = nrn(extra, perm=xor_pairs(sides, 1))
+    for slot, array, here in ((2, extra, upward), (3, extra_near, ~upward)):
+        arrays.append(array)
+        slots.append(slot)
+        places.append(jnp.where(here == (2 * spot < line), last_row, -1))
 
     for h, part in enumerate(parts):
         other = both(part, perm=pairs(0, beside))
@@ -208,10 +227,13 @@
             held[h] = both(held[h], perm=pairs(s - 1, onward))
             keep(held[h], 2 + h, s, False, False)
             keep(nrn(held[h], perm=xor_pairs(sides, 1)), 3 - h, s, False, True)
-            other = both(held[h], perm=pairs(s, beside))
-            keep(other, 2 + h, s, True, False)
-            keep(nrn(other, perm=xor_pairs(sides, 1)), 3 - h, s, True, True)
-    return arrays, slots, jnp.stack(places).astype(jnp.int32)
+            moves = pairs(s, beside, direct=h == 1)
+            if not moves:
+                continue
+            other = both(held[h], perm=moves)
+            keep(other, 2 + h, s, True, False, direct=h == 1)
+            keep(nrn(other, perm=xor_pairs(sides, 1)), 3 - h, s, True, True, direct=h == 1)
+    return arrays, slots, jnp.stack(places).astype(jnp.int32), parts[0]
 
 
 def per_device(images, weights, block_index, bias):
@@ -228,16 +250,17 @@
     nrn = functools.partial(lax.ppermute, axis_name="nrn")
 
     weights = weights.reshape(layers, rows * deep, width)
-    pieces, slots, places = gather_far(weights, position, group, sides, groups)
-
+    pieces, slots, places, arrived = gather_far(weights, position, group, sides, groups)
+
+    tables = position.reshape(1), places, block_index.reshape(-1), bias.reshape(layers * sides * rows, width)
+    sent_weights, (place, places, blocks, biases) = lax.optimization_barrier((weights, tables))
+    near_weights = nrn(sent_weights, perm=xor_pairs(sides, 1))
     kept = lax.dynamic_slice(images, (core * half, 0), (half, shard))
-    given = lax.dynamic_slice(images, ((1 - core) * half, 0), (half, shard))
     far = nrn(kept, perm=xor_pairs(sides, 2))
+    late_images, _ = lax.optimization_barrier((images, arrived))
+    given = lax.dynamic_slice(late_images, ((1 - core) * half, 0), (half, shard))
     cross = nrn(given, perm=xor_pairs(sides, 3))
-    tables = position.reshape(1), places, block_index.reshape(-1), bias.reshape(layers * sides * rows, width)
-    given, (place, places, blocks, biases) = lax.optimization_barrier((given, tables))
     near = nrn(given, perm=xor_pairs(sides, 1))
-    near_weights = nrn(weights, perm=xor_pairs(sides, 1))
 
     any_space = pl.BlockSpec(memory_space=pl.ANY)
     smem = pl.BlockSpec(memory_space=pltpu.SMEM)
@@ -256,16 +279,15 @@
         compiler_params=pltpu.CompilerParams(vmem_limit_bytes=near_limit),
         cost_estimate=pl.CostEstimate(flops=2 * flops, bytes_accessed=2**24, transcendentals=0),
     )(place, blocks, biases, images, near, far, cross, weights, near_weights)
-    activations, theirs, first_sums, second_sums = pl.pallas_call(
+    activations, theirs, sums = pl.pallas_call(
         functools.partial(far_kernel, slots),
         out_shape=(
             jax.ShapeDtypeStruct((count, shard), jnp.bfloat16),
             jax.ShapeDtypeStruct((half, shard), jnp.bfloat16),
-            jax.ShapeDtypeStruct((8, half), jnp.float32),
-            jax.ShapeDtypeStruct((8, half), jnp.float32),
+            jax.ShapeDtypeStruct((layers, 8, half), jnp.float32),
         ),
         in_specs=[smem] * 3 + [vmem] * 4 + [any_space] * (2 + len(pieces)),
-        out_specs=(any_space, any_space, vmem, vmem),
+        out_specs=(any_space, any_space, vmem),
         scratch_shapes=[
             pltpu.VMEM((sides * rows, half, width), jnp.bfloat16),
             pltpu.VMEM((2, rows * deep, width), jnp.bfloat16),
@@ -280,14 +302,16 @@
     back = nrn(theirs, perm=xor_pairs(sides, 1))
     activations = lax.dynamic_update_slice(activations, back, ((1 - core) * half, 0))
 
-    second_sums = second_sums + nrn(second_sums, perm=xor_pairs(sides, 2))
-    totals = jnp.stack([first_sums[0], second_sums[0]])
-    live = jnp.sum(jnp.minimum(1.0, totals / neurons / live_level), axis=1)
+    held = [sums]
+    for mask in range(1, sides):
+        held.append(nrn(sums, perm=xor_pairs(sides, mask)))
+    totals = jnp.stack([
+        jnp.stack([held[core_mask][0, 0], held[core_mask][1, 0] + held[core_mask ^ 2][1, 0]]) for core_mask in range(2)
+    ])
+    live = jnp.sum(jnp.minimum(1.0, totals / neurons / live_level), axis=(0, 2))
     if groups & (groups - 1):
-        live = live + nrn(live, perm=xor_pairs(sides, 1))
         live = lax.psum(live, "img")
     else:
-        live = live + nrn(live, perm=xor_pairs(sides, 1))
         mask = 1
         while mask < groups:
             live = live + lax.ppermute(live, "img", xor_pairs(groups, mask))

time: 159 us -> 138 us (0.87)
  waiting for transfers between devices: 66.3 us -> 34.2 us
  starting transfers between devices: 68.9 us -> 74.6 us
  local copies, waits for them, and re-layouts: 6.16 us -> 11.4 us
    ppermute x1, waiting for transfers between devices: 20.9 us -> 2.73 us  [per_device(): cross = nrn(given, perm=xor_pairs(sides, 3))]
    ppermute x1, waiting for transfers between devices: 19.2 us -> 6.04 us  [per_device(): far = nrn(kept, perm=xor_pairs(sides, 2))]
    ppermute x6, starting transfers between devices: 9.72 us -> 16.6 us  [gather_far(): held[h] = both(held[h], perm=pairs(s - 1, onward))]
    ppermute x6, waiting for transfers between devices: 4.85 us -> 8.67 us  [gather_far(): held[h] = both(held[h], perm=pairs(s - 1, onward))]
    ppermute x6, starting transfers between devices: 21.8 us -> 18.1 us  [gather_far(): keep(nrn(held[h], perm=xor_pairs(sides, 1)), 3 - h, s, False, True)]
    unnamed x4 -> x16, local copies, waits for them, and re-layouts: 0.84 us -> 4 us
    ppermute x3, starting transfers between devices: 5.09 us -> 8.25 us  [per_device(): live = live + lax.ppermute(live, 'img', xor_pairs(groups, mask))]
    ppermute x15 -> x16, starting transfers between devices: 22.4 us -> 19.8 us  [the longest x5 9.38 us: gather_far(): nrn(other, perm=xor_pairs(sides, 1))]
  transfers between devices with their start and end apart: 41 -> 42, of which waited for: 14 -> 15; matrix products, arithmetic and copies ran while one was open for 4% -> 5% of each run, Pallas kernels for 4% -> 5%
where the time goes in v3:
time: 138 us; the launch traced here: 137 us
  starting transfers between devices  74.6 us (54%)
  waiting for transfers between devices  34.2 us (25%)
  Pallas kernels  15.2 us (11%)
  local copies, waits for them, and re-layouts  11.4 us (8%)
    ppermute x6, starting transfers between devices, gather_far(): keep(nrn(held[h], perm=xor_pairs(sides, 1)), 3 - h, s, False, True)  18.1 us
    ppermute x6, starting transfers between devices, gather_far(): held[h] = both(held[h], perm=pairs(s - 1, onward))  16.6 us
    ppermute x5, starting transfers between devices, gather_far(): nrn(other, perm=xor_pairs(sides, 1))  9.38 us
    pallas_call x1, Pallas kernels, per_device(): pl.pallas_call(functools.partial(far_kernel, slots), out_shape=(jax.Shape...  8.8 us
    ppermute x6, waiting for transfers between devices, gather_far(): held[h] = both(held[h], perm=pairs(s - 1, onward))  8.67 us
    ppermute x3, starting transfers between devices, per_device(): live = live + lax.ppermute(live, 'img', xor_pairs(groups, mask))  8.25 us
    ppermute x3, waiting for transfers between devices, per_device(): live = live + lax.ppermute(live, 'img', xor_pairs(groups, mask))  7.64 us
    pallas_call x1, Pallas kernels, per_device(): pl.pallas_call(near_kernel, out_shape=(jax.ShapeDtypeStruct((sides * rows...  6.44 us
  transfers between devices with their start and end apart: 42, of which 15 were waited for; matrix products, arithmetic and copies ran while one was open for 5% of the time, Pallas kernels for 5%

profile of v3, /device:TPU:0, one launch (start us, length us, event | category | flops | bytes accessed | tf_op | source)
XLA Modules:
  0.0 137.3 jit_solution(2430395796181305342)
XLA Ops:
  0.9 0.9 copy.6
  1.9 1.0 reshape.55.bias_ref
  3.6 1.1 dynamic-slice_bitcast_fusion.1
  4.7 2.6 %collective-permute-start.9 = (bf16[1024,128]{1,0:T(8,128)(2,1)S(1)}, bf16[1024,128]{1,0:T(8,128)(2,1)}, u32[]{:S(2)}, u32[]{:S(2)}) collective-permute-start(bf16[1024,128]{1,0:T(8,128)(2,1)S(1)} %get-tuple-element.26), channel_id=1, source_target_pairs={{0,2},{1,3},{2,0},{3,1},{4,6},{5,7},{6,4},{7,5},{8,10},{9,11},{10,... | collective-permute-start | bytes 786440 | tf_op jit(solution)/shard_map/ppermute | solution.py:162
  7.3 1.9 %dynamic-slice_bitcast_fusion = bf16[2048,128]{1,0:T(8,128)(2,1)} fusion(bf16[2,16384,128]{2,1,0:T(8,128)(2,1)} %bitcast.43, s32[]{:T(128)S(6)} %select_n.177), kind=kLoop, calls=%fused_computation | loop fusion | bytes 1048580 | tf_op jit(solution)/shard_map/squeeze | solution.py:207
  9.2 3.8 %collective-permute-start.5 = (bf16[2048,128]{1,0:T(8,128)(2,1)}, bf16[2048,128]{1,0:T(8,128)(2,1)S(1)}, u32[]{:S(2)}, u32[]{:S(2)}) collective-permute-start(bf16[2048,128]{1,0:T(8,128)(2,1)} %dynamic-slice_bitcast_fusion), channel_id=1, source_target_pairs={{0,2},{2,0},{4,6},{6,4},{8,10},{10,8},{12,14},{14,12},{17,19},{19,... | collective-permute-start | bytes 1572872 | tf_op jit(solution)/shard_map/ppermute | solution.py:208
  13.1 1.5 %collective-permute-done.9 = bf16[1024,128]{1,0:T(8,128)(2,1)} collective-permute-done((bf16[1024,128]{1,0:T(8,128)(2,1)S(1)}, bf16[1024,128]{1,0:T(8,128)(2,1)}, u32[]{:S(2)}, u32[]{:S(2)}) %collective-permute-start.9) | collective-permute-done | bytes 262176 | tf_op jit(solution)/shard_map/ppermute | solution.py:162
  14.5 2.0 %collective-permute-start.10 = (bf16[1024,128]{1,0:T(8,128)(2,1)}, bf16[1024,128]{1,0:T(8,128)(2,1)S(1)}, u32[]{:S(2)}, u32[]{:S(2)}) collective-permute-start(bf16[1024,128]{1,0:T(8,128)(2,1)} %collective-permute-done.9), channel_id=1, source_target_pairs={{0,4},{1,5},{2,6},{3,7},{4,0},{5,1},{6,2},{7,3},{8,12},{9,13},{10,... | collective-permute-start | bytes 786440 | tf_op jit(solution)/shard_map/ppermute | solution.py:218
  16.6 3.4 %collective-permute-done = bf16[1024,128]{1,0:T(8,128)(2,1)} collective-permute-done((bf16[1024,128]{1,0:T(8,128)(2,1)S(1)}, bf16[1024,128]{1,0:T(8,128)(2,1)}, u32[]{:S(2)}, u32[]{:S(2)}) %collective-permute-start) | collective-permute-done | bytes 262176 | tf_op jit(solution)/shard_map/ppermute | solution.py:162
  19.9 1.8 %collective-permute-start.7 = (bf16[1024,128]{1,0:T(8,128)(2,1)}, bf16[1024,128]{1,0:T(8,128)(2,1)S(1)}, u32[]{:S(2)}, u32[]{:S(2)}) collective-permute-start(bf16[1024,128]{1,0:T(8,128)(2,1)} %collective-permute-done), channel_id=1, source_target_pairs={{0,4},{1,5},{2,6},{3,7},{4,0},{5,1},{6,2},{7,3},{8,12},{9,13},{10,... | collective-permute-start | bytes 786440 | tf_op jit(solution)/shard_map/ppermute | solution.py:218
  21.7 1.1 constant_dynamic-slice_fusion
  22.8 1.5 %collective-permute-start.2 = (bf16[128,4096]{1,0:T(8,128)(2,1)}, bf16[128,4096]{1,0:T(8,128)(2,1)}, u32[]{:S(2)}, u32[]{:S(2)}) collective-permute-start(bf16[128,4096]{1,0:T(8,128)(2,1)} %constant_dynamic-slice_fusion), channel_id=1, source_target_pairs={{0,2},{1,3},{2,0},{3,1},{4,6},{5,7},{6,4},{7,5},{8,10},{9,11},{10,... | collective-permute-start | bytes 3145736 | tf_op jit(solution)/shard_map/ppermute | solution.py:259
  24.3 1.0 constant_dynamic-update-slice_fusion.1
  25.3 1.0 constant_dynamic-update-slice_fusion.refs_6_
  26.3 2.0 %collective-permute-done.7.refs_2_ = bf16[1024,128]{1,0:T(8,128)(2,1)S(1)} collective-permute-done((bf16[1024,128]{1,0:T(8,128)(2,1)}, bf16[1024,128]{1,0:T(8,128)(2,1)S(1)}, u32[]{:S(2)}, u32[]{:S(2)}) %collective-permute-start.7) | collective-permute-done | bytes 262176 | tf_op jit(solution)/shard_map/ppermute | solution.py:218
  28.3 4.3 %collective-permute-start.13 = (bf16[2048,128]{1,0:T(8,128)(2,1)S(1)}, bf16[2048,128]{1,0:T(8,128)(2,1)}, u32[]{:S(2)}, u32[]{:S(2)}) collective-permute-start(bf16[2048,128]{1,0:T(8,128)(2,1)S(1)} %constant_dynamic-update-slice_fusion.refs_6_), channel_id=1, source_target_pairs={{0,8},{2,10},{4,12},{6,14},{8,16},{9,1},{10,18},{11,3},{12,20},{13... | collective-permute-start | bytes 1572872 | tf_op jit(solution)/shard_map/ppermute | solution.py:227
  32.6 0.7 copy-done.3
  33.7 0.7 copy-done.1
  34.9 0.7 copy-done.5
  36.0 2.4 %collective-permute-done.13.refs_8_ = bf16[2048,128]{1,0:T(8,128)(2,1)} collective-permute-done((bf16[2048,128]{1,0:T(8,128)(2,1)S(1)}, bf16[2048,128]{1,0:T(8,128)(2,1)}, u32[]{:S(2)}, u32[]{:S(2)}) %collective-permute-start.13) | collective-permute-done | bytes 524320 | tf_op jit(solution)/shard_map/ppermute | solution.py:227
  38.4 0.7 collective-permute-start.21
  39.1 0.7 collective-permute-start.15
  39.9 3.1 %collective-permute-start.3 = (bf16[128,4096]{1,0:T(8,128)(2,1)S(1)}, bf16[128,4096]{1,0:T(8,128)(2,1)S(1)}, u32[]{:S(2)}, u32[]{:S(2)}) collective-permute-start(bf16[128,4096]{1,0:T(8,128)(2,1)S(1)} %constant_dynamic-slice_fusion.1), channel_id=1, source_target_pairs={{0,3},{1,2},{2,1},{3,0},{4,7},{5,6},{6,5},{7,4},{8,11},{9,10},{10,... | collective-permute-start | bytes 3145736 | tf_op jit(solution)/shard_map/ppermute | solution.py:262
  43.1 6.0 %collective-permute-done.2.far_ref = bf16[128,4096]{1,0:T(8,128)(2,1)} collective-permute-done((bf16[128,4096]{1,0:T(8,128)(2,1)}, bf16[128,4096]{1,0:T(8,128)(2,1)}, u32[]{:S(2)}, u32[]{:S(2)}) %collective-permute-start.2) | collective-permute-done | bytes 1048608 | tf_op jit(solution)/shard_map/ppermute | solution.py:259
  49.6 9.6 %collective-permute-start.17 = (bf16[2048,128]{1,0:T(8,128)(2,1)}, bf16[2048,128]{1,0:T(8,128)(2,1)S(1)}, u32[]{:S(2)}, u32[]{:S(2)}) collective-permute-start(bf16[2048,128]{1,0:T(8,128)(2,1)} %collective-permute-done.12.refs_7_), channel_id=1, source_target_pairs={{0,8},{2,10},{4,12},{6,14},{8,16},{9,1},{10,18},{11,3},{12,20},{13... | collective-permute-start | bytes 1572872 | tf_op jit(solution)/shard_map/ppermute | solution.py:227
  59.3 0.7 collective-permute-start.29
  60.0 6.3 %collective-permute-done.17.refs_12_ = bf16[2048,128]{1,0:T(8,128)(2,1)S(1)} collective-permute-done((bf16[2048,128]{1,0:T(8,128)(2,1)}, bf16[2048,128]{1,0:T(8,128)(2,1)S(1)}, u32[]{:S(2)}, u32[]{:S(2)}) %collective-permute-start.17) | collective-permute-done | bytes 524320 | tf_op jit(solution)/shard_map/ppermute | solution.py:227
  66.2 0.7 collective-permute-start.23
  66.9 2.7 %collective-permute-done.3.cross_ref = bf16[128,4096]{1,0:T(8,128)(2,1)S(1)} collective-permute-done((bf16[128,4096]{1,0:T(8,128)(2,1)S(1)}, bf16[128,4096]{1,0:T(8,128)(2,1)S(1)}, u32[]{:S(2)}, u32[]{:S(2)}) %collective-permute-start.3) | collective-permute-done | bytes 1048608 | tf_op jit(solution)/shard_map/ppermute | solution.py:262
  70.2 0.7 collective-permute-start.25
  70.9 0.7 collective-permute-start.19
  71.7 3.8 %collective-permute-start.18 = (bf16[2048,128]{1,0:T(8,128)(2,1)S(1)}, bf16[2048,128]{1,0:T(8,128)(2,1)S(1)}, u32[]{:S(2)}, u32[]{:S(2)}) collective-permute-start(bf16[2048,128]{1,0:T(8,128)(2,1)S(1)} %collective-permute-done.17.refs_12_), channel_id=1, source_target_pairs={{0,1},{1,0},{2,3},{3,2},{4,5},{5,4},{6,7},{7,6},{8,9},{9,8},{10,11... | collective-permute-start | bytes 1572872 | tf_op jit(solution)/shard_map/ppermute | solution.py:229
  75.5 0.7 collective-permute-start.31
  76.2 6.2 %collective-permute-start.30 = (bf16[2048,128]{1,0:T(8,128)(2,1)S(1)}, bf16[2048,128]{1,0:T(8,128)(2,1)S(1)}, u32[]{:S(2)}, u32[]{:S(2)}) collective-permute-start(bf16[2048,128]{1,0:T(8,128)(2,1)S(1)} %collective-permute-done.29.refs_24_), channel_id=1, source_target_pairs={{0,1},{1,0},{2,3},{3,2},{4,5},{5,4},{6,7},{7,6},{8,9},{9,8},{10,11... | collective-permute-start | bytes 1572872 | tf_op jit(solution)/shard_map/ppermute | solution.py:229
  82.4 0.7 collective-permute-start.33
  83.1 0.7 collective-permute-start.27
  83.9 7.1 %collective-permute-start.26 = (bf16[2048,128]{1,0:T(8,128)(2,1)S(1)}, bf16[2048,128]{1,0:T(8,128)(2,1)S(1)}, u32[]{:S(2)}, u32[]{:S(2)}) collective-permute-start(bf16[2048,128]{1,0:T(8,128)(2,1)S(1)} %collective-permute-done.25.refs_20_), channel_id=1, source_target_pairs={{0,1},{1,0},{2,3},{3,2},{4,5},{5,4},{6,7},{7,6},{8,9},{9,8},{10,11... | collective-permute-start | bytes 1572872 | tf_op jit(solution)/shard_map/ppermute | solution.py:229
  91.1 8.8 %collective-permute-start.32 = (bf16[2048,128]{1,0:T(8,128)(2,1)S(1)}, bf16[2048,128]{1,0:T(8,128)(2,1)S(1)}, u32[]{:S(2)}, u32[]{:S(2)}) collective-permute-start(bf16[2048,128]{1,0:T(8,128)(2,1)S(1)} %collective-permute-done.31.refs_26_), channel_id=1, source_target_pairs={{0,1},{1,0},{2,3},{3,2},{4,5},{5,4},{6,7},{7,6},{8,9},{9,8},{10,11... | collective-permute-start | bytes 1572872 | tf_op jit(solution)/shard_map/ppermute | solution.py:235
  100.4 6.4 %shard_map.59 = (bf16[128,128,128]{2,1,0:T(8,128)(2,1)S(1)}, bf16[2,32,128,128]{3,2,1,0:T(8,128)(2,1)S(1)}, f32[128,128]{1,0:T(8,128)S(1)}) custom-call(s32[1]{0:T(128)} %bitcast.1.position_ref, s32[1024]{0:T(1024)S(1)} %reshape.54.block_ref, f32[256,128]{1,0:T(8,128)S(1)} %reshape.55.bias_ref, bf16[256,4096]{1,0:T(8,128)(2,1)S(1)} %copy-done, ...), custom_call_target="tpu_custom_call" | custom-call | flops 1073741824 | bytes 16777216 | tf_op jit(solution)/shard_map/pallas_call | solution.py:269
  107.0 8.8 %shard_map.60 = (bf16[256,4096]{1,0:T(8,128)(2,1)}, bf16[128,4096]{1,0:T(8,128)(2,1)S(1)}, f32[2,8,128]{2,1,0:T(8,128)S(1)}) custom-call(s32[1]{0:T(128)} %bitcast.1.position_ref, s32[30]{0:T(128)S(1)} %stack.113.place_ref, s32[1024]{0:T(1024)S(1)} %reshape.54.block_ref, f32[256,128]{1,0:T(8,128)S(1)} %reshape.55.bias_ref, ...), custom_call_target="tpu_custom_call" | custom-call | flops 2147483648 | bytes 16777216 | tf_op jit(solution)/shard_map/pallas_call | solution.py:282
  116.6 1.5 %collective-permute-start.38 = (f32[2,8,128]{2,1,0:T(8,128)S(1)}, f32[2,8,128]{2,1,0:T(8,128)S(1)}, u32[]{:S(2)}, u32[]{:S(2)}) collective-permute-start(f32[2,8,128]{2,1,0:T(8,128)S(1)} %get-tuple-element.25), channel_id=1, source_target_pairs={{0,3},{1,2},{2,1},{3,0},{4,7},{5,6},{6,5},{7,4},{8,11},{9,10},{10,... | collective-permute-start | bytes 24584 | tf_op jit(solution)/shard_map/ppermute | solution.py:307
  118.0 1.5 %collective-permute-done.36 = f32[2,8,128]{2,1,0:T(8,128)S(1)} collective-permute-done((f32[2,8,128]{2,1,0:T(8,128)S(1)}, f32[2,8,128]{2,1,0:T(8,128)S(1)}, u32[]{:S(2)}, u32[]{:S(2)}) %collective-permute-start.36) | collective-permute-done | bytes 8224 | tf_op jit(solution)/shard_map/ppermute | solution.py:307
  119.8 1.1 collective-permute-start.39
  120.9 2.5 %collective-permute-done.39 = f32[2]{0:T(128)S(1)} collective-permute-done((f32[2]{0:T(128)S(1)}, f32[2]{0:T(128)S(1)}, u32[]{:S(2)}, u32[]{:S(2)}) %collective-permute-start.39) | collective-permute-done | bytes 40 | tf_op jit(solution)/shard_map/ppermute | solution.py:317
  123.4 3.6 %collective-permute-done.40 = f32[2]{0:T(128)S(1)} collective-permute-done((f32[2]{0:T(128)S(1)}, f32[2]{0:T(128)S(1)}, u32[]{:S(2)}, u32[]{:S(2)}) %collective-permute-start.40) | collective-permute-done | bytes 40 | tf_op jit(solution)/shard_map/ppermute | solution.py:317
  127.0 7.2 %collective-permute-start.41 = (f32[2]{0:T(128)S(1)}, f32[2]{0:T(128)S(1)}, u32[]{:S(2)}, u32[]{:S(2)}) collective-permute-start(f32[2]{0:T(128)S(1)} %add.198), channel_id=1, source_target_pairs={{0,16},{4,20},{8,24},{12,28},{16,0},{20,4},{24,8},{28,12},{1,17},{... | collective-permute-start | bytes 32 | tf_op jit(solution)/shard_map/ppermute | solution.py:317
  134.2 1.5 %collective-permute-done.41 = f32[2]{0:T(128)S(1)} collective-permute-done((f32[2]{0:T(128)S(1)}, f32[2]{0:T(128)S(1)}, u32[]{:S(2)}, u32[]{:S(2)}) %collective-permute-start.41) | collective-permute-done | bytes 40 | tf_op jit(solution)/shard_map/ppermute | solution.py:317
  136.2 1.1 constant_dynamic-update-slice_fusion.2
  (70 shorter events, 6.0 us)
Async XLA Ops:
  0.6 21.1 %copy-start = (bf16[256,4096]{1,0:T(8,128)(2,1)S(1)}, bf16[256,4096]{1,0:T(8,128)(2,1)}, u32[]{:S(2)}) copy-start(bf16[256,4096]{1,0:T(8,128)(2,1)} %own_ref.1) | copy-start | bytes 6291460
  3.1 96.9 %collective-permute-start.4 = (bf16[2,16384,128]{2,1,0:T(8,128)(2,1)}, bf16[2,16384,128]{2,1,0:T(8,128)(2,1)}, u32[]{:S(2)}, u32[]{:S(2)}) collective-permute-start(bf16[2,16384,128]{2,1,0:T(8,128)(2,1)} %bitcast.41), channel_id=1, source_target_pairs={{0,1},{1,0},{2,3},{3,2},{4,5},{5,4},{6,7},{7,6},{8,9},{9,8},{10,11... | collective-permute-start | bytes 25165832 | tf_op jit(solution)/shard_map/ppermute | solution.py:257
  4.7 9.8 %collective-permute-start.9 = (bf16[1024,128]{1,0:T(8,128)(2,1)S(1)}, bf16[1024,128]{1,0:T(8,128)(2,1)}, u32[]{:S(2)}, u32[]{:S(2)}) collective-permute-start(bf16[1024,128]{1,0:T(8,128)(2,1)S(1)} %get-tuple-element.26), channel_id=1, source_target_pairs={{0,2},{1,3},{2,0},{3,1},{4,6},{5,7},{6,4},{7,5},{8,10},{9,11},{10,... | collective-permute-start | bytes 786440 | tf_op jit(solution)/shard_map/ppermute | solution.py:162
  7.3 12.7 %collective-permute-start = (bf16[1024,128]{1,0:T(8,128)(2,1)S(1)}, bf16[1024,128]{1,0:T(8,128)(2,1)}, u32[]{:S(2)}, u32[]{:S(2)}) collective-permute-start(bf16[1024,128]{1,0:T(8,128)(2,1)S(1)} %get-tuple-element.27), channel_id=1, source_target_pairs={{0,2},{1,3},{2,0},{3,1},{4,6},{5,7},{6,4},{7,5},{8,10},{9,11},{10,... | collective-permute-start | bytes 786440 | tf_op jit(solution)/shard_map/ppermute | solution.py:162
  9.2 23.3 %collective-permute-start.5 = (bf16[2048,128]{1,0:T(8,128)(2,1)}, bf16[2048,128]{1,0:T(8,128)(2,1)S(1)}, u32[]{:S(2)}, u32[]{:S(2)}) collective-permute-start(bf16[2048,128]{1,0:T(8,128)(2,1)} %dynamic-slice_bitcast_fusion), channel_id=1, source_target_pairs={{0,2},{2,0},{4,6},{6,4},{8,10},{10,8},{12,14},{14,12},{17,19},{19,... | collective-permute-start | bytes 1572872 | tf_op jit(solution)/shard_map/ppermute | solution.py:208
  14.5 10.7 %collective-permute-start.10 = (bf16[1024,128]{1,0:T(8,128)(2,1)}, bf16[1024,128]{1,0:T(8,128)(2,1)S(1)}, u32[]{:S(2)}, u32[]{:S(2)}) collective-permute-start(bf16[1024,128]{1,0:T(8,128)(2,1)} %collective-permute-done.9), channel_id=1, source_target_pairs={{0,4},{1,5},{2,6},{3,7},{4,0},{5,1},{6,2},{7,3},{8,12},{9,13},{10,... | collective-permute-start | bytes 786440 | tf_op jit(solution)/shard_map/ppermute | solution.py:218
  19.9 8.3 %collective-permute-start.7 = (bf16[1024,128]{1,0:T(8,128)(2,1)}, bf16[1024,128]{1,0:T(8,128)(2,1)S(1)}, u32[]{:S(2)}, u32[]{:S(2)}) collective-permute-start(bf16[1024,128]{1,0:T(8,128)(2,1)} %collective-permute-done), channel_id=1, source_target_pairs={{0,4},{1,5},{2,6},{3,7},{4,0},{5,1},{6,2},{7,3},{8,12},{9,13},{10,... | collective-permute-start | bytes 786440 | tf_op jit(solution)/shard_map/ppermute | solution.py:218
  22.8 26.3 %collective-permute-start.2 = (bf16[128,4096]{1,0:T(8,128)(2,1)}, bf16[128,4096]{1,0:T(8,128)(2,1)}, u32[]{:S(2)}, u32[]{:S(2)}) collective-permute-start(bf16[128,4096]{1,0:T(8,128)(2,1)} %constant_dynamic-slice_fusion), channel_id=1, source_target_pairs={{0,2},{1,3},{2,0},{3,1},{4,6},{5,7},{6,4},{7,5},{8,10},{9,11},{10,... | collective-permute-start | bytes 3145736 | tf_op jit(solution)/shard_map/ppermute | solution.py:259
  25.2 7.3 %collective-permute-start.11 = (bf16[1024,128]{1,0:T(8,128)(2,1)S(1)}, bf16[1024,128]{1,0:T(8,128)(2,1)S(1)}, u32[]{:S(2)}, u32[]{:S(2)}) collective-permute-start(bf16[1024,128]{1,0:T(8,128)(2,1)S(1)} %collective-permute-done.10.refs_4_), channel_id=1, source_target_pairs={{0,1},{1,0},{2,3},{3,2},{4,5},{5,4},{6,7},{7,6},{8,9},{9,8},{10,11... | collective-permute-start | bytes 786440 | tf_op jit(solution)/shard_map/ppermute | solution.py:220
  28.3 10.1 %collective-permute-start.13 = (bf16[2048,128]{1,0:T(8,128)(2,1)S(1)}, bf16[2048,128]{1,0:T(8,128)(2,1)}, u32[]{:S(2)}, u32[]{:S(2)}) collective-permute-start(bf16[2048,128]{1,0:T(8,128)(2,1)S(1)} %constant_dynamic-update-slice_fusion.refs_6_), channel_id=1, source_target_pairs={{0,8},{2,10},{4,12},{6,14},{8,16},{9,1},{10,18},{11,3},{12,20},{13... | collective-permute-start | bytes 1572872 | tf_op jit(solution)/shard_map/ppermute | solution.py:227
  32.5 6.5 %collective-permute-start.12 = (bf16[2048,128]{1,0:T(8,128)(2,1)S(1)}, bf16[2048,128]{1,0:T(8,128)(2,1)}, u32[]{:S(2)}, u32[]{:S(2)}) collective-permute-start(bf16[2048,128]{1,0:T(8,128)(2,1)S(1)} %constant_dynamic-update-slice_fusion.refs_6_), channel_id=1, source_target_pairs={{0,1},{1,0},{2,3},{3,2},{4,5},{5,4},{6,7},{7,6},{8,9},{9,8},{10,11... | collective-permute-start | bytes 1572872 | tf_op jit(solution)/shard_map/ppermute | solution.py:222
  32.5 0.7 copy-start.3
  33.2 1.7 %collective-permute-start.8 = (bf16[1024,128]{1,0:T(8,128)(2,1)S(1)}, bf16[1024,128]{1,0:T(8,128)(2,1)S(1)}, u32[]{:S(2)}, u32[]{:S(2)}) collective-permute-start(bf16[1024,128]{1,0:T(8,128)(2,1)S(1)} %collective-permute-done.7.refs_2_), channel_id=1, source_target_pairs={{0,1},{1,0},{2,3},{3,2},{4,5},{5,4},{6,7},{7,6},{8,9},{9,8},{10,11... | collective-permute-start | bytes 786440 | tf_op jit(solution)/shard_map/ppermute | solution.py:220
  33.7 0.7 copy-start.1
  35.6 4.3 %collective-permute-start.6 = (bf16[2048,128]{1,0:T(8,128)(2,1)S(1)}, bf16[2048,128]{1,0:T(8,128)(2,1)}, u32[]{:S(2)}, u32[]{:S(2)}) collective-permute-start(bf16[2048,128]{1,0:T(8,128)(2,1)S(1)} %collective-permute-done.5.refs_0_), channel_id=1, source_target_pairs={{0,1},{1,0},{2,3},{3,2},{4,5},{5,4},{6,7},{7,6},{8,9},{9,8},{10,11... | collective-permute-start | bytes 1572872 | tf_op jit(solution)/shard_map/ppermute | solution.py:211
  38.4 10.7 %collective-permute-start.21 = (bf16[2048,128]{1,0:T(8,128)(2,1)}, bf16[2048,128]{1,0:T(8,128)(2,1)S(1)}, u32[]{:S(2)}, u32[]{:S(2)}) collective-permute-start(bf16[2048,128]{1,0:T(8,128)(2,1)} %collective-permute-done.13.refs_8_), channel_id=1, source_target_pairs={{8,16},{9,1},{10,18},{11,3},{12,20},{13,5},{14,22},{15,7},{16,24},... | collective-permute-start | bytes 1572872 | tf_op jit(solution)/shard_map/ppermute | solution.py:227
  39.1 10.5 %collective-permute-start.15 = (bf16[2048,128]{1,0:T(8,128)(2,1)}, bf16[2048,128]{1,0:T(8,128)(2,1)S(1)}, u32[]{:S(2)}, u32[]{:S(2)}) collective-permute-start(bf16[2048,128]{1,0:T(8,128)(2,1)} %collective-permute-done.13.refs_8_), channel_id=1, source_target_pairs={{1,5},{3,7},{5,1},{7,3},{8,12},{9,13},{10,14},{11,15},{12,8},{13,9... | collective-permute-start | bytes 1572872 | tf_op jit(solution)/shard_map/ppermute | solution.py:233
  39.9 67.0 %copy-start.2 = (bf16[1024,128]{1,0:T(8,128)(2,1)S(1)}, bf16[1024,128]{1,0:T(8,128)(2,1)}, u32[]{:S(2)}) copy-start(bf16[1024,128]{1,0:T(8,128)(2,1)} %copy-done.1) | copy-start | bytes 786436
  39.9 67.0 %copy-start.4 = (bf16[1024,128]{1,0:T(8,128)(2,1)S(1)}, bf16[1024,128]{1,0:T(8,128)(2,1)}, u32[]{:S(2)}) copy-start(bf16[1024,128]{1,0:T(8,128)(2,1)} %copy-done.3) | copy-start | bytes 786436
  39.9 67.0 %copy-start.6 = (bf16[1024,128]{1,0:T(8,128)(2,1)S(1)}, bf16[1024,128]{1,0:T(8,128)(2,1)}, u32[]{:S(2)}) copy-start(bf16[1024,128]{1,0:T(8,128)(2,1)} %copy-done.5) | copy-start | bytes 786436
  39.9 29.7 %collective-permute-start.3 = (bf16[128,4096]{1,0:T(8,128)(2,1)S(1)}, bf16[128,4096]{1,0:T(8,128)(2,1)S(1)}, u32[]{:S(2)}, u32[]{:S(2)}) collective-permute-start(bf16[128,4096]{1,0:T(8,128)(2,1)S(1)} %constant_dynamic-slice_fusion.1), channel_id=1, source_target_pairs={{0,3},{1,2},{2,1},{3,0},{4,7},{5,6},{6,5},{7,4},{8,11},{9,10},{10,... | collective-permute-start | bytes 3145736 | tf_op jit(solution)/shard_map/ppermute | solution.py:262
  49.1 21.1 %collective-permute-start.1 = (bf16[128,4096]{1,0:T(8,128)(2,1)S(1)}, bf16[128,4096]{1,0:T(8,128)(2,1)S(1)}, u32[]{:S(2)}, u32[]{:S(2)}) collective-permute-start(bf16[128,4096]{1,0:T(8,128)(2,1)S(1)} %constant_dynamic-slice_fusion.1), channel_id=1, source_target_pairs={{0,1},{1,0},{2,3},{3,2},{4,5},{5,4},{6,7},{7,6},{8,9},{9,8},{10,11... | collective-permute-start | bytes 3145736 | tf_op jit(solution)/shard_map/ppermute | solution.py:263
  49.1 10.1 %collective-permute-start.14 = (bf16[2048,128]{1,0:T(8,128)(2,1)}, bf16[2048,128]{1,0:T(8,128)(2,1)S(1)}, u32[]{:S(2)}, u32[]{:S(2)}) collective-permute-start(bf16[2048,128]{1,0:T(8,128)(2,1)} %collective-permute-done.13.refs_8_), channel_id=1, source_target_pairs={{0,1},{1,0},{2,3},{3,2},{4,5},{5,4},{6,7},{7,6},{8,9},{9,8},{10,11... | collective-permute-start | bytes 1572872 | tf_op jit(solution)/shard_map/ppermute | solution.py:229
  49.6 16.6 %collective-permute-start.17 = (bf16[2048,128]{1,0:T(8,128)(2,1)}, bf16[2048,128]{1,0:T(8,128)(2,1)S(1)}, u32[]{:S(2)}, u32[]{:S(2)}) collective-permute-start(bf16[2048,128]{1,0:T(8,128)(2,1)} %collective-permute-done.12.refs_7_), channel_id=1, source_target_pairs={{0,8},{2,10},{4,12},{6,14},{8,16},{9,1},{10,18},{11,3},{12,20},{13... | collective-permute-start | bytes 1572872 | tf_op jit(solution)/shard_map/ppermute | solution.py:227
  59.3 10.9 %collective-permute-start.29 = (bf16[2048,128]{1,0:T(8,128)(2,1)S(1)}, bf16[2048,128]{1,0:T(8,128)(2,1)S(1)}, u32[]{:S(2)}, u32[]{:S(2)}) collective-permute-start(bf16[2048,128]{1,0:T(8,128)(2,1)S(1)} %collective-permute-done.21.refs_16_), channel_id=1, source_target_pairs={{9,1},{11,3},{13,5},{15,7},{16,24},{18,26},{20,28},{22,30}} | collective-permute-start | bytes 1572872 | tf_op jit(solution)/shard_map/ppermute | solution.py:227
  66.2 4.7 %collective-permute-start.23 = (bf16[2048,128]{1,0:T(8,128)(2,1)S(1)}, bf16[2048,128]{1,0:T(8,128)(2,1)S(1)}, u32[]{:S(2)}, u32[]{:S(2)}) collective-permute-start(bf16[2048,128]{1,0:T(8,128)(2,1)S(1)} %collective-permute-done.21.refs_16_), channel_id=1, source_target_pairs={{1,5},{3,7},{5,1},{7,3},{9,13},{11,15},{13,9},{15,11},{16,20},{18,... | collective-permute-start | bytes 1572872 | tf_op jit(solution)/shard_map/ppermute | solution.py:233
  69.6 2.1 %collective-permute-start.22 = (bf16[2048,128]{1,0:T(8,128)(2,1)S(1)}, bf16[2048,128]{1,0:T(8,128)(2,1)S(1)}, u32[]{:S(2)}, u32[]{:S(2)}) collective-permute-start(bf16[2048,128]{1,0:T(8,128)(2,1)S(1)} %collective-permute-done.21.refs_16_), channel_id=1, source_target_pairs={{0,1},{1,0},{2,3},{3,2},{4,5},{5,4},{6,7},{7,6},{8,9},{9,8},{10,11... | collective-permute-start | bytes 1572872 | tf_op jit(solution)/shard_map/ppermute | solution.py:229
  70.2 5.3 %collective-permute-start.16 = (bf16[2048,128]{1,0:T(8,128)(2,1)S(1)}, bf16[2048,128]{1,0:T(8,128)(2,1)S(1)}, u32[]{:S(2)}, u32[]{:S(2)}) collective-permute-start(bf16[2048,128]{1,0:T(8,128)(2,1)S(1)} %collective-permute-done.15.refs_10_), channel_id=1, source_target_pairs={{0,1},{1,0},{2,3},{3,2},{4,5},{5,4},{6,7},{7,6},{8,9},{9,8},{10,11... | collective-permute-start | bytes 1572872 | tf_op jit(solution)/shard_map/ppermute | solution.py:235
  70.2 6.0 %collective-permute-start.25 = (bf16[2048,128]{1,0:T(8,128)(2,1)S(1)}, bf16[2048,128]{1,0:T(8,128)(2,1)S(1)}, u32[]{:S(2)}, u32[]{:S(2)}) collective-permute-start(bf16[2048,128]{1,0:T(8,128)(2,1)S(1)} %collective-permute-done.17.refs_12_), channel_id=1, source_target_pairs={{8,16},{9,1},{10,18},{11,3},{12,20},{13,5},{14,22},{15,7},{16,24},... | collective-permute-start | bytes 1572872 | tf_op jit(solution)/shard_map/ppermute | solution.py:227
  70.9 11.4 %collective-permute-start.19 = (bf16[2048,128]{1,0:T(8,128)(2,1)S(1)}, bf16[2048,128]{1,0:T(8,128)(2,1)S(1)}, u32[]{:S(2)}, u32[]{:S(2)}) collective-permute-start(bf16[2048,128]{1,0:T(8,128)(2,1)S(1)} %collective-permute-done.17.refs_12_), channel_id=1, source_target_pairs={{1,5},{3,7},{5,1},{7,3},{8,12},{9,13},{10,14},{11,15},{12,8},{13,9... | collective-permute-start | bytes 1572872 | tf_op jit(solution)/shard_map/ppermute | solution.py:233
  71.7 10.6 %collective-permute-start.18 = (bf16[2048,128]{1,0:T(8,128)(2,1)S(1)}, bf16[2048,128]{1,0:T(8,128)(2,1)S(1)}, u32[]{:S(2)}, u32[]{:S(2)}) collective-permute-start(bf16[2048,128]{1,0:T(8,128)(2,1)S(1)} %collective-permute-done.17.refs_12_), channel_id=1, source_target_pairs={{0,1},{1,0},{2,3},{3,2},{4,5},{5,4},{6,7},{7,6},{8,9},{9,8},{10,11... | collective-permute-start | bytes 1572872 | tf_op jit(solution)/shard_map/ppermute | solution.py:229
  75.5 7.6 %collective-permute-start.31 = (bf16[2048,128]{1,0:T(8,128)(2,1)S(1)}, bf16[2048,128]{1,0:T(8,128)(2,1)S(1)}, u32[]{:S(2)}, u32[]{:S(2)}) collective-permute-start(bf16[2048,128]{1,0:T(8,128)(2,1)S(1)} %collective-permute-done.29.refs_24_), channel_id=1, source_target_pairs={{1,5},{3,7},{5,1},{7,3},{24,28},{26,30},{28,24},{30,26}} | collective-permute-start | bytes 1572872 | tf_op jit(solution)/shard_map/ppermute | solution.py:233
  76.2 7.7 %collective-permute-start.30 = (bf16[2048,128]{1,0:T(8,128)(2,1)S(1)}, bf16[2048,128]{1,0:T(8,128)(2,1)S(1)}, u32[]{:S(2)}, u32[]{:S(2)}) collective-permute-start(bf16[2048,128]{1,0:T(8,128)(2,1)S(1)} %collective-permute-done.29.refs_24_), channel_id=1, source_target_pairs={{0,1},{1,0},{2,3},{3,2},{4,5},{5,4},{6,7},{7,6},{8,9},{9,8},{10,11... | collective-permute-start | bytes 1572872 | tf_op jit(solution)/shard_map/ppermute | solution.py:229
  82.4 8.7 %collective-permute-start.24 = (bf16[2048,128]{1,0:T(8,128)(2,1)S(1)}, bf16[2048,128]{1,0:T(8,128)(2,1)S(1)}, u32[]{:S(2)}, u32[]{:S(2)}) collective-permute-start(bf16[2048,128]{1,0:T(8,128)(2,1)S(1)} %collective-permute-done.23.refs_18_), channel_id=1, source_target_pairs={{0,1},{1,0},{2,3},{3,2},{4,5},{5,4},{6,7},{7,6},{8,9},{9,8},{10,11... | collective-permute-start | bytes 1572872 | tf_op jit(solution)/shard_map/ppermute | solution.py:235
  82.4 8.7 %collective-permute-start.33 = (bf16[2048,128]{1,0:T(8,128)(2,1)S(1)}, bf16[2048,128]{1,0:T(8,128)(2,1)S(1)}, u32[]{:S(2)}, u32[]{:S(2)}) collective-permute-start(bf16[2048,128]{1,0:T(8,128)(2,1)S(1)} %collective-permute-done.25.refs_20_), channel_id=1, source_target_pairs={{9,1},{11,3},{13,5},{15,7},{16,24},{18,26},{20,28},{22,30}} | collective-permute-start | bytes 1572872 | tf_op jit(solution)/shard_map/ppermute | solution.py:227
  83.1 16.8 %collective-permute-start.27 = (bf16[2048,128]{1,0:T(8,128)(2,1)S(1)}, bf16[2048,128]{1,0:T(8,128)(2,1)S(1)}, u32[]{:S(2)}, u32[]{:S(2)}) collective-permute-start(bf16[2048,128]{1,0:T(8,128)(2,1)S(1)} %collective-permute-done.25.refs_20_), channel_id=1, source_target_pairs={{1,5},{3,7},{5,1},{7,3},{24,28},{26,30},{28,24},{30,26}} | collective-permute-start | bytes 1572872 | tf_op jit(solution)/shard_map/ppermute | solution.py:233
  83.9 23.0 %collective-permute-start.26 = (bf16[2048,128]{1,0:T(8,128)(2,1)S(1)}, bf16[2048,128]{1,0:T(8,128)(2,1)S(1)}, u32[]{:S(2)}, u32[]{:S(2)}) collective-permute-start(bf16[2048,128]{1,0:T(8,128)(2,1)S(1)} %collective-permute-done.25.refs_20_), channel_id=1, source_target_pairs={{0,1},{1,0},{2,3},{3,2},{4,5},{5,4},{6,7},{7,6},{8,9},{9,8},{10,11... | collective-permute-start | bytes 1572872 | tf_op jit(solution)/shard_map/ppermute | solution.py:229
  91.0 15.8 %collective-permute-start.20 = (bf16[2048,128]{1,0:T(8,128)(2,1)S(1)}, bf16[2048,128]{1,0:T(8,128)(2,1)S(1)}, u32[]{:S(2)}, u32[]{:S(2)}) collective-permute-start(bf16[2048,128]{1,0:T(8,128)(2,1)S(1)} %collective-permute-done.19.refs_14_), channel_id=1, source_target_pairs={{0,1},{1,0},{2,3},{3,2},{4,5},{5,4},{6,7},{7,6},{8,9},{9,8},{10,11... | collective-permute-start | bytes 1572872 | tf_op jit(solution)/shard_map/ppermute | solution.py:235
  91.1 15.8 %collective-permute-start.32 = (bf16[2048,128]{1,0:T(8,128)(2,1)S(1)}, bf16[2048,128]{1,0:T(8,128)(2,1)S(1)}, u32[]{:S(2)}, u32[]{:S(2)}) collective-permute-start(bf16[2048,128]{1,0:T(8,128)(2,1)S(1)} %collective-permute-done.31.refs_26_), channel_id=1, source_target_pairs={{0,1},{1,0},{2,3},{3,2},{4,5},{5,4},{6,7},{7,6},{8,9},{9,8},{10,11... | collective-permute-start | bytes 1572872 | tf_op jit(solution)/shard_map/ppermute | solution.py:235
  99.9 7.0 %collective-permute-start.34 = (bf16[2048,128]{1,0:T(8,128)(2,1)S(1)}, bf16[2048,128]{1,0:T(8,128)(2,1)S(1)}, u32[]{:S(2)}, u32[]{:S(2)}) collective-permute-start(bf16[2048,128]{1,0:T(8,128)(2,1)S(1)} %collective-permute-done.33.refs_28_), channel_id=1, source_target_pairs={{0,1},{1,0},{2,3},{3,2},{4,5},{5,4},{6,7},{7,6},{8,9},{9,8},{10,11... | collective-permute-start | bytes 1572872 | tf_op jit(solution)/shard_map/ppermute | solution.py:229
  99.9 7.0 %collective-permute-start.28 = (bf16[2048,128]{1,0:T(8,128)(2,1)S(1)}, bf16[2048,128]{1,0:T(8,128)(2,1)S(1)}, u32[]{:S(2)}, u32[]{:S(2)}) collective-permute-start(bf16[2048,128]{1,0:T(8,128)(2,1)S(1)} %collective-permute-done.27.refs_22_), channel_id=1, source_target_pairs={{0,1},{1,0},{2,3},{3,2},{4,5},{5,4},{6,7},{7,6},{8,9},{9,8},{10,11... | collective-permute-start | bytes 1572872 | tf_op jit(solution)/shard_map/ppermute | solution.py:235
  115.8 20.5 %collective-permute-start.35 = (bf16[128,4096]{1,0:T(8,128)(2,1)S(1)}, bf16[128,4096]{1,0:T(8,128)(2,1)S(1)}, u32[]{:S(2)}, u32[]{:S(2)}) collective-permute-start(bf16[128,4096]{1,0:T(8,128)(2,1)S(1)} %get-tuple-element.24), channel_id=1, source_target_pairs={{0,1},{1,0},{2,3},{3,2},{4,5},{5,4},{6,7},{7,6},{8,9},{9,8},{10,11... | collective-permute-start | bytes 3145736 | tf_op jit(solution)/shard_map/ppermute | solution.py:302
  115.9 3.7 %collective-permute-start.36 = (f32[2,8,128]{2,1,0:T(8,128)S(1)}, f32[2,8,128]{2,1,0:T(8,128)S(1)}, u32[]{:S(2)}, u32[]{:S(2)}) collective-permute-start(f32[2,8,128]{2,1,0:T(8,128)S(1)} %get-tuple-element.25), channel_id=1, source_target_pairs={{0,2},{1,3},{2,0},{3,1},{4,6},{5,7},{6,4},{7,5},{8,10},{9,11},{10,... | collective-permute-start | bytes 24584 | tf_op jit(solution)/shard_map/ppermute | solution.py:307
  116.4 3.1 %collective-permute-start.37 = (f32[2,8,128]{2,1,0:T(8,128)S(1)}, f32[2,8,128]{2,1,0:T(8,128)S(1)}, u32[]{:S(2)}, u32[]{:S(2)}) collective-permute-start(f32[2,8,128]{2,1,0:T(8,128)S(1)} %get-tuple-element.25), channel_id=1, source_target_pairs={{0,1},{1,0},{2,3},{3,2},{4,5},{5,4},{6,7},{7,6},{8,9},{9,8},{10,11... | collective-permute-start | bytes 24584 | tf_op jit(solution)/shard_map/ppermute | solution.py:307
  116.6 3.1 %collective-permute-start.38 = (f32[2,8,128]{2,1,0:T(8,128)S(1)}, f32[2,8,128]{2,1,0:T(8,128)S(1)}, u32[]{:S(2)}, u32[]{:S(2)}) collective-permute-start(f32[2,8,128]{2,1,0:T(8,128)S(1)} %get-tuple-element.25), channel_id=1, source_target_pairs={{0,3},{1,2},{2,1},{3,0},{4,7},{5,6},{6,5},{7,4},{8,11},{9,10},{10,... | collective-permute-start | bytes 24584 | tf_op jit(solution)/shard_map/ppermute | solution.py:307
  119.8 3.6 %collective-permute-start.39 = (f32[2]{0:T(128)S(1)}, f32[2]{0:T(128)S(1)}, u32[]{:S(2)}, u32[]{:S(2)}) collective-permute-start(f32[2]{0:T(128)S(1)} %fusion.1), channel_id=1, source_target_pairs={{0,4},{4,0},{8,12},{12,8},{16,20},{20,16},{24,28},{28,24},{1,5},{5... | collective-permute-start | bytes 32 | tf_op jit(solution)/shard_map/ppermute | solution.py:317
  123.4 3.6 %collective-permute-start.40 = (f32[2]{0:T(128)S(1)}, f32[2]{0:T(128)S(1)}, u32[]{:S(2)}, u32[]{:S(2)}) collective-permute-start(f32[2]{0:T(128)S(1)} %add.197), channel_id=1, source_target_pairs={{0,8},{4,12},{8,0},{12,4},{16,24},{20,28},{24,16},{28,20},{1,9},{5... | collective-permute-start | bytes 32 | tf_op jit(solution)/shard_map/ppermute | solution.py:317
  127.0 8.7 %collective-permute-start.41 = (f32[2]{0:T(128)S(1)}, f32[2]{0:T(128)S(1)}, u32[]{:S(2)}, u32[]{:S(2)}) collective-permute-start(f32[2]{0:T(128)S(1)} %add.198), channel_id=1, source_target_pairs={{0,16},{4,20},{8,24},{12,28},{16,0},{20,4},{24,8},{28,12},{1,17},{... | collective-permute-start | bytes 32 | tf_op jit(solution)/shard_map/ppermute | solution.py:317
  (1 other events, 0.7 us)

commit v4 on v3

--- a/solution.py
+++ b/solution.py
@@ -9,6 +9,7 @@
 
 
 live_level = 0.25
+ahead_limit = 20 * 2**20
 near_limit = 36 * 2**20
 far_limit = 32 * 2**20
 
@@ -29,42 +30,46 @@
     )
 
 
-def near_kernel(
-    position_ref, block_ref, bias_ref, own_ref, near_ref, far_ref, cross_ref, weights_ref, near_weights_ref,
-    inputs, first, total_ref, tiles, sems,
-):
+def ahead_kernel(position_ref, own_ref, near_ref, far_ref, weights_ref, inputs, tile, sems):
     position = position_ref[0]
-    core = lax.rem(position, 2)
-    half = near_ref.shape[0]
-    slots, rows, _, width = first.shape
-    deep = tiles.shape[1] // rows
-    own_rows = pl.ds(pl.multiple_of(core * half, half), half)
-    for mask, ref in ((0, own_ref.at[own_rows]), (1, near_ref), (2, far_ref), (3, cross_ref)):
+    half, width = inputs.shape[1:]
+    rows = own_ref.shape[1] // width
+    own_rows = pl.ds(pl.multiple_of(lax.rem(position, 2) * half, half), half)
+    for mask, ref in ((0, own_ref.at[own_rows]), (1, near_ref), (2, far_ref)):
         for r in range(rows):
             block = (position ^ mask) * rows + r
             pltpu.make_async_copy(ref.at[:, pl.ds(r * width, width)], inputs.at[block], sems.at[0]).start()
-    loads = [
-        pltpu.make_async_copy(ref.at[0], tiles.at[mask], sems.at[1 + mask])
-        for mask, ref in enumerate((weights_ref, near_weights_ref))
-    ]
-    for load in loads:
-        load.start()
-    pltpu.make_async_copy(inputs, inputs, sems.at[0]).wait()
-
-    def layer(mask, total):
-        for slot in range(slots):
-            @pl.when(mask == slot)
-            def _():
-                loads[slot].wait()
-
+    load = pltpu.make_async_copy(weights_ref.at[0], tile, sems.at[1])
+    load.start()
+    here = inputs.at[pl.ds(0, 3 * rows)]
+    pltpu.make_async_copy(here, here, sems.at[0]).wait()
+    load.wait()
+
+
+def near_kernel(
+    position_ref, block_ref, bias_ref, _, tile_ref, cross_ref, near_weights_ref, inputs, first, total_ref, near_tile, sems,
+):
+    position = position_ref[0]
+    _, rows, half, width = first.shape
+    deep = near_tile.shape[0] // rows
+    for r in range(rows):
+        block = (position ^ 3) * rows + r
+        pltpu.make_async_copy(cross_ref.at[:, pl.ds(r * width, width)], inputs.at[block], sems.at[0]).start()
+    load = pltpu.make_async_copy(near_weights_ref.at[0], near_tile, sems.at[1])
+    load.start()
+    here = inputs.at[pl.ds(0, rows)]
+    pltpu.make_async_copy(here, here, sems.at[0]).wait()
+
+    total = jnp.zeros((half, width), jnp.float32)
+    for mask, tile in enumerate((tile_ref, near_tile)):
+        if mask:
+            load.wait()
         for r in range(rows):
             row = (position ^ mask) * rows + r
             parts = [inputs[block_ref[row * 4 + k]] for k in range(4)]
-            first[mask, r] = result = outcome(parts, tiles[mask, r * deep : (r + 1) * deep, :], bias_ref[pl.ds(row, 1), :])
+            first[mask, r] = result = outcome(parts, tile[r * deep : (r + 1) * deep, :], bias_ref[pl.ds(row, 1), :])
             total = total + result.astype(jnp.float32)
-        return total
-
-    total_ref[...] = lax.fori_loop(0, slots, layer, jnp.zeros((half, width), jnp.float32))
+    total_ref[...] = total
 
 
 def far_kernel(
@@ -159,6 +164,7 @@
     parts = []
     for h in range(splits):
         part = lax.dynamic_slice(weights, (0, group * piece_rows + h * part_rows, 0), (1, part_rows, width))[0]
+        weights, part = lax.optimization_barrier((weights, part))
         parts.append(nrn(part, perm=xor_pairs(sides, 2)))
     if groups % 2 or groups > 8:
         piece = jnp.concatenate(parts)
@@ -266,6 +272,18 @@
     smem = pl.BlockSpec(memory_space=pltpu.SMEM)
     vmem = pl.BlockSpec(memory_space=pltpu.VMEM)
     flops = 2 * half * rows * deep * width
+    inputs, tile = pl.pallas_call(
+        ahead_kernel,
+        out_shape=(
+            jax.ShapeDtypeStruct((sides * rows, half, width), jnp.bfloat16),
+            jax.ShapeDtypeStruct((rows * deep, width), jnp.bfloat16),
+        ),
+        in_specs=[smem] + [any_space] * 4,
+        out_specs=(vmem,) * 2,
+        scratch_shapes=[pltpu.SemaphoreType.DMA((2,))],
+        compiler_params=pltpu.CompilerParams(vmem_limit_bytes=ahead_limit),
+        cost_estimate=pl.CostEstimate(flops=flops, bytes_accessed=2**23, transcendentals=0),
+    )(place, images, near, far, weights)
     inputs, near_first, total = pl.pallas_call(
         near_kernel,
         out_shape=(
@@ -273,12 +291,13 @@
             jax.ShapeDtypeStruct((2, rows, half, width), jnp.bfloat16),
             jax.ShapeDtypeStruct((half, width), jnp.float32),
         ),
-        in_specs=[smem] * 2 + [vmem] + [any_space] * 6,
+        in_specs=[smem] * 2 + [vmem] * 3 + [any_space] * 2,
         out_specs=(vmem,) * 3,
-        scratch_shapes=[pltpu.VMEM((2, rows * deep, width), jnp.bfloat16), pltpu.SemaphoreType.DMA((3,))],
+        scratch_shapes=[pltpu.VMEM((rows * deep, width), jnp.bfloat16), pltpu.SemaphoreType.DMA((2,))],
+        input_output_aliases={3: 0},
         compiler_params=pltpu.CompilerParams(vmem_limit_bytes=near_limit),
         cost_estimate=pl.CostEstimate(flops=2 * flops, bytes_accessed=2**24, transcendentals=0),
-    )(place, blocks, biases, images, near, far, cross, weights, near_weights)
+    )(place, blocks, biases, inputs, tile, cross, near_weights)
     activations, theirs, sums = pl.pallas_call(
         functools.partial(far_kernel, slots),
         out_shape=(

time: 138 us -> 172 us (1.25)
  waiting for transfers between devices: 34.2 us -> 65.9 us
  local copies, waits for them, and re-layouts: 11.4 us -> 22.5 us
  starting transfers between devices: 74.6 us -> 66.2 us
    ppermute x1, waiting for transfers between devices: 2.73 us -> 13.9 us  [per_device(): cross = nrn(given, perm=xor_pairs(sides, 3))]
    unnamed x16 -> x34, local copies, waits for them, and re-layouts: 4 us -> 14.3 us
    ppermute x1, waiting for transfers between devices: 6.04 us -> 16.3 us  [per_device(): far = nrn(kept, perm=xor_pairs(sides, 2))]
    ppermute x2, waiting for transfers between devices: 4.82 us -> 14.1 us  [gather_far(): parts.append(nrn(part, perm=xor_pairs(sides, 2)))]
    ppermute x6, waiting for transfers between devices: 8.67 us -> 0.02 us  [gather_far(): held[h] = both(held[h], perm=pairs(s - 1, onward))]
    ppermute x2, waiting for transfers between devices: 1.95 us -> 10.1 us  [gather_far(): other = both(part, perm=pairs(0, beside))]
    ppermute x5, starting transfers between devices: 9.38 us -> 14.5 us  [gather_far(): nrn(other, perm=xor_pairs(sides, 1))]
    ppermute x6, starting transfers between devices: 16.6 us -> 11.6 us  [gather_far(): held[h] = both(held[h], perm=pairs(s - 1, onward))]
  transfers between devices with their start and end apart: 42 -> 42, of which waited for: 15 -> 14; matrix products, arithmetic and copies ran while one was open for 5% -> 4% of each run, Pallas kernels for 5% -> 3%
where the time goes in v4:
time: 172 us; the launch traced here: 171 us
  starting transfers between devices  66.2 us (38%)
  waiting for transfers between devices  65.9 us (38%)
  local copies, waits for them, and re-layouts  22.5 us (13%)
  Pallas kernels  14.4 us (8%)
    ppermute x6, starting transfers between devices, gather_far(): keep(nrn(held[h], perm=xor_pairs(sides, 1)), 3 - h, s, False, True)  16.9 us
    ppermute x1, waiting for transfers between devices, per_device(): far = nrn(kept, perm=xor_pairs(sides, 2))  16.3 us
    ppermute x5, starting transfers between devices, gather_far(): nrn(other, perm=xor_pairs(sides, 1))  14.5 us
    unnamed x34, local copies, waits for them, and re-layouts  14.3 us
    ppermute x2, waiting for transfers between devices, gather_far(): parts.append(nrn(part, perm=xor_pairs(sides, 2)))  14.1 us
    ppermute x1, waiting for transfers between devices, per_device(): cross = nrn(given, perm=xor_pairs(sides, 3))  13.9 us
    ppermute x6, starting transfers between devices, gather_far(): held[h] = both(held[h], perm=pairs(s - 1, onward))  11.6 us
    ppermute x2, waiting for transfers between devices, gather_far(): other = both(part, perm=pairs(0, beside))  10.1 us
  transfers between devices with their start and end apart: 42, of which 14 were waited for; matrix products, arithmetic and copies ran while one was open for 4% of the time, Pallas kernels for 3%

profile of v4, /device:TPU:0, one launch (start us, length us, event | category | flops | bytes accessed | tf_op | source)
XLA Modules:
  0.0 170.9 jit_solution(10181795960783707631)
XLA Ops:
  0.9 0.9 copy.7
  1.9 1.0 reshape.55.bias_ref
  3.6 1.0 dynamic-slice_bitcast_fusion.2
  4.6 1.0 dynamic-slice_bitcast_fusion.1
  5.6 1.9 %dynamic-slice_bitcast_fusion = bf16[2048,128]{1,0:T(8,128)(2,1)} fusion(bf16[2,16384,128]{2,1,0:T(8,128)(2,1)} %bitcast.44, s32[]{:T(128)S(6)} %select_n.178), kind=kLoop, calls=%fused_computation | loop fusion | bytes 1048580 | tf_op jit(solution)/shard_map/squeeze | solution.py:213
  7.4 4.4 %collective-permute-start.5 = (bf16[2048,128]{1,0:T(8,128)(2,1)}, bf16[2048,128]{1,0:T(8,128)(2,1)S(1)}, u32[]{:S(2)}, u32[]{:S(2)}) collective-permute-start(bf16[2048,128]{1,0:T(8,128)(2,1)} %dynamic-slice_bitcast_fusion), channel_id=1, source_target_pairs={{0,2},{2,0},{4,6},{6,4},{8,10},{10,8},{12,14},{14,12},{17,19},{19,... | collective-permute-start | bytes 1572872 | tf_op jit(solution)/shard_map/ppermute | solution.py:214
  11.9 2.0 %collective-permute-start.9 = (bf16[1024,128]{1,0:T(8,128)(2,1)S(1)}, bf16[1024,128]{1,0:T(8,128)(2,1)}, u32[]{:S(2)}, u32[]{:S(2)}) collective-permute-start(bf16[1024,128]{1,0:T(8,128)(2,1)S(1)} %dynamic-slice_bitcast_fusion.1), channel_id=1, source_target_pairs={{0,2},{1,3},{2,0},{3,1},{4,6},{5,7},{6,4},{7,5},{8,10},{9,11},{10,... | collective-permute-start | bytes 786440 | tf_op jit(solution)/shard_map/ppermute | solution.py:168
  13.9 12.2 %collective-permute-done = bf16[1024,128]{1,0:T(8,128)(2,1)} collective-permute-done((bf16[1024,128]{1,0:T(8,128)(2,1)S(1)}, bf16[1024,128]{1,0:T(8,128)(2,1)}, u32[]{:S(2)}, u32[]{:S(2)}) %collective-permute-start) | collective-permute-done | bytes 262176 | tf_op jit(solution)/shard_map/ppermute | solution.py:168
  26.2 1.0 constant_dynamic-update-slice_fusion.1
  27.1 1.8 %collective-permute-done.9 = bf16[1024,128]{1,0:T(8,128)(2,1)} collective-permute-done((bf16[1024,128]{1,0:T(8,128)(2,1)S(1)}, bf16[1024,128]{1,0:T(8,128)(2,1)}, u32[]{:S(2)}, u32[]{:S(2)}) %collective-permute-start.9) | collective-permute-done | bytes 262176 | tf_op jit(solution)/shard_map/ppermute | solution.py:168
  29.0 1.0 constant_dynamic-update-slice_fusion.refs_6_
  30.0 4.5 %collective-permute-start.13 = (bf16[2048,128]{1,0:T(8,128)(2,1)S(1)}, bf16[2048,128]{1,0:T(8,128)(2,1)}, u32[]{:S(2)}, u32[]{:S(2)}) collective-permute-start(bf16[2048,128]{1,0:T(8,128)(2,1)S(1)} %constant_dynamic-update-slice_fusion.refs_6_), channel_id=1, source_target_pairs={{0,8},{2,10},{4,12},{6,14},{8,16},{9,1},{10,18},{11,3},{12,20},{13... | collective-permute-start | bytes 1572872 | tf_op jit(solution)/shard_map/ppermute | solution.py:233
  34.5 1.5 collective-permute-start.10
  36.5 1.1 constant_dynamic-slice_fusion
  37.6 6.3 %collective-permute-done.10.refs_4_ = bf16[1024,128]{1,0:T(8,128)(2,1)S(1)} collective-permute-done((bf16[1024,128]{1,0:T(8,128)(2,1)}, bf16[1024,128]{1,0:T(8,128)(2,1)S(1)}, u32[]{:S(2)}, u32[]{:S(2)}) %collective-permute-start.10) | collective-permute-done | bytes 262176 | tf_op jit(solution)/shard_map/ppermute | solution.py:224
  43.9 1.5 collective-permute-start.2
  45.4 3.8 %collective-permute-done.7.refs_2_ = bf16[1024,128]{1,0:T(8,128)(2,1)} collective-permute-done((bf16[1024,128]{1,0:T(8,128)(2,1)}, bf16[1024,128]{1,0:T(8,128)(2,1)}, u32[]{:S(2)}, u32[]{:S(2)}) %collective-permute-start.7) | collective-permute-done | bytes 262176 | tf_op jit(solution)/shard_map/ppermute | solution.py:224
  49.8 1.2 collective-permute-start.3
  51.4 1.4 collective-permute-done.8.refs_3_
  53.9 16.3 %collective-permute-done.2.far_ref = bf16[128,4096]{1,0:T(8,128)(2,1)S(1)} collective-permute-done((bf16[128,4096]{1,0:T(8,128)(2,1)}, bf16[128,4096]{1,0:T(8,128)(2,1)S(1)}, u32[]{:S(2)}, u32[]{:S(2)}) %collective-permute-start.2) | collective-permute-done | bytes 1048608 | tf_op jit(solution)/shard_map/ppermute | solution.py:265
  70.8 4.4 %collective-permute-start.17 = (bf16[2048,128]{1,0:T(8,128)(2,1)}, bf16[2048,128]{1,0:T(8,128)(2,1)S(1)}, u32[]{:S(2)}, u32[]{:S(2)}) collective-permute-start(bf16[2048,128]{1,0:T(8,128)(2,1)} %collective-permute-done.12.refs_7_), channel_id=1, source_target_pairs={{0,8},{2,10},{4,12},{6,14},{8,16},{9,1},{10,18},{11,3},{12,20},{13... | collective-permute-start | bytes 1572872 | tf_op jit(solution)/shard_map/ppermute | solution.py:233
  75.9 13.9 %collective-permute-done.3.cross_ref = bf16[128,4096]{1,0:T(8,128)(2,1)S(1)} collective-permute-done((bf16[128,4096]{1,0:T(8,128)(2,1)S(1)}, bf16[128,4096]{1,0:T(8,128)(2,1)S(1)}, u32[]{:S(2)}, u32[]{:S(2)}) %collective-permute-start.3) | collective-permute-done | bytes 1048608 | tf_op jit(solution)/shard_map/ppermute | solution.py:268
  89.8 0.8 collective-permute-start.14
  92.8 3.7 %collective-permute-start.22 = (bf16[2048,128]{1,0:T(8,128)(2,1)S(1)}, bf16[2048,128]{1,0:T(8,128)(2,1)S(1)}, u32[]{:S(2)}, u32[]{:S(2)}) collective-permute-start(bf16[2048,128]{1,0:T(8,128)(2,1)S(1)} %collective-permute-done.21.refs_16_), channel_id=1, source_target_pairs={{0,1},{1,0},{2,3},{3,2},{4,5},{5,4},{6,7},{7,6},{8,9},{9,8},{10,11... | collective-permute-start | bytes 1572872 | tf_op jit(solution)/shard_map/ppermute | solution.py:235
  97.2 9.0 %collective-permute-start.16 = (bf16[2048,128]{1,0:T(8,128)(2,1)S(1)}, bf16[2048,128]{1,0:T(8,128)(2,1)S(1)}, u32[]{:S(2)}, u32[]{:S(2)}) collective-permute-start(bf16[2048,128]{1,0:T(8,128)(2,1)S(1)} %collective-permute-done.15.refs_10_), channel_id=1, source_target_pairs={{0,1},{1,0},{2,3},{3,2},{4,5},{5,4},{6,7},{7,6},{8,9},{9,8},{10,11... | collective-permute-start | bytes 1572872 | tf_op jit(solution)/shard_map/ppermute | solution.py:241
  108.5 6.5 %collective-permute-start.30 = (bf16[2048,128]{1,0:T(8,128)(2,1)S(1)}, bf16[2048,128]{1,0:T(8,128)(2,1)S(1)}, u32[]{:S(2)}, u32[]{:S(2)}) collective-permute-start(bf16[2048,128]{1,0:T(8,128)(2,1)S(1)} %collective-permute-done.29.refs_24_), channel_id=1, source_target_pairs={{0,1},{1,0},{2,3},{3,2},{4,5},{5,4},{6,7},{7,6},{8,9},{9,8},{10,11... | collective-permute-start | bytes 1572872 | tf_op jit(solution)/shard_map/ppermute | solution.py:235
  115.0 1.6 collective-permute-start.24
  116.6 5.6 %collective-permute-start.26 = (bf16[2048,128]{1,0:T(8,128)(2,1)S(1)}, bf16[2048,128]{1,0:T(8,128)(2,1)S(1)}, u32[]{:S(2)}, u32[]{:S(2)}) collective-permute-start(bf16[2048,128]{1,0:T(8,128)(2,1)S(1)} %collective-permute-done.25.refs_20_), channel_id=1, source_target_pairs={{0,1},{1,0},{2,3},{3,2},{4,5},{5,4},{6,7},{7,6},{8,9},{9,8},{10,11... | collective-permute-start | bytes 1572872 | tf_op jit(solution)/shard_map/ppermute | solution.py:235
  122.2 3.5 %collective-permute-start.20 = (bf16[2048,128]{1,0:T(8,128)(2,1)S(1)}, bf16[2048,128]{1,0:T(8,128)(2,1)S(1)}, u32[]{:S(2)}, u32[]{:S(2)}) collective-permute-start(bf16[2048,128]{1,0:T(8,128)(2,1)S(1)} %collective-permute-done.19.refs_14_), channel_id=1, source_target_pairs={{0,1},{1,0},{2,3},{3,2},{4,5},{5,4},{6,7},{7,6},{8,9},{9,8},{10,11... | collective-permute-start | bytes 1572872 | tf_op jit(solution)/shard_map/ppermute | solution.py:241
  125.8 0.9 copy-done.4
  127.2 3.4 %copy-done = bf16[2,32,512,128]{3,2,1,0:T(8,128)(2,1)S(1)} copy-done((bf16[2,32,512,128]{3,2,1,0:T(8,128)(2,1)S(1)}, bf16[2,32,512,128]{3,2,1,0:T(8,128)(2,1)}, u32[]{:S(2)}) %copy-start) | copy-done | bytes 8388632
  130.6 1.2 shard_map.59
  131.8 4.4 %shard_map.60 = (bf16[128,128,128]{2,1,0:T(8,128)(2,1)S(1)}, bf16[2,32,128,128]{3,2,1,0:T(8,128)(2,1)S(1)}, f32[128,128]{1,0:T(8,128)S(1)}) custom-call(s32[1]{0:T(128)} %bitcast.1.position_ref, s32[1024]{0:T(1024)S(1)} %reshape.54.block_ref, f32[256,128]{1,0:T(8,128)S(1)} %reshape.55.bias_ref, ...), custom_call_target="tpu_custom_call", output_to_operand_aliasing={{0}: (3, {})} | custom-call | flops 1073741824 | bytes 16777216 | tf_op jit(solution)/shard_map/pallas_call | solution.py:287
  137.8 0.8 copy-done.10
  139.5 1.0 copy-done.7
  140.5 1.0 copy-done.9
  141.5 1.0 copy-done.11
  142.6 1.0 copy-done.13
  143.6 8.9 %shard_map.61 = (bf16[256,4096]{1,0:T(8,128)(2,1)}, bf16[128,4096]{1,0:T(8,128)(2,1)S(1)}, f32[2,8,128]{2,1,0:T(8,128)S(1)}) custom-call(s32[1]{0:T(128)} %bitcast.1.position_ref, s32[30]{0:T(128)S(1)} %stack.113.place_ref, s32[1024]{0:T(1024)S(1)} %reshape.54.block_ref, f32[256,128]{1,0:T(8,128)S(1)} %reshape.55.bias_ref, ...), custom_call_target="tpu_custom_call" | custom-call | flops 2147483648 | bytes 16777216 | tf_op jit(solution)/shard_map/pallas_call | solution.py:301
  152.9 1.5 collective-permute-start.36
  155.1 1.5 collective-permute-done.36
  156.6 0.9 collective-permute-done.38
  157.6 1.6 collective-permute-start.39
  159.2 2.0 %collective-permute-done.39 = f32[2]{0:T(128)S(1)} collective-permute-done((f32[2]{0:T(128)S(1)}, f32[2]{0:T(128)S(1)}, u32[]{:S(2)}, u32[]{:S(2)}) %collective-permute-start.39) | collective-permute-done | bytes 40 | tf_op jit(solution)/shard_map/ppermute | solution.py:336
  161.3 3.6 %collective-permute-done.40 = f32[2]{0:T(128)S(1)} collective-permute-done((f32[2]{0:T(128)S(1)}, f32[2]{0:T(128)S(1)}, u32[]{:S(2)}, u32[]{:S(2)}) %collective-permute-start.40) | collective-permute-done | bytes 40 | tf_op jit(solution)/shard_map/ppermute | solution.py:336
  164.8 2.6 %collective-permute-start.41 = (f32[2]{0:T(128)S(1)}, f32[2]{0:T(128)S(1)}, u32[]{:S(2)}, u32[]{:S(2)}) collective-permute-start(f32[2]{0:T(128)S(1)} %add.198), channel_id=1, source_target_pairs={{0,16},{4,20},{8,24},{12,28},{16,0},{20,4},{24,8},{28,12},{1,17},{... | collective-permute-start | bytes 32 | tf_op jit(solution)/shard_map/ppermute | solution.py:336
  167.4 1.9 %collective-permute-done.41 = f32[2]{0:T(128)S(1)} collective-permute-done((f32[2]{0:T(128)S(1)}, f32[2]{0:T(128)S(1)}, u32[]{:S(2)}, u32[]{:S(2)}) %collective-permute-start.41) | collective-permute-done | bytes 40 | tf_op jit(solution)/shard_map/ppermute | solution.py:336
  169.8 1.1 constant_dynamic-update-slice_fusion.2
  (90 shorter events, 14.6 us)
Async XLA Ops:
  0.6 35.9 %copy-start.1 = (bf16[256,4096]{1,0:T(8,128)(2,1)S(1)}, bf16[256,4096]{1,0:T(8,128)(2,1)}, u32[]{:S(2)}) copy-start(bf16[256,4096]{1,0:T(8,128)(2,1)} %own_ref.1) | copy-start | bytes 6291460
  3.0 124.0 %collective-permute-start.4 = (bf16[2,16384,128]{2,1,0:T(8,128)(2,1)}, bf16[2,16384,128]{2,1,0:T(8,128)(2,1)}, u32[]{:S(2)}, u32[]{:S(2)}) collective-permute-start(bf16[2,16384,128]{2,1,0:T(8,128)(2,1)} %bitcast.41), channel_id=1, source_target_pairs={{0,1},{1,0},{2,3},{3,2},{4,5},{5,4},{6,7},{7,6},{8,9},{9,8},{10,11... | collective-permute-start | bytes 25165832 | tf_op jit(solution)/shard_map/ppermute | solution.py:263
  7.4 28.6 %collective-permute-start.5 = (bf16[2048,128]{1,0:T(8,128)(2,1)}, bf16[2048,128]{1,0:T(8,128)(2,1)S(1)}, u32[]{:S(2)}, u32[]{:S(2)}) collective-permute-start(bf16[2048,128]{1,0:T(8,128)(2,1)} %dynamic-slice_bitcast_fusion), channel_id=1, source_target_pairs={{0,2},{2,0},{4,6},{6,4},{8,10},{10,8},{12,14},{14,12},{17,19},{19,... | collective-permute-start | bytes 1572872 | tf_op jit(solution)/shard_map/ppermute | solution.py:214
  11.8 14.3 %collective-permute-start = (bf16[1024,128]{1,0:T(8,128)(2,1)S(1)}, bf16[1024,128]{1,0:T(8,128)(2,1)}, u32[]{:S(2)}, u32[]{:S(2)}) collective-permute-start(bf16[1024,128]{1,0:T(8,128)(2,1)S(1)} %dynamic-slice_bitcast_fusion.2), channel_id=1, source_target_pairs={{0,2},{1,3},{2,0},{3,1},{4,6},{5,7},{6,4},{7,5},{8,10},{9,11},{10,... | collective-permute-start | bytes 786440 | tf_op jit(solution)/shard_map/ppermute | solution.py:168
  11.9 17.1 %collective-permute-start.9 = (bf16[1024,128]{1,0:T(8,128)(2,1)S(1)}, bf16[1024,128]{1,0:T(8,128)(2,1)}, u32[]{:S(2)}, u32[]{:S(2)}) collective-permute-start(bf16[1024,128]{1,0:T(8,128)(2,1)S(1)} %dynamic-slice_bitcast_fusion.1), channel_id=1, source_target_pairs={{0,2},{1,3},{2,0},{3,1},{4,6},{5,7},{6,4},{7,5},{8,10},{9,11},{10,... | collective-permute-start | bytes 786440 | tf_op jit(solution)/shard_map/ppermute | solution.py:168
  30.0 19.3 %collective-permute-start.13 = (bf16[2048,128]{1,0:T(8,128)(2,1)S(1)}, bf16[2048,128]{1,0:T(8,128)(2,1)}, u32[]{:S(2)}, u32[]{:S(2)}) collective-permute-start(bf16[2048,128]{1,0:T(8,128)(2,1)S(1)} %constant_dynamic-update-slice_fusion.refs_6_), channel_id=1, source_target_pairs={{0,8},{2,10},{4,12},{6,14},{8,16},{9,1},{10,18},{11,3},{12,20},{13... | collective-permute-start | bytes 1572872 | tf_op jit(solution)/shard_map/ppermute | solution.py:233
  34.5 15.3 %collective-permute-start.12 = (bf16[2048,128]{1,0:T(8,128)(2,1)S(1)}, bf16[2048,128]{1,0:T(8,128)(2,1)}, u32[]{:S(2)}, u32[]{:S(2)}) collective-permute-start(bf16[2048,128]{1,0:T(8,128)(2,1)S(1)} %constant_dynamic-update-slice_fusion.refs_6_), channel_id=1, source_target_pairs={{0,1},{1,0},{2,3},{3,2},{4,5},{5,4},{6,7},{7,6},{8,9},{9,8},{10,11... | collective-permute-start | bytes 1572872 | tf_op jit(solution)/shard_map/ppermute | solution.py:228
  34.5 9.4 %collective-permute-start.10 = (bf16[1024,128]{1,0:T(8,128)(2,1)}, bf16[1024,128]{1,0:T(8,128)(2,1)S(1)}, u32[]{:S(2)}, u32[]{:S(2)}) collective-permute-start(bf16[1024,128]{1,0:T(8,128)(2,1)} %collective-permute-done.9), channel_id=1, source_target_pairs={{0,4},{1,5},{2,6},{3,7},{4,0},{5,1},{6,2},{7,3},{8,12},{9,13},{10,... | collective-permute-start | bytes 786440 | tf_op jit(solution)/shard_map/ppermute | solution.py:224
  36.0 13.1 %collective-permute-start.7 = (bf16[1024,128]{1,0:T(8,128)(2,1)}, bf16[1024,128]{1,0:T(8,128)(2,1)}, u32[]{:S(2)}, u32[]{:S(2)}) collective-permute-start(bf16[1024,128]{1,0:T(8,128)(2,1)} %collective-permute-done), channel_id=1, source_target_pairs={{0,4},{1,5},{2,6},{3,7},{4,0},{5,1},{6,2},{7,3},{8,12},{9,13},{10,... | collective-permute-start | bytes 786440 | tf_op jit(solution)/shard_map/ppermute | solution.py:224
  43.9 26.2 %collective-permute-start.2 = (bf16[128,4096]{1,0:T(8,128)(2,1)}, bf16[128,4096]{1,0:T(8,128)(2,1)S(1)}, u32[]{:S(2)}, u32[]{:S(2)}) collective-permute-start(bf16[128,4096]{1,0:T(8,128)(2,1)} %constant_dynamic-slice_fusion), channel_id=1, source_target_pairs={{0,2},{1,3},{2,0},{3,1},{4,6},{5,7},{6,4},{7,5},{8,10},{9,11},{10,... | collective-permute-start | bytes 3145736 | tf_op jit(solution)/shard_map/ppermute | solution.py:265
  49.2 1.8 %collective-permute-start.11 = (bf16[1024,128]{1,0:T(8,128)(2,1)S(1)}, bf16[1024,128]{1,0:T(8,128)(2,1)S(1)}, u32[]{:S(2)}, u32[]{:S(2)}) collective-permute-start(bf16[1024,128]{1,0:T(8,128)(2,1)S(1)} %collective-permute-done.10.refs_4_), channel_id=1, source_target_pairs={{0,1},{1,0},{2,3},{3,2},{4,5},{5,4},{6,7},{7,6},{8,9},{9,8},{10,11... | collective-permute-start | bytes 786440 | tf_op jit(solution)/shard_map/ppermute | solution.py:226
  49.2 26.0 %collective-permute-start.1 = (bf16[128,4096]{1,0:T(8,128)(2,1)S(1)}, bf16[128,4096]{1,0:T(8,128)(2,1)S(1)}, u32[]{:S(2)}, u32[]{:S(2)}) collective-permute-start(bf16[128,4096]{1,0:T(8,128)(2,1)S(1)} %constant_dynamic-slice_fusion.1), channel_id=1, source_target_pairs={{0,1},{1,0},{2,3},{3,2},{4,5},{5,4},{6,7},{7,6},{8,9},{9,8},{10,11... | collective-permute-start | bytes 3145736 | tf_op jit(solution)/shard_map/ppermute | solution.py:269
  49.8 40.0 %collective-permute-start.3 = (bf16[128,4096]{1,0:T(8,128)(2,1)S(1)}, bf16[128,4096]{1,0:T(8,128)(2,1)S(1)}, u32[]{:S(2)}, u32[]{:S(2)}) collective-permute-start(bf16[128,4096]{1,0:T(8,128)(2,1)S(1)} %constant_dynamic-slice_fusion.1), channel_id=1, source_target_pairs={{0,3},{1,2},{2,1},{3,0},{4,7},{5,6},{6,5},{7,4},{8,11},{9,10},{10,... | collective-permute-start | bytes 3145736 | tf_op jit(solution)/shard_map/ppermute | solution.py:268
  51.0 1.8 %collective-permute-start.8 = (bf16[1024,128]{1,0:T(8,128)(2,1)}, bf16[1024,128]{1,0:T(8,128)(2,1)S(1)}, u32[]{:S(2)}, u32[]{:S(2)}) collective-permute-start(bf16[1024,128]{1,0:T(8,128)(2,1)} %collective-permute-done.7.refs_2_), channel_id=1, source_target_pairs={{0,1},{1,0},{2,3},{3,2},{4,5},{5,4},{6,7},{7,6},{8,9},{9,8},{10,11... | collective-permute-start | bytes 786440 | tf_op jit(solution)/shard_map/ppermute | solution.py:226
  53.5 17.3 %collective-permute-start.6 = (bf16[2048,128]{1,0:T(8,128)(2,1)S(1)}, bf16[2048,128]{1,0:T(8,128)(2,1)S(1)}, u32[]{:S(2)}, u32[]{:S(2)}) collective-permute-start(bf16[2048,128]{1,0:T(8,128)(2,1)S(1)} %collective-permute-done.5.refs_0_), channel_id=1, source_target_pairs={{0,1},{1,0},{2,3},{3,2},{4,5},{5,4},{6,7},{7,6},{8,9},{9,8},{10,11... | collective-permute-start | bytes 1572872 | tf_op jit(solution)/shard_map/ppermute | solution.py:217
  70.1 20.5 %collective-permute-start.21 = (bf16[2048,128]{1,0:T(8,128)(2,1)}, bf16[2048,128]{1,0:T(8,128)(2,1)S(1)}, u32[]{:S(2)}, u32[]{:S(2)}) collective-permute-start(bf16[2048,128]{1,0:T(8,128)(2,1)} %collective-permute-done.13.refs_8_), channel_id=1, source_target_pairs={{8,16},{9,1},{10,18},{11,3},{12,20},{13,5},{14,22},{15,7},{16,24},... | collective-permute-start | bytes 1572872 | tf_op jit(solution)/shard_map/ppermute | solution.py:233
  70.8 20.5 %collective-permute-start.17 = (bf16[2048,128]{1,0:T(8,128)(2,1)}, bf16[2048,128]{1,0:T(8,128)(2,1)S(1)}, u32[]{:S(2)}, u32[]{:S(2)}) collective-permute-start(bf16[2048,128]{1,0:T(8,128)(2,1)} %collective-permute-done.12.refs_7_), channel_id=1, source_target_pairs={{0,8},{2,10},{4,12},{6,14},{8,16},{9,1},{10,18},{11,3},{12,20},{13... | collective-permute-start | bytes 1572872 | tf_op jit(solution)/shard_map/ppermute | solution.py:233
  75.2 16.8 %collective-permute-start.15 = (bf16[2048,128]{1,0:T(8,128)(2,1)}, bf16[2048,128]{1,0:T(8,128)(2,1)S(1)}, u32[]{:S(2)}, u32[]{:S(2)}) collective-permute-start(bf16[2048,128]{1,0:T(8,128)(2,1)} %collective-permute-done.13.refs_8_), channel_id=1, source_target_pairs={{1,5},{3,7},{5,1},{7,3},{8,12},{9,13},{10,14},{11,15},{12,8},{13,9... | collective-permute-start | bytes 1572872 | tf_op jit(solution)/shard_map/ppermute | solution.py:239
  89.8 2.9 %collective-permute-start.14 = (bf16[2048,128]{1,0:T(8,128)(2,1)}, bf16[2048,128]{1,0:T(8,128)(2,1)S(1)}, u32[]{:S(2)}, u32[]{:S(2)}) collective-permute-start(bf16[2048,128]{1,0:T(8,128)(2,1)} %collective-permute-done.13.refs_8_), channel_id=1, source_target_pairs={{0,1},{1,0},{2,3},{3,2},{4,5},{5,4},{6,7},{7,6},{8,9},{9,8},{10,11... | collective-permute-start | bytes 1572872 | tf_op jit(solution)/shard_map/ppermute | solution.py:235
  90.7 5.8 %collective-permute-start.29 = (bf16[2048,128]{1,0:T(8,128)(2,1)S(1)}, bf16[2048,128]{1,0:T(8,128)(2,1)S(1)}, u32[]{:S(2)}, u32[]{:S(2)}) collective-permute-start(bf16[2048,128]{1,0:T(8,128)(2,1)S(1)} %collective-permute-done.21.refs_16_), channel_id=1, source_target_pairs={{9,1},{11,3},{13,5},{15,7},{16,24},{18,26},{20,28},{22,30}} | collective-permute-start | bytes 1572872 | tf_op jit(solution)/shard_map/ppermute | solution.py:233
  91.4 5.8 %collective-permute-start.25 = (bf16[2048,128]{1,0:T(8,128)(2,1)S(1)}, bf16[2048,128]{1,0:T(8,128)(2,1)S(1)}, u32[]{:S(2)}, u32[]{:S(2)}) collective-permute-start(bf16[2048,128]{1,0:T(8,128)(2,1)S(1)} %collective-permute-done.17.refs_12_), channel_id=1, source_target_pairs={{8,16},{9,1},{10,18},{11,3},{12,20},{13,5},{14,22},{15,7},{16,24},... | collective-permute-start | bytes 1572872 | tf_op jit(solution)/shard_map/ppermute | solution.py:233
  92.1 14.1 %collective-permute-start.23 = (bf16[2048,128]{1,0:T(8,128)(2,1)S(1)}, bf16[2048,128]{1,0:T(8,128)(2,1)S(1)}, u32[]{:S(2)}, u32[]{:S(2)}) collective-permute-start(bf16[2048,128]{1,0:T(8,128)(2,1)S(1)} %collective-permute-done.21.refs_16_), channel_id=1, source_target_pairs={{1,5},{3,7},{5,1},{7,3},{9,13},{11,15},{13,9},{15,11},{16,20},{18,... | collective-permute-start | bytes 1572872 | tf_op jit(solution)/shard_map/ppermute | solution.py:239
  92.8 13.4 %collective-permute-start.22 = (bf16[2048,128]{1,0:T(8,128)(2,1)S(1)}, bf16[2048,128]{1,0:T(8,128)(2,1)S(1)}, u32[]{:S(2)}, u32[]{:S(2)}) collective-permute-start(bf16[2048,128]{1,0:T(8,128)(2,1)S(1)} %collective-permute-done.21.refs_16_), channel_id=1, source_target_pairs={{0,1},{1,0},{2,3},{3,2},{4,5},{5,4},{6,7},{7,6},{8,9},{9,8},{10,11... | collective-permute-start | bytes 1572872 | tf_op jit(solution)/shard_map/ppermute | solution.py:235
  96.5 10.4 %collective-permute-start.19 = (bf16[2048,128]{1,0:T(8,128)(2,1)S(1)}, bf16[2048,128]{1,0:T(8,128)(2,1)S(1)}, u32[]{:S(2)}, u32[]{:S(2)}) collective-permute-start(bf16[2048,128]{1,0:T(8,128)(2,1)S(1)} %collective-permute-done.17.refs_12_), channel_id=1, source_target_pairs={{1,5},{3,7},{5,1},{7,3},{8,12},{9,13},{10,14},{11,15},{12,8},{13,9... | collective-permute-start | bytes 1572872 | tf_op jit(solution)/shard_map/ppermute | solution.py:239
  97.2 10.5 %collective-permute-start.16 = (bf16[2048,128]{1,0:T(8,128)(2,1)S(1)}, bf16[2048,128]{1,0:T(8,128)(2,1)S(1)}, u32[]{:S(2)}, u32[]{:S(2)}) collective-permute-start(bf16[2048,128]{1,0:T(8,128)(2,1)S(1)} %collective-permute-done.15.refs_10_), channel_id=1, source_target_pairs={{0,1},{1,0},{2,3},{3,2},{4,5},{5,4},{6,7},{7,6},{8,9},{9,8},{10,11... | collective-permute-start | bytes 1572872 | tf_op jit(solution)/shard_map/ppermute | solution.py:241
  106.2 2.3 %collective-permute-start.18 = (bf16[2048,128]{1,0:T(8,128)(2,1)S(1)}, bf16[2048,128]{1,0:T(8,128)(2,1)S(1)}, u32[]{:S(2)}, u32[]{:S(2)}) collective-permute-start(bf16[2048,128]{1,0:T(8,128)(2,1)S(1)} %collective-permute-done.17.refs_12_), channel_id=1, source_target_pairs={{0,1},{1,0},{2,3},{3,2},{4,5},{5,4},{6,7},{7,6},{8,9},{9,8},{10,11... | collective-permute-start | bytes 1572872 | tf_op jit(solution)/shard_map/ppermute | solution.py:235
  106.2 8.8 %collective-permute-start.31 = (bf16[2048,128]{1,0:T(8,128)(2,1)S(1)}, bf16[2048,128]{1,0:T(8,128)(2,1)S(1)}, u32[]{:S(2)}, u32[]{:S(2)}) collective-permute-start(bf16[2048,128]{1,0:T(8,128)(2,1)S(1)} %collective-permute-done.29.refs_24_), channel_id=1, source_target_pairs={{1,5},{3,7},{5,1},{7,3},{24,28},{26,30},{28,24},{30,26}} | collective-permute-start | bytes 1572872 | tf_op jit(solution)/shard_map/ppermute | solution.py:239
  106.9 9.7 %collective-permute-start.27 = (bf16[2048,128]{1,0:T(8,128)(2,1)S(1)}, bf16[2048,128]{1,0:T(8,128)(2,1)S(1)}, u32[]{:S(2)}, u32[]{:S(2)}) collective-permute-start(bf16[2048,128]{1,0:T(8,128)(2,1)S(1)} %collective-permute-done.25.refs_20_), channel_id=1, source_target_pairs={{1,5},{3,7},{5,1},{7,3},{24,28},{26,30},{28,24},{30,26}} | collective-permute-start | bytes 1572872 | tf_op jit(solution)/shard_map/ppermute | solution.py:239
  107.7 14.5 %collective-permute-start.33 = (bf16[2048,128]{1,0:T(8,128)(2,1)S(1)}, bf16[2048,128]{1,0:T(8,128)(2,1)S(1)}, u32[]{:S(2)}, u32[]{:S(2)}) collective-permute-start(bf16[2048,128]{1,0:T(8,128)(2,1)S(1)} %collective-permute-done.25.refs_20_), channel_id=1, source_target_pairs={{9,1},{11,3},{13,5},{15,7},{16,24},{18,26},{20,28},{22,30}} | collective-permute-start | bytes 1572872 | tf_op jit(solution)/shard_map/ppermute | solution.py:233
  108.5 17.2 %collective-permute-start.30 = (bf16[2048,128]{1,0:T(8,128)(2,1)S(1)}, bf16[2048,128]{1,0:T(8,128)(2,1)S(1)}, u32[]{:S(2)}, u32[]{:S(2)}) collective-permute-start(bf16[2048,128]{1,0:T(8,128)(2,1)S(1)} %collective-permute-done.29.refs_24_), channel_id=1, source_target_pairs={{0,1},{1,0},{2,3},{3,2},{4,5},{5,4},{6,7},{7,6},{8,9},{9,8},{10,11... | collective-permute-start | bytes 1572872 | tf_op jit(solution)/shard_map/ppermute | solution.py:235
  115.0 10.8 %collective-permute-start.24 = (bf16[2048,128]{1,0:T(8,128)(2,1)S(1)}, bf16[2048,128]{1,0:T(8,128)(2,1)S(1)}, u32[]{:S(2)}, u32[]{:S(2)}) collective-permute-start(bf16[2048,128]{1,0:T(8,128)(2,1)S(1)} %collective-permute-done.23.refs_18_), channel_id=1, source_target_pairs={{0,1},{1,0},{2,3},{3,2},{4,5},{5,4},{6,7},{7,6},{8,9},{9,8},{10,11... | collective-permute-start | bytes 1572872 | tf_op jit(solution)/shard_map/ppermute | solution.py:241
  116.6 19.6 %collective-permute-start.26 = (bf16[2048,128]{1,0:T(8,128)(2,1)S(1)}, bf16[2048,128]{1,0:T(8,128)(2,1)S(1)}, u32[]{:S(2)}, u32[]{:S(2)}) collective-permute-start(bf16[2048,128]{1,0:T(8,128)(2,1)S(1)} %collective-permute-done.25.refs_20_), channel_id=1, source_target_pairs={{0,1},{1,0},{2,3},{3,2},{4,5},{5,4},{6,7},{7,6},{8,9},{9,8},{10,11... | collective-permute-start | bytes 1572872 | tf_op jit(solution)/shard_map/ppermute | solution.py:235
  122.2 14.7 %collective-permute-start.20 = (bf16[2048,128]{1,0:T(8,128)(2,1)S(1)}, bf16[2048,128]{1,0:T(8,128)(2,1)S(1)}, u32[]{:S(2)}, u32[]{:S(2)}) collective-permute-start(bf16[2048,128]{1,0:T(8,128)(2,1)S(1)} %collective-permute-done.19.refs_14_), channel_id=1, source_target_pairs={{0,1},{1,0},{2,3},{3,2},{4,5},{5,4},{6,7},{7,6},{8,9},{9,8},{10,11... | collective-permute-start | bytes 1572872 | tf_op jit(solution)/shard_map/ppermute | solution.py:241
  125.7 6.1 %copy-start.2 = (bf16[2048,128]{1,0:T(8,128)(2,1)}, bf16[2048,128]{1,0:T(8,128)(2,1)S(1)}, u32[]{:S(2)}) copy-start(bf16[2048,128]{1,0:T(8,128)(2,1)S(1)} %collective-permute-done.30.refs_25_) | copy-start | bytes 1572868
  125.7 12.1 %collective-permute-start.32 = (bf16[2048,128]{1,0:T(8,128)(2,1)S(1)}, bf16[2048,128]{1,0:T(8,128)(2,1)S(1)}, u32[]{:S(2)}, u32[]{:S(2)}) collective-permute-start(bf16[2048,128]{1,0:T(8,128)(2,1)S(1)} %collective-permute-done.31.refs_26_), channel_id=1, source_target_pairs={{0,1},{1,0},{2,3},{3,2},{4,5},{5,4},{6,7},{7,6},{8,9},{9,8},{10,11... | collective-permute-start | bytes 1572872 | tf_op jit(solution)/shard_map/ppermute | solution.py:241
  126.7 11.9 %collective-permute-start.28 = (bf16[2048,128]{1,0:T(8,128)(2,1)S(1)}, bf16[2048,128]{1,0:T(8,128)(2,1)S(1)}, u32[]{:S(2)}, u32[]{:S(2)}) collective-permute-start(bf16[2048,128]{1,0:T(8,128)(2,1)S(1)} %collective-permute-done.27.refs_22_), channel_id=1, source_target_pairs={{0,1},{1,0},{2,3},{3,2},{4,5},{5,4},{6,7},{7,6},{8,9},{9,8},{10,11... | collective-permute-start | bytes 1572872 | tf_op jit(solution)/shard_map/ppermute | solution.py:241
  127.1 12.4 %collective-permute-start.34 = (bf16[2048,128]{1,0:T(8,128)(2,1)S(1)}, bf16[2048,128]{1,0:T(8,128)(2,1)}, u32[]{:S(2)}, u32[]{:S(2)}) collective-permute-start(bf16[2048,128]{1,0:T(8,128)(2,1)S(1)} %collective-permute-done.33.refs_28_), channel_id=1, source_target_pairs={{0,1},{1,0},{2,3},{3,2},{4,5},{5,4},{6,7},{7,6},{8,9},{9,8},{10,11... | collective-permute-start | bytes 1572872 | tf_op jit(solution)/shard_map/ppermute | solution.py:235
  127.2 3.4 %copy-start = (bf16[2,32,512,128]{3,2,1,0:T(8,128)(2,1)S(1)}, bf16[2,32,512,128]{3,2,1,0:T(8,128)(2,1)}, u32[]{:S(2)}) copy-start(bf16[2,32,512,128]{3,2,1,0:T(8,128)(2,1)} %param.5) | copy-start | bytes 25165828
  131.8 7.6 %copy-start.3 = (bf16[2048,128]{1,0:T(8,128)(2,1)S(1)}, bf16[2048,128]{1,0:T(8,128)(2,1)}, u32[]{:S(2)}) copy-start(bf16[2048,128]{1,0:T(8,128)(2,1)} %copy-done.2) | copy-start | bytes 1572868
  131.8 7.6 %copy-start.5 = (bf16[2048,128]{1,0:T(8,128)(2,1)S(1)}, bf16[2048,128]{1,0:T(8,128)(2,1)}, u32[]{:S(2)}) copy-start(bf16[2048,128]{1,0:T(8,128)(2,1)} %copy-done.4) | copy-start | bytes 1572868
  131.8 7.6 %copy-start.15 = (bf16[1024,128]{1,0:T(8,128)(2,1)S(1)}, bf16[1024,128]{1,0:T(8,128)(2,1)}, u32[]{:S(2)}) copy-start(bf16[1024,128]{1,0:T(8,128)(2,1)} %copy-done.14) | copy-start | bytes 786436
  152.5 17.3 %collective-permute-start.35 = (bf16[128,4096]{1,0:T(8,128)(2,1)S(1)}, bf16[128,4096]{1,0:T(8,128)(2,1)S(1)}, u32[]{:S(2)}, u32[]{:S(2)}) collective-permute-start(bf16[128,4096]{1,0:T(8,128)(2,1)S(1)} %get-tuple-element.36), channel_id=1, source_target_pairs={{0,1},{1,0},{2,3},{3,2},{4,5},{5,4},{6,7},{7,6},{8,9},{9,8},{10,11... | collective-permute-start | bytes 3145736 | tf_op jit(solution)/shard_map/ppermute | solution.py:321
  152.9 3.7 %collective-permute-start.36 = (f32[2,8,128]{2,1,0:T(8,128)S(1)}, f32[2,8,128]{2,1,0:T(8,128)S(1)}, u32[]{:S(2)}, u32[]{:S(2)}) collective-permute-start(f32[2,8,128]{2,1,0:T(8,128)S(1)} %get-tuple-element.37), channel_id=1, source_target_pairs={{0,2},{1,3},{2,0},{3,1},{4,6},{5,7},{6,4},{7,5},{8,10},{9,11},{10,... | collective-permute-start | bytes 24584 | tf_op jit(solution)/shard_map/ppermute | solution.py:326
  154.4 2.2 %collective-permute-start.37 = (f32[2,8,128]{2,1,0:T(8,128)S(1)}, f32[2,8,128]{2,1,0:T(8,128)S(1)}, u32[]{:S(2)}, u32[]{:S(2)}) collective-permute-start(f32[2,8,128]{2,1,0:T(8,128)S(1)} %get-tuple-element.37), channel_id=1, source_target_pairs={{0,1},{1,0},{2,3},{3,2},{4,5},{5,4},{6,7},{7,6},{8,9},{9,8},{10,11... | collective-permute-start | bytes 24584 | tf_op jit(solution)/shard_map/ppermute | solution.py:326
  154.4 3.1 %collective-permute-start.38 = (f32[2,8,128]{2,1,0:T(8,128)S(1)}, f32[2,8,128]{2,1,0:T(8,128)S(1)}, u32[]{:S(2)}, u32[]{:S(2)}) collective-permute-start(f32[2,8,128]{2,1,0:T(8,128)S(1)} %get-tuple-element.37), channel_id=1, source_target_pairs={{0,3},{1,2},{2,1},{3,0},{4,7},{5,6},{6,5},{7,4},{8,11},{9,10},{10,... | collective-permute-start | bytes 24584 | tf_op jit(solution)/shard_map/ppermute | solution.py:326
  157.6 3.6 %collective-permute-start.39 = (f32[2]{0:T(128)S(1)}, f32[2]{0:T(128)S(1)}, u32[]{:S(2)}, u32[]{:S(2)}) collective-permute-start(f32[2]{0:T(128)S(1)} %fusion.1), channel_id=1, source_target_pairs={{0,4},{4,0},{8,12},{12,8},{16,20},{20,16},{24,28},{28,24},{1,5},{5... | collective-permute-start | bytes 32 | tf_op jit(solution)/shard_map/ppermute | solution.py:336
  161.3 3.6 %collective-permute-start.40 = (f32[2]{0:T(128)S(1)}, f32[2]{0:T(128)S(1)}, u32[]{:S(2)}, u32[]{:S(2)}) collective-permute-start(f32[2]{0:T(128)S(1)} %add.197), channel_id=1, source_target_pairs={{0,8},{4,12},{8,0},{12,4},{16,24},{20,28},{24,16},{28,20},{1,9},{5... | collective-permute-start | bytes 32 | tf_op jit(solution)/shard_map/ppermute | solution.py:336
  164.8 4.5 %collective-permute-start.41 = (f32[2]{0:T(128)S(1)}, f32[2]{0:T(128)S(1)}, u32[]{:S(2)}, u32[]{:S(2)}) collective-permute-start(f32[2]{0:T(128)S(1)} %add.198), channel_id=1, source_target_pairs={{0,16},{4,20},{8,24},{12,28},{16,0},{20,4},{24,8},{28,12},{1,17},{... | collective-permute-start | bytes 32 | tf_op jit(solution)/shard_map/ppermute | solution.py:336
  (10 other events, 9.0 us)

commit v5 on v4

--- a/solution.py
+++ b/solution.py
@@ -108,49 +108,32 @@
     for copy in loads + moves:
         copy.start()
 
-    def first_layer(step, total):
-        for slot in (2, 3):
-            @pl.when(step == slot - 2)
-            def _():
-                each_piece(slot, lambda copy: copy.wait())
-
+    total = total_ref[...]
+    for step in range(2):
+        each_piece(step + 2, lambda copy: copy.wait())
         for r in range(rows):
             row = (position ^ (step + 2)) * rows + r
             parts = [inputs[block_ref[row * 4 + k]] for k in range(4)]
             first[row] = result = outcome(parts, tiles[step, r * deep : (r + 1) * deep, :], bias_ref[pl.ds(row, 1), :])
             total = total + result.astype(jnp.float32)
-        return total
-
-    sums_ref[0] = collapse(lax.fori_loop(0, 2, first_layer, total_ref[...]))
+    sums_ref[0] = collapse(total)
     for move in moves:
         move.wait()
 
-    def second_layer(step, total):
-        mask = 1 - step
-        for slot in range(2):
-            @pl.when(mask == slot)
-            def _():
-                loads[slot].wait()
-
+    own_rows = pl.ds(pl.multiple_of(core * half, half), half)
+    mine = pltpu.make_async_copy(outputs, activations_ref.at[own_rows], sems.at[4])
+    total = jnp.zeros((half, width), jnp.float32)
+    for mask, out_ref in enumerate((outputs, theirs_ref)):
+        loads[mask].wait()
         for r in range(rows):
             row = (position ^ mask) * rows + r + blocks
             parts = [first[block_ref[row * 4 + k]] for k in range(4)]
             result = outcome(parts, second_tiles[mask, r * deep : (r + 1) * deep, :], bias_ref[pl.ds(row, 1), :])
-            outputs[mask, :, r * width : (r + 1) * width] = result
+            out_ref[:, r * width : (r + 1) * width] = result
             total = total + result.astype(jnp.float32)
-
-        @pl.when(mask == 1)
-        def _():
-            pltpu.make_async_copy(outputs.at[1], theirs_ref, sems.at[4]).start()
-
-        return total
-
-    second_total = lax.fori_loop(0, 2, second_layer, jnp.zeros((half, width), jnp.float32))
-    own_rows = pl.ds(pl.multiple_of(core * half, half), half)
-    mine = pltpu.make_async_copy(outputs.at[0], activations_ref.at[own_rows], sems.at[5])
-    mine.start()
-    sums_ref[1] = collapse(second_total)
-    pltpu.make_async_copy(outputs.at[1], theirs_ref, sems.at[4]).wait()
+        if mask == 0:
+            mine.start()
+    sums_ref[1] = collapse(total)
     mine.wait()
 
 
@@ -306,12 +289,12 @@
             jax.ShapeDtypeStruct((layers, 8, half), jnp.float32),
         ),
         in_specs=[smem] * 3 + [vmem] * 4 + [any_space] * (2 + len(pieces)),
-        out_specs=(any_space, any_space, vmem),
+        out_specs=(any_space, vmem, vmem),
         scratch_shapes=[
             pltpu.VMEM((sides * rows, half, width), jnp.bfloat16),
             pltpu.VMEM((2, rows * deep, width), jnp.bfloat16),
             pltpu.VMEM((2, rows * deep, width), jnp.bfloat16),
-            pltpu.VMEM((2, half, shard), jnp.bfloat16),
+            pltpu.VMEM((half, shard), jnp.bfloat16),
             pltpu.SemaphoreType.DMA((6 + len(pieces),)),
         ],
         compiler_params=pltpu.CompilerParams(vmem_limit_bytes=far_limit),

time: 172 us -> 171 us (level)
  no operation moved by 1% of the time
where the time goes in v5:
time: 171 us; the launch traced here: 170 us
  starting transfers between devices  66 us (39%)
  waiting for transfers between devices  66 us (39%)
  local copies, waits for them, and re-layouts  22.5 us (13%)
  Pallas kernels  13.6 us (8%)
    ppermute x6, starting transfers between devices, gather_far(): keep(nrn(held[h], perm=xor_pairs(sides, 1)), 3 - h, s, False, True)  16.9 us
    ppermute x1, waiting for transfers between devices, per_device(): far = nrn(kept, perm=xor_pairs(sides, 2))  16.3 us
    ppermute x5, starting transfers between devices, gather_far(): nrn(other, perm=xor_pairs(sides, 1))  14.5 us
    unnamed x34, local copies, waits for them, and re-layouts  14.3 us
    ppermute x2, waiting for transfers between devices, gather_far(): parts.append(nrn(part, perm=xor_pairs(sides, 2)))  14.1 us
    ppermute x1, waiting for transfers between devices, per_device(): cross = nrn(given, perm=xor_pairs(sides, 3))  13.9 us
    ppermute x6, starting transfers between devices, gather_far(): held[h] = both(held[h], perm=pairs(s - 1, onward))  11.6 us
    ppermute x2, waiting for transfers between devices, gather_far(): other = both(part, perm=pairs(0, beside))  10.1 us
  transfers between devices with their start and end apart: 42, of which 14 were waited for; matrix products, arithmetic and copies ran while one was open for 4% of the time, Pallas kernels for 3%

profile of v5, /device:TPU:0, one launch (start us, length us, event | category | flops | bytes accessed | tf_op | source)
XLA Modules:
  0.0 170.0 jit_solution(12036011530419287458)
XLA Ops:
  0.9 0.9 copy.7
  1.9 1.0 reshape.55.bias_ref
  3.6 1.0 dynamic-slice_bitcast_fusion.2
  4.6 1.0 dynamic-slice_bitcast_fusion.1
  5.6 1.9 %dynamic-slice_bitcast_fusion = bf16[2048,128]{1,0:T(8,128)(2,1)} fusion(bf16[2,16384,128]{2,1,0:T(8,128)(2,1)} %bitcast.44, s32[]{:T(128)S(6)} %select_n.178), kind=kLoop, calls=%fused_computation | loop fusion | bytes 1048580 | tf_op jit(solution)/shard_map/squeeze | solution.py:196
  7.4 4.4 %collective-permute-start.5 = (bf16[2048,128]{1,0:T(8,128)(2,1)}, bf16[2048,128]{1,0:T(8,128)(2,1)S(1)}, u32[]{:S(2)}, u32[]{:S(2)}) collective-permute-start(bf16[2048,128]{1,0:T(8,128)(2,1)} %dynamic-slice_bitcast_fusion), channel_id=1, source_target_pairs={{0,2},{2,0},{4,6},{6,4},{8,10},{10,8},{12,14},{14,12},{17,19},{19,... | collective-permute-start | bytes 1572872 | tf_op jit(solution)/shard_map/ppermute | solution.py:197
  11.9 2.0 %collective-permute-start.9 = (bf16[1024,128]{1,0:T(8,128)(2,1)S(1)}, bf16[1024,128]{1,0:T(8,128)(2,1)}, u32[]{:S(2)}, u32[]{:S(2)}) collective-permute-start(bf16[1024,128]{1,0:T(8,128)(2,1)S(1)} %dynamic-slice_bitcast_fusion.1), channel_id=1, source_target_pairs={{0,2},{1,3},{2,0},{3,1},{4,6},{5,7},{6,4},{7,5},{8,10},{9,11},{10,... | collective-permute-start | bytes 786440 | tf_op jit(solution)/shard_map/ppermute | solution.py:151
  13.9 12.2 %collective-permute-done = bf16[1024,128]{1,0:T(8,128)(2,1)} collective-permute-done((bf16[1024,128]{1,0:T(8,128)(2,1)S(1)}, bf16[1024,128]{1,0:T(8,128)(2,1)}, u32[]{:S(2)}, u32[]{:S(2)}) %collective-permute-start) | collective-permute-done | bytes 262176 | tf_op jit(solution)/shard_map/ppermute | solution.py:151
  26.2 1.0 constant_dynamic-update-slice_fusion.1
  27.1 1.8 %collective-permute-done.9 = bf16[1024,128]{1,0:T(8,128)(2,1)} collective-permute-done((bf16[1024,128]{1,0:T(8,128)(2,1)S(1)}, bf16[1024,128]{1,0:T(8,128)(2,1)}, u32[]{:S(2)}, u32[]{:S(2)}) %collective-permute-start.9) | collective-permute-done | bytes 262176 | tf_op jit(solution)/shard_map/ppermute | solution.py:151
  29.0 1.0 constant_dynamic-update-slice_fusion.refs_6_
  30.0 4.5 %collective-permute-start.13 = (bf16[2048,128]{1,0:T(8,128)(2,1)S(1)}, bf16[2048,128]{1,0:T(8,128)(2,1)}, u32[]{:S(2)}, u32[]{:S(2)}) collective-permute-start(bf16[2048,128]{1,0:T(8,128)(2,1)S(1)} %constant_dynamic-update-slice_fusion.refs_6_), channel_id=1, source_target_pairs={{0,8},{2,10},{4,12},{6,14},{8,16},{9,1},{10,18},{11,3},{12,20},{13... | collective-permute-start | bytes 1572872 | tf_op jit(solution)/shard_map/ppermute | solution.py:216
  34.5 1.5 collective-permute-start.10
  36.5 1.1 constant_dynamic-slice_fusion
  37.6 6.3 %collective-permute-done.10.refs_4_ = bf16[1024,128]{1,0:T(8,128)(2,1)S(1)} collective-permute-done((bf16[1024,128]{1,0:T(8,128)(2,1)}, bf16[1024,128]{1,0:T(8,128)(2,1)S(1)}, u32[]{:S(2)}, u32[]{:S(2)}) %collective-permute-start.10) | collective-permute-done | bytes 262176 | tf_op jit(solution)/shard_map/ppermute | solution.py:207
  43.9 1.5 collective-permute-start.2
  45.4 3.8 %collective-permute-done.7.refs_2_ = bf16[1024,128]{1,0:T(8,128)(2,1)} collective-permute-done((bf16[1024,128]{1,0:T(8,128)(2,1)}, bf16[1024,128]{1,0:T(8,128)(2,1)}, u32[]{:S(2)}, u32[]{:S(2)}) %collective-permute-start.7) | collective-permute-done | bytes 262176 | tf_op jit(solution)/shard_map/ppermute | solution.py:207
  49.8 1.2 collective-permute-start.3
  51.4 1.4 collective-permute-done.8.refs_3_
  53.9 16.3 %collective-permute-done.2.far_ref = bf16[128,4096]{1,0:T(8,128)(2,1)S(1)} collective-permute-done((bf16[128,4096]{1,0:T(8,128)(2,1)}, bf16[128,4096]{1,0:T(8,128)(2,1)S(1)}, u32[]{:S(2)}, u32[]{:S(2)}) %collective-permute-start.2) | collective-permute-done | bytes 1048608 | tf_op jit(solution)/shard_map/ppermute | solution.py:248
  70.8 4.4 %collective-permute-start.17 = (bf16[2048,128]{1,0:T(8,128)(2,1)}, bf16[2048,128]{1,0:T(8,128)(2,1)S(1)}, u32[]{:S(2)}, u32[]{:S(2)}) collective-permute-start(bf16[2048,128]{1,0:T(8,128)(2,1)} %collective-permute-done.12.refs_7_), channel_id=1, source_target_pairs={{0,8},{2,10},{4,12},{6,14},{8,16},{9,1},{10,18},{11,3},{12,20},{13... | collective-permute-start | bytes 1572872 | tf_op jit(solution)/shard_map/ppermute | solution.py:216
  75.9 13.9 %collective-permute-done.3.cross_ref = bf16[128,4096]{1,0:T(8,128)(2,1)S(1)} collective-permute-done((bf16[128,4096]{1,0:T(8,128)(2,1)S(1)}, bf16[128,4096]{1,0:T(8,128)(2,1)S(1)}, u32[]{:S(2)}, u32[]{:S(2)}) %collective-permute-start.3) | collective-permute-done | bytes 1048608 | tf_op jit(solution)/shard_map/ppermute | solution.py:251
  89.8 0.8 collective-permute-start.14
  92.8 3.7 %collective-permute-start.22 = (bf16[2048,128]{1,0:T(8,128)(2,1)S(1)}, bf16[2048,128]{1,0:T(8,128)(2,1)S(1)}, u32[]{:S(2)}, u32[]{:S(2)}) collective-permute-start(bf16[2048,128]{1,0:T(8,128)(2,1)S(1)} %collective-permute-done.21.refs_16_), channel_id=1, source_target_pairs={{0,1},{1,0},{2,3},{3,2},{4,5},{5,4},{6,7},{7,6},{8,9},{9,8},{10,11... | collective-permute-start | bytes 1572872 | tf_op jit(solution)/shard_map/ppermute | solution.py:218
  97.2 9.0 %collective-permute-start.16 = (bf16[2048,128]{1,0:T(8,128)(2,1)S(1)}, bf16[2048,128]{1,0:T(8,128)(2,1)S(1)}, u32[]{:S(2)}, u32[]{:S(2)}) collective-permute-start(bf16[2048,128]{1,0:T(8,128)(2,1)S(1)} %collective-permute-done.15.refs_10_), channel_id=1, source_target_pairs={{0,1},{1,0},{2,3},{3,2},{4,5},{5,4},{6,7},{7,6},{8,9},{9,8},{10,11... | collective-permute-start | bytes 1572872 | tf_op jit(solution)/shard_map/ppermute | solution.py:224
  108.5 6.5 %collective-permute-start.30 = (bf16[2048,128]{1,0:T(8,128)(2,1)S(1)}, bf16[2048,128]{1,0:T(8,128)(2,1)S(1)}, u32[]{:S(2)}, u32[]{:S(2)}) collective-permute-start(bf16[2048,128]{1,0:T(8,128)(2,1)S(1)} %collective-permute-done.29.refs_24_), channel_id=1, source_target_pairs={{0,1},{1,0},{2,3},{3,2},{4,5},{5,4},{6,7},{7,6},{8,9},{9,8},{10,11... | collective-permute-start | bytes 1572872 | tf_op jit(solution)/shard_map/ppermute | solution.py:218
  115.0 1.6 collective-permute-start.24
  116.6 5.6 %collective-permute-start.26 = (bf16[2048,128]{1,0:T(8,128)(2,1)S(1)}, bf16[2048,128]{1,0:T(8,128)(2,1)S(1)}, u32[]{:S(2)}, u32[]{:S(2)}) collective-permute-start(bf16[2048,128]{1,0:T(8,128)(2,1)S(1)} %collective-permute-done.25.refs_20_), channel_id=1, source_target_pairs={{0,1},{1,0},{2,3},{3,2},{4,5},{5,4},{6,7},{7,6},{8,9},{9,8},{10,11... | collective-permute-start | bytes 1572872 | tf_op jit(solution)/shard_map/ppermute | solution.py:218
  122.2 3.5 %collective-permute-start.20 = (bf16[2048,128]{1,0:T(8,128)(2,1)S(1)}, bf16[2048,128]{1,0:T(8,128)(2,1)S(1)}, u32[]{:S(2)}, u32[]{:S(2)}) collective-permute-start(bf16[2048,128]{1,0:T(8,128)(2,1)S(1)} %collective-permute-done.19.refs_14_), channel_id=1, source_target_pairs={{0,1},{1,0},{2,3},{3,2},{4,5},{5,4},{6,7},{7,6},{8,9},{9,8},{10,11... | collective-permute-start | bytes 1572872 | tf_op jit(solution)/shard_map/ppermute | solution.py:224
  125.8 0.9 copy-done.4
  127.2 3.4 %copy-done = bf16[2,32,512,128]{3,2,1,0:T(8,128)(2,1)S(1)} copy-done((bf16[2,32,512,128]{3,2,1,0:T(8,128)(2,1)S(1)}, bf16[2,32,512,128]{3,2,1,0:T(8,128)(2,1)}, u32[]{:S(2)}) %copy-start) | copy-done | bytes 8388632
  130.6 1.2 shard_map.59
  131.8 4.4 %shard_map.60 = (bf16[128,128,128]{2,1,0:T(8,128)(2,1)S(1)}, bf16[2,32,128,128]{3,2,1,0:T(8,128)(2,1)S(1)}, f32[128,128]{1,0:T(8,128)S(1)}) custom-call(s32[1]{0:T(128)} %bitcast.1.position_ref, s32[1024]{0:T(1024)S(1)} %reshape.54.block_ref, f32[256,128]{1,0:T(8,128)S(1)} %reshape.55.bias_ref, ...), custom_call_target="tpu_custom_call", output_to_operand_aliasing={{0}: (3, {})} | custom-call | flops 1073741824 | bytes 16777216 | tf_op jit(solution)/shard_map/pallas_call | solution.py:270
  137.8 0.8 copy-done.10
  139.5 1.0 copy-done.7
  140.5 1.0 copy-done.9
  141.5 1.0 copy-done.11
  142.6 1.0 copy-done.13
  143.6 8.1 %shard_map.61 = (bf16[256,4096]{1,0:T(8,128)(2,1)}, bf16[128,4096]{1,0:T(8,128)(2,1)S(1)}, f32[2,8,128]{2,1,0:T(8,128)S(1)}) custom-call(s32[1]{0:T(128)} %bitcast.1.position_ref, s32[30]{0:T(128)S(1)} %stack.113.place_ref, s32[1024]{0:T(1024)S(1)} %reshape.54.block_ref, f32[256,128]{1,0:T(8,128)S(1)} %reshape.55.bias_ref, ...), custom_call_target="tpu_custom_call" | custom-call | flops 2147483648 | bytes 16777216 | tf_op jit(solution)/shard_map/pallas_call | solution.py:284
  151.9 1.5 collective-permute-start.36
  154.0 1.5 collective-permute-done.36
  155.5 1.0 collective-permute-done.38
  156.7 1.6 collective-permute-start.39
  158.3 2.0 %collective-permute-done.39 = f32[2]{0:T(128)S(1)} collective-permute-done((f32[2]{0:T(128)S(1)}, f32[2]{0:T(128)S(1)}, u32[]{:S(2)}, u32[]{:S(2)}) %collective-permute-start.39) | collective-permute-done | bytes 40 | tf_op jit(solution)/shard_map/ppermute | solution.py:319
  160.3 3.6 %collective-permute-done.40 = f32[2]{0:T(128)S(1)} collective-permute-done((f32[2]{0:T(128)S(1)}, f32[2]{0:T(128)S(1)}, u32[]{:S(2)}, u32[]{:S(2)}) %collective-permute-start.40) | collective-permute-done | bytes 40 | tf_op jit(solution)/shard_map/ppermute | solution.py:319
  163.9 2.6 %collective-permute-start.41 = (f32[2]{0:T(128)S(1)}, f32[2]{0:T(128)S(1)}, u32[]{:S(2)}, u32[]{:S(2)}) collective-permute-start(f32[2]{0:T(128)S(1)} %add.198), channel_id=1, source_target_pairs={{0,16},{4,20},{8,24},{12,28},{16,0},{20,4},{24,8},{28,12},{1,17},{... | collective-permute-start | bytes 32 | tf_op jit(solution)/shard_map/ppermute | solution.py:319
  166.5 1.9 %collective-permute-done.41 = f32[2]{0:T(128)S(1)} collective-permute-done((f32[2]{0:T(128)S(1)}, f32[2]{0:T(128)S(1)}, u32[]{:S(2)}, u32[]{:S(2)}) %collective-permute-start.41) | collective-permute-done | bytes 40 | tf_op jit(solution)/shard_map/ppermute | solution.py:319
  168.9 1.1 constant_dynamic-update-slice_fusion.2
  (90 shorter events, 14.4 us)
Async XLA Ops:
  0.6 35.9 %copy-start.1 = (bf16[256,4096]{1,0:T(8,128)(2,1)S(1)}, bf16[256,4096]{1,0:T(8,128)(2,1)}, u32[]{:S(2)}) copy-start(bf16[256,4096]{1,0:T(8,128)(2,1)} %own_ref.1) | copy-start | bytes 6291460
  3.0 124.0 %collective-permute-start.4 = (bf16[2,16384,128]{2,1,0:T(8,128)(2,1)}, bf16[2,16384,128]{2,1,0:T(8,128)(2,1)}, u32[]{:S(2)}, u32[]{:S(2)}) collective-permute-start(bf16[2,16384,128]{2,1,0:T(8,128)(2,1)} %bitcast.41), channel_id=1, source_target_pairs={{0,1},{1,0},{2,3},{3,2},{4,5},{5,4},{6,7},{7,6},{8,9},{9,8},{10,11... | collective-permute-start | bytes 25165832 | tf_op jit(solution)/shard_map/ppermute | solution.py:246
  7.4 28.6 %collective-permute-start.5 = (bf16[2048,128]{1,0:T(8,128)(2,1)}, bf16[2048,128]{1,0:T(8,128)(2,1)S(1)}, u32[]{:S(2)}, u32[]{:S(2)}) collective-permute-start(bf16[2048,128]{1,0:T(8,128)(2,1)} %dynamic-slice_bitcast_fusion), channel_id=1, source_target_pairs={{0,2},{2,0},{4,6},{6,4},{8,10},{10,8},{12,14},{14,12},{17,19},{19,... | collective-permute-start | bytes 1572872 | tf_op jit(solution)/shard_map/ppermute | solution.py:197
  11.8 14.3 %collective-permute-start = (bf16[1024,128]{1,0:T(8,128)(2,1)S(1)}, bf16[1024,128]{1,0:T(8,128)(2,1)}, u32[]{:S(2)}, u32[]{:S(2)}) collective-permute-start(bf16[1024,128]{1,0:T(8,128)(2,1)S(1)} %dynamic-slice_bitcast_fusion.2), channel_id=1, source_target_pairs={{0,2},{1,3},{2,0},{3,1},{4,6},{5,7},{6,4},{7,5},{8,10},{9,11},{10,... | collective-permute-start | bytes 786440 | tf_op jit(solution)/shard_map/ppermute | solution.py:151
  11.9 17.1 %collective-permute-start.9 = (bf16[1024,128]{1,0:T(8,128)(2,1)S(1)}, bf16[1024,128]{1,0:T(8,128)(2,1)}, u32[]{:S(2)}, u32[]{:S(2)}) collective-permute-start(bf16[1024,128]{1,0:T(8,128)(2,1)S(1)} %dynamic-slice_bitcast_fusion.1), channel_id=1, source_target_pairs={{0,2},{1,3},{2,0},{3,1},{4,6},{5,7},{6,4},{7,5},{8,10},{9,11},{10,... | collective-permute-start | bytes 786440 | tf_op jit(solution)/shard_map/ppermute | solution.py:151
  30.0 19.3 %collective-permute-start.13 = (bf16[2048,128]{1,0:T(8,128)(2,1)S(1)}, bf16[2048,128]{1,0:T(8,128)(2,1)}, u32[]{:S(2)}, u32[]{:S(2)}) collective-permute-start(bf16[2048,128]{1,0:T(8,128)(2,1)S(1)} %constant_dynamic-update-slice_fusion.refs_6_), channel_id=1, source_target_pairs={{0,8},{2,10},{4,12},{6,14},{8,16},{9,1},{10,18},{11,3},{12,20},{13... | collective-permute-start | bytes 1572872 | tf_op jit(solution)/shard_map/ppermute | solution.py:216
  34.5 15.3 %collective-permute-start.12 = (bf16[2048,128]{1,0:T(8,128)(2,1)S(1)}, bf16[2048,128]{1,0:T(8,128)(2,1)}, u32[]{:S(2)}, u32[]{:S(2)}) collective-permute-start(bf16[2048,128]{1,0:T(8,128)(2,1)S(1)} %constant_dynamic-update-slice_fusion.refs_6_), channel_id=1, source_target_pairs={{0,1},{1,0},{2,3},{3,2},{4,5},{5,4},{6,7},{7,6},{8,9},{9,8},{10,11... | collective-permute-start | bytes 1572872 | tf_op jit(solution)/shard_map/ppermute | solution.py:211
  34.5 9.4 %collective-permute-start.10 = (bf16[1024,128]{1,0:T(8,128)(2,1)}, bf16[1024,128]{1,0:T(8,128)(2,1)S(1)}, u32[]{:S(2)}, u32[]{:S(2)}) collective-permute-start(bf16[1024,128]{1,0:T(8,128)(2,1)} %collective-permute-done.9), channel_id=1, source_target_pairs={{0,4},{1,5},{2,6},{3,7},{4,0},{5,1},{6,2},{7,3},{8,12},{9,13},{10,... | collective-permute-start | bytes 786440 | tf_op jit(solution)/shard_map/ppermute | solution.py:207
  36.0 13.1 %collective-permute-start.7 = (bf16[1024,128]{1,0:T(8,128)(2,1)}, bf16[1024,128]{1,0:T(8,128)(2,1)}, u32[]{:S(2)}, u32[]{:S(2)}) collective-permute-start(bf16[1024,128]{1,0:T(8,128)(2,1)} %collective-permute-done), channel_id=1, source_target_pairs={{0,4},{1,5},{2,6},{3,7},{4,0},{5,1},{6,2},{7,3},{8,12},{9,13},{10,... | collective-permute-start | bytes 786440 | tf_op jit(solution)/shard_map/ppermute | solution.py:207
  43.9 26.2 %collective-permute-start.2 = (bf16[128,4096]{1,0:T(8,128)(2,1)}, bf16[128,4096]{1,0:T(8,128)(2,1)S(1)}, u32[]{:S(2)}, u32[]{:S(2)}) collective-permute-start(bf16[128,4096]{1,0:T(8,128)(2,1)} %constant_dynamic-slice_fusion), channel_id=1, source_target_pairs={{0,2},{1,3},{2,0},{3,1},{4,6},{5,7},{6,4},{7,5},{8,10},{9,11},{10,... | collective-permute-start | bytes 3145736 | tf_op jit(solution)/shard_map/ppermute | solution.py:248
  49.2 1.8 %collective-permute-start.11 = (bf16[1024,128]{1,0:T(8,128)(2,1)S(1)}, bf16[1024,128]{1,0:T(8,128)(2,1)S(1)}, u32[]{:S(2)}, u32[]{:S(2)}) collective-permute-start(bf16[1024,128]{1,0:T(8,128)(2,1)S(1)} %collective-permute-done.10.refs_4_), channel_id=1, source_target_pairs={{0,1},{1,0},{2,3},{3,2},{4,5},{5,4},{6,7},{7,6},{8,9},{9,8},{10,11... | collective-permute-start | bytes 786440 | tf_op jit(solution)/shard_map/ppermute | solution.py:209
  49.2 26.0 %collective-permute-start.1 = (bf16[128,4096]{1,0:T(8,128)(2,1)S(1)}, bf16[128,4096]{1,0:T(8,128)(2,1)S(1)}, u32[]{:S(2)}, u32[]{:S(2)}) collective-permute-start(bf16[128,4096]{1,0:T(8,128)(2,1)S(1)} %constant_dynamic-slice_fusion.1), channel_id=1, source_target_pairs={{0,1},{1,0},{2,3},{3,2},{4,5},{5,4},{6,7},{7,6},{8,9},{9,8},{10,11... | collective-permute-start | bytes 3145736 | tf_op jit(solution)/shard_map/ppermute | solution.py:252
  49.8 40.0 %collective-permute-start.3 = (bf16[128,4096]{1,0:T(8,128)(2,1)S(1)}, bf16[128,4096]{1,0:T(8,128)(2,1)S(1)}, u32[]{:S(2)}, u32[]{:S(2)}) collective-permute-start(bf16[128,4096]{1,0:T(8,128)(2,1)S(1)} %constant_dynamic-slice_fusion.1), channel_id=1, source_target_pairs={{0,3},{1,2},{2,1},{3,0},{4,7},{5,6},{6,5},{7,4},{8,11},{9,10},{10,... | collective-permute-start | bytes 3145736 | tf_op jit(solution)/shard_map/ppermute | solution.py:251
  51.0 1.8 %collective-permute-start.8 = (bf16[1024,128]{1,0:T(8,128)(2,1)}, bf16[1024,128]{1,0:T(8,128)(2,1)S(1)}, u32[]{:S(2)}, u32[]{:S(2)}) collective-permute-start(bf16[1024,128]{1,0:T(8,128)(2,1)} %collective-permute-done.7.refs_2_), channel_id=1, source_target_pairs={{0,1},{1,0},{2,3},{3,2},{4,5},{5,4},{6,7},{7,6},{8,9},{9,8},{10,11... | collective-permute-start | bytes 786440 | tf_op jit(solution)/shard_map/ppermute | solution.py:209
  53.5 17.3 %collective-permute-start.6 = (bf16[2048,128]{1,0:T(8,128)(2,1)S(1)}, bf16[2048,128]{1,0:T(8,128)(2,1)S(1)}, u32[]{:S(2)}, u32[]{:S(2)}) collective-permute-start(bf16[2048,128]{1,0:T(8,128)(2,1)S(1)} %collective-permute-done.5.refs_0_), channel_id=1, source_target_pairs={{0,1},{1,0},{2,3},{3,2},{4,5},{5,4},{6,7},{7,6},{8,9},{9,8},{10,11... | collective-permute-start | bytes 1572872 | tf_op jit(solution)/shard_map/ppermute | solution.py:200
  70.1 20.5 %collective-permute-start.21 = (bf16[2048,128]{1,0:T(8,128)(2,1)}, bf16[2048,128]{1,0:T(8,128)(2,1)S(1)}, u32[]{:S(2)}, u32[]{:S(2)}) collective-permute-start(bf16[2048,128]{1,0:T(8,128)(2,1)} %collective-permute-done.13.refs_8_), channel_id=1, source_target_pairs={{8,16},{9,1},{10,18},{11,3},{12,20},{13,5},{14,22},{15,7},{16,24},... | collective-permute-start | bytes 1572872 | tf_op jit(solution)/shard_map/ppermute | solution.py:216
  70.8 20.5 %collective-permute-start.17 = (bf16[2048,128]{1,0:T(8,128)(2,1)}, bf16[2048,128]{1,0:T(8,128)(2,1)S(1)}, u32[]{:S(2)}, u32[]{:S(2)}) collective-permute-start(bf16[2048,128]{1,0:T(8,128)(2,1)} %collective-permute-done.12.refs_7_), channel_id=1, source_target_pairs={{0,8},{2,10},{4,12},{6,14},{8,16},{9,1},{10,18},{11,3},{12,20},{13... | collective-permute-start | bytes 1572872 | tf_op jit(solution)/shard_map/ppermute | solution.py:216
  75.2 16.8 %collective-permute-start.15 = (bf16[2048,128]{1,0:T(8,128)(2,1)}, bf16[2048,128]{1,0:T(8,128)(2,1)S(1)}, u32[]{:S(2)}, u32[]{:S(2)}) collective-permute-start(bf16[2048,128]{1,0:T(8,128)(2,1)} %collective-permute-done.13.refs_8_), channel_id=1, source_target_pairs={{1,5},{3,7},{5,1},{7,3},{8,12},{9,13},{10,14},{11,15},{12,8},{13,9... | collective-permute-start | bytes 1572872 | tf_op jit(solution)/shard_map/ppermute | solution.py:222
  89.8 2.9 %collective-permute-start.14 = (bf16[2048,128]{1,0:T(8,128)(2,1)}, bf16[2048,128]{1,0:T(8,128)(2,1)S(1)}, u32[]{:S(2)}, u32[]{:S(2)}) collective-permute-start(bf16[2048,128]{1,0:T(8,128)(2,1)} %collective-permute-done.13.refs_8_), channel_id=1, source_target_pairs={{0,1},{1,0},{2,3},{3,2},{4,5},{5,4},{6,7},{7,6},{8,9},{9,8},{10,11... | collective-permute-start | bytes 1572872 | tf_op jit(solution)/shard_map/ppermute | solution.py:218
  90.7 5.8 %collective-permute-start.29 = (bf16[2048,128]{1,0:T(8,128)(2,1)S(1)}, bf16[2048,128]{1,0:T(8,128)(2,1)S(1)}, u32[]{:S(2)}, u32[]{:S(2)}) collective-permute-start(bf16[2048,128]{1,0:T(8,128)(2,1)S(1)} %collective-permute-done.21.refs_16_), channel_id=1, source_target_pairs={{9,1},{11,3},{13,5},{15,7},{16,24},{18,26},{20,28},{22,30}} | collective-permute-start | bytes 1572872 | tf_op jit(solution)/shard_map/ppermute | solution.py:216
  91.4 5.8 %collective-permute-start.25 = (bf16[2048,128]{1,0:T(8,128)(2,1)S(1)}, bf16[2048,128]{1,0:T(8,128)(2,1)S(1)}, u32[]{:S(2)}, u32[]{:S(2)}) collective-permute-start(bf16[2048,128]{1,0:T(8,128)(2,1)S(1)} %collective-permute-done.17.refs_12_), channel_id=1, source_target_pairs={{8,16},{9,1},{10,18},{11,3},{12,20},{13,5},{14,22},{15,7},{16,24},... | collective-permute-start | bytes 1572872 | tf_op jit(solution)/shard_map/ppermute | solution.py:216
  92.1 14.1 %collective-permute-start.23 = (bf16[2048,128]{1,0:T(8,128)(2,1)S(1)}, bf16[2048,128]{1,0:T(8,128)(2,1)S(1)}, u32[]{:S(2)}, u32[]{:S(2)}) collective-permute-start(bf16[2048,128]{1,0:T(8,128)(2,1)S(1)} %collective-permute-done.21.refs_16_), channel_id=1, source_target_pairs={{1,5},{3,7},{5,1},{7,3},{9,13},{11,15},{13,9},{15,11},{16,20},{18,... | collective-permute-start | bytes 1572872 | tf_op jit(solution)/shard_map/ppermute | solution.py:222
  92.8 13.4 %collective-permute-start.22 = (bf16[2048,128]{1,0:T(8,128)(2,1)S(1)}, bf16[2048,128]{1,0:T(8,128)(2,1)S(1)}, u32[]{:S(2)}, u32[]{:S(2)}) collective-permute-start(bf16[2048,128]{1,0:T(8,128)(2,1)S(1)} %collective-permute-done.21.refs_16_), channel_id=1, source_target_pairs={{0,1},{1,0},{2,3},{3,2},{4,5},{5,4},{6,7},{7,6},{8,9},{9,8},{10,11... | collective-permute-start | bytes 1572872 | tf_op jit(solution)/shard_map/ppermute | solution.py:218
  96.5 10.4 %collective-permute-start.19 = (bf16[2048,128]{1,0:T(8,128)(2,1)S(1)}, bf16[2048,128]{1,0:T(8,128)(2,1)S(1)}, u32[]{:S(2)}, u32[]{:S(2)}) collective-permute-start(bf16[2048,128]{1,0:T(8,128)(2,1)S(1)} %collective-permute-done.17.refs_12_), channel_id=1, source_target_pairs={{1,5},{3,7},{5,1},{7,3},{8,12},{9,13},{10,14},{11,15},{12,8},{13,9... | collective-permute-start | bytes 1572872 | tf_op jit(solution)/shard_map/ppermute | solution.py:222
  97.2 10.5 %collective-permute-start.16 = (bf16[2048,128]{1,0:T(8,128)(2,1)S(1)}, bf16[2048,128]{1,0:T(8,128)(2,1)S(1)}, u32[]{:S(2)}, u32[]{:S(2)}) collective-permute-start(bf16[2048,128]{1,0:T(8,128)(2,1)S(1)} %collective-permute-done.15.refs_10_), channel_id=1, source_target_pairs={{0,1},{1,0},{2,3},{3,2},{4,5},{5,4},{6,7},{7,6},{8,9},{9,8},{10,11... | collective-permute-start | bytes 1572872 | tf_op jit(solution)/shard_map/ppermute | solution.py:224
  106.2 2.3 %collective-permute-start.18 = (bf16[2048,128]{1,0:T(8,128)(2,1)S(1)}, bf16[2048,128]{1,0:T(8,128)(2,1)S(1)}, u32[]{:S(2)}, u32[]{:S(2)}) collective-permute-start(bf16[2048,128]{1,0:T(8,128)(2,1)S(1)} %collective-permute-done.17.refs_12_), channel_id=1, source_target_pairs={{0,1},{1,0},{2,3},{3,2},{4,5},{5,4},{6,7},{7,6},{8,9},{9,8},{10,11... | collective-permute-start | bytes 1572872 | tf_op jit(solution)/shard_map/ppermute | solution.py:218
  106.2 8.8 %collective-permute-start.31 = (bf16[2048,128]{1,0:T(8,128)(2,1)S(1)}, bf16[2048,128]{1,0:T(8,128)(2,1)S(1)}, u32[]{:S(2)}, u32[]{:S(2)}) collective-permute-start(bf16[2048,128]{1,0:T(8,128)(2,1)S(1)} %collective-permute-done.29.refs_24_), channel_id=1, source_target_pairs={{1,5},{3,7},{5,1},{7,3},{24,28},{26,30},{28,24},{30,26}} | collective-permute-start | bytes 1572872 | tf_op jit(solution)/shard_map/ppermute | solution.py:222
  106.9 9.7 %collective-permute-start.27 = (bf16[2048,128]{1,0:T(8,128)(2,1)S(1)}, bf16[2048,128]{1,0:T(8,128)(2,1)S(1)}, u32[]{:S(2)}, u32[]{:S(2)}) collective-permute-start(bf16[2048,128]{1,0:T(8,128)(2,1)S(1)} %collective-permute-done.25.refs_20_), channel_id=1, source_target_pairs={{1,5},{3,7},{5,1},{7,3},{24,28},{26,30},{28,24},{30,26}} | collective-permute-start | bytes 1572872 | tf_op jit(solution)/shard_map/ppermute | solution.py:222
  107.7 14.5 %collective-permute-start.33 = (bf16[2048,128]{1,0:T(8,128)(2,1)S(1)}, bf16[2048,128]{1,0:T(8,128)(2,1)S(1)}, u32[]{:S(2)}, u32[]{:S(2)}) collective-permute-start(bf16[2048,128]{1,0:T(8,128)(2,1)S(1)} %collective-permute-done.25.refs_20_), channel_id=1, source_target_pairs={{9,1},{11,3},{13,5},{15,7},{16,24},{18,26},{20,28},{22,30}} | collective-permute-start | bytes 1572872 | tf_op jit(solution)/shard_map/ppermute | solution.py:216
  108.5 17.2 %collective-permute-start.30 = (bf16[2048,128]{1,0:T(8,128)(2,1)S(1)}, bf16[2048,128]{1,0:T(8,128)(2,1)S(1)}, u32[]{:S(2)}, u32[]{:S(2)}) collective-permute-start(bf16[2048,128]{1,0:T(8,128)(2,1)S(1)} %collective-permute-done.29.refs_24_), channel_id=1, source_target_pairs={{0,1},{1,0},{2,3},{3,2},{4,5},{5,4},{6,7},{7,6},{8,9},{9,8},{10,11... | collective-permute-start | bytes 1572872 | tf_op jit(solution)/shard_map/ppermute | solution.py:218
  115.0 10.8 %collective-permute-start.24 = (bf16[2048,128]{1,0:T(8,128)(2,1)S(1)}, bf16[2048,128]{1,0:T(8,128)(2,1)S(1)}, u32[]{:S(2)}, u32[]{:S(2)}) collective-permute-start(bf16[2048,128]{1,0:T(8,128)(2,1)S(1)} %collective-permute-done.23.refs_18_), channel_id=1, source_target_pairs={{0,1},{1,0},{2,3},{3,2},{4,5},{5,4},{6,7},{7,6},{8,9},{9,8},{10,11... | collective-permute-start | bytes 1572872 | tf_op jit(solution)/shard_map/ppermute | solution.py:224
  116.6 19.6 %collective-permute-start.26 = (bf16[2048,128]{1,0:T(8,128)(2,1)S(1)}, bf16[2048,128]{1,0:T(8,128)(2,1)S(1)}, u32[]{:S(2)}, u32[]{:S(2)}) collective-permute-start(bf16[2048,128]{1,0:T(8,128)(2,1)S(1)} %collective-permute-done.25.refs_20_), channel_id=1, source_target_pairs={{0,1},{1,0},{2,3},{3,2},{4,5},{5,4},{6,7},{7,6},{8,9},{9,8},{10,11... | collective-permute-start | bytes 1572872 | tf_op jit(solution)/shard_map/ppermute | solution.py:218
  122.2 14.7 %collective-permute-start.20 = (bf16[2048,128]{1,0:T(8,128)(2,1)S(1)}, bf16[2048,128]{1,0:T(8,128)(2,1)S(1)}, u32[]{:S(2)}, u32[]{:S(2)}) collective-permute-start(bf16[2048,128]{1,0:T(8,128)(2,1)S(1)} %collective-permute-done.19.refs_14_), channel_id=1, source_target_pairs={{0,1},{1,0},{2,3},{3,2},{4,5},{5,4},{6,7},{7,6},{8,9},{9,8},{10,11... | collective-permute-start | bytes 1572872 | tf_op jit(solution)/shard_map/ppermute | solution.py:224
  125.7 6.1 %copy-start.2 = (bf16[2048,128]{1,0:T(8,128)(2,1)}, bf16[2048,128]{1,0:T(8,128)(2,1)S(1)}, u32[]{:S(2)}) copy-start(bf16[2048,128]{1,0:T(8,128)(2,1)S(1)} %collective-permute-done.30.refs_25_) | copy-start | bytes 1572868
  125.7 12.1 %collective-permute-start.32 = (bf16[2048,128]{1,0:T(8,128)(2,1)S(1)}, bf16[2048,128]{1,0:T(8,128)(2,1)S(1)}, u32[]{:S(2)}, u32[]{:S(2)}) collective-permute-start(bf16[2048,128]{1,0:T(8,128)(2,1)S(1)} %collective-permute-done.31.refs_26_), channel_id=1, source_target_pairs={{0,1},{1,0},{2,3},{3,2},{4,5},{5,4},{6,7},{7,6},{8,9},{9,8},{10,11... | collective-permute-start | bytes 1572872 | tf_op jit(solution)/shard_map/ppermute | solution.py:224
  126.7 11.9 %collective-permute-start.28 = (bf16[2048,128]{1,0:T(8,128)(2,1)S(1)}, bf16[2048,128]{1,0:T(8,128)(2,1)S(1)}, u32[]{:S(2)}, u32[]{:S(2)}) collective-permute-start(bf16[2048,128]{1,0:T(8,128)(2,1)S(1)} %collective-permute-done.27.refs_22_), channel_id=1, source_target_pairs={{0,1},{1,0},{2,3},{3,2},{4,5},{5,4},{6,7},{7,6},{8,9},{9,8},{10,11... | collective-permute-start | bytes 1572872 | tf_op jit(solution)/shard_map/ppermute | solution.py:224
  127.1 12.4 %collective-permute-start.34 = (bf16[2048,128]{1,0:T(8,128)(2,1)S(1)}, bf16[2048,128]{1,0:T(8,128)(2,1)}, u32[]{:S(2)}, u32[]{:S(2)}) collective-permute-start(bf16[2048,128]{1,0:T(8,128)(2,1)S(1)} %collective-permute-done.33.refs_28_), channel_id=1, source_target_pairs={{0,1},{1,0},{2,3},{3,2},{4,5},{5,4},{6,7},{7,6},{8,9},{9,8},{10,11... | collective-permute-start | bytes 1572872 | tf_op jit(solution)/shard_map/ppermute | solution.py:218
  127.2 3.4 %copy-start = (bf16[2,32,512,128]{3,2,1,0:T(8,128)(2,1)S(1)}, bf16[2,32,512,128]{3,2,1,0:T(8,128)(2,1)}, u32[]{:S(2)}) copy-start(bf16[2,32,512,128]{3,2,1,0:T(8,128)(2,1)} %param.5) | copy-start | bytes 25165828
  131.8 7.6 %copy-start.3 = (bf16[2048,128]{1,0:T(8,128)(2,1)S(1)}, bf16[2048,128]{1,0:T(8,128)(2,1)}, u32[]{:S(2)}) copy-start(bf16[2048,128]{1,0:T(8,128)(2,1)} %copy-done.2) | copy-start | bytes 1572868
  131.8 7.6 %copy-start.5 = (bf16[2048,128]{1,0:T(8,128)(2,1)S(1)}, bf16[2048,128]{1,0:T(8,128)(2,1)}, u32[]{:S(2)}) copy-start(bf16[2048,128]{1,0:T(8,128)(2,1)} %copy-done.4) | copy-start | bytes 1572868
  131.8 7.6 %copy-start.15 = (bf16[1024,128]{1,0:T(8,128)(2,1)S(1)}, bf16[1024,128]{1,0:T(8,128)(2,1)}, u32[]{:S(2)}) copy-start(bf16[1024,128]{1,0:T(8,128)(2,1)} %copy-done.14) | copy-start | bytes 786436
  151.7 17.2 %collective-permute-start.35 = (bf16[128,4096]{1,0:T(8,128)(2,1)S(1)}, bf16[128,4096]{1,0:T(8,128)(2,1)S(1)}, u32[]{:S(2)}, u32[]{:S(2)}) collective-permute-start(bf16[128,4096]{1,0:T(8,128)(2,1)S(1)} %get-tuple-element.36), channel_id=1, source_target_pairs={{0,1},{1,0},{2,3},{3,2},{4,5},{5,4},{6,7},{7,6},{8,9},{9,8},{10,11... | collective-permute-start | bytes 3145736 | tf_op jit(solution)/shard_map/ppermute | solution.py:304
  151.9 3.7 %collective-permute-start.36 = (f32[2,8,128]{2,1,0:T(8,128)S(1)}, f32[2,8,128]{2,1,0:T(8,128)S(1)}, u32[]{:S(2)}, u32[]{:S(2)}) collective-permute-start(f32[2,8,128]{2,1,0:T(8,128)S(1)} %get-tuple-element.37), channel_id=1, source_target_pairs={{0,2},{1,3},{2,0},{3,1},{4,6},{5,7},{6,4},{7,5},{8,10},{9,11},{10,... | collective-permute-start | bytes 24584 | tf_op jit(solution)/shard_map/ppermute | solution.py:309
  153.4 2.2 %collective-permute-start.37 = (f32[2,8,128]{2,1,0:T(8,128)S(1)}, f32[2,8,128]{2,1,0:T(8,128)S(1)}, u32[]{:S(2)}, u32[]{:S(2)}) collective-permute-start(f32[2,8,128]{2,1,0:T(8,128)S(1)} %get-tuple-element.37), channel_id=1, source_target_pairs={{0,1},{1,0},{2,3},{3,2},{4,5},{5,4},{6,7},{7,6},{8,9},{9,8},{10,11... | collective-permute-start | bytes 24584 | tf_op jit(solution)/shard_map/ppermute | solution.py:309
  153.5 3.1 %collective-permute-start.38 = (f32[2,8,128]{2,1,0:T(8,128)S(1)}, f32[2,8,128]{2,1,0:T(8,128)S(1)}, u32[]{:S(2)}, u32[]{:S(2)}) collective-permute-start(f32[2,8,128]{2,1,0:T(8,128)S(1)} %get-tuple-element.37), channel_id=1, source_target_pairs={{0,3},{1,2},{2,1},{3,0},{4,7},{5,6},{6,5},{7,4},{8,11},{9,10},{10,... | collective-permute-start | bytes 24584 | tf_op jit(solution)/shard_map/ppermute | solution.py:309
  156.7 3.6 %collective-permute-start.39 = (f32[2]{0:T(128)S(1)}, f32[2]{0:T(128)S(1)}, u32[]{:S(2)}, u32[]{:S(2)}) collective-permute-start(f32[2]{0:T(128)S(1)} %fusion.1), channel_id=1, source_target_pairs={{0,4},{4,0},{8,12},{12,8},{16,20},{20,16},{24,28},{28,24},{1,5},{5... | collective-permute-start | bytes 32 | tf_op jit(solution)/shard_map/ppermute | solution.py:319
  160.3 3.6 %collective-permute-start.40 = (f32[2]{0:T(128)S(1)}, f32[2]{0:T(128)S(1)}, u32[]{:S(2)}, u32[]{:S(2)}) collective-permute-start(f32[2]{0:T(128)S(1)} %add.197), channel_id=1, source_target_pairs={{0,8},{4,12},{8,0},{12,4},{16,24},{20,28},{24,16},{28,20},{1,9},{5... | collective-permute-start | bytes 32 | tf_op jit(solution)/shard_map/ppermute | solution.py:319
  163.9 4.5 %collective-permute-start.41 = (f32[2]{0:T(128)S(1)}, f32[2]{0:T(128)S(1)}, u32[]{:S(2)}, u32[]{:S(2)}) collective-permute-start(f32[2]{0:T(128)S(1)} %add.198), channel_id=1, source_target_pairs={{0,16},{4,20},{8,24},{12,28},{16,0},{20,4},{24,8},{28,12},{1,17},{... | collective-permute-start | bytes 32 | tf_op jit(solution)/shard_map/ppermute | solution.py:319
  (10 other events, 9.0 us)
